TPU v7x, 32 devices: a whole 2x2x4 slice. The times are simulated.
32 devices in a mesh: gx: 8 (over z, core), gy: 4 (over y, x).
Axes of the slice: x: 2, y: 2, z: 4, core: 2. Of those that a mesh axis runs over, the one named last changes fastest.
Arguments:
- earlier_heat_field: float32 [6, 1024, 512], P(None, 'gx', 'gy'), may hold values from -6 to 6
- substance_per_voxel: int32 [6, 1024, 512], P(None, 'gx', 'gy'), may hold values from 0 to 7
- patch_wattage_category: int32 [64, 32], P('gx', 'gy'), may hold values from 0 to 63
- planar_coupling: float32 [8], replicated, may hold values from 0.3 to 3
- vertical_coupling_per_substance: float32 [8], replicated, may hold values from 0.05 to 0.5
- heat_mass_ratio: float32 [8], replicated, may hold values from 2e-05 to 0.0002
- wattage_per_category: float32 [64], replicated, may hold values from 2e-06 to 2e-05
Outputs:
- temperature: float32 [6, 1024, 512], P(None, 'gx', 'gy')
All inputs are finite; a program needn't handle non-finite values.
Results may differ from a plain program's by a relative error of at most 0.0003.
Values sent between devices are 32-bit elements; how exact they have to be, the bound alone decides.
No kernel may reach another device: no remote copies, remote signals or barrier semaphores. Data moves between devices by JAX's collectives and lax.ppermute only.
A program may use at most 192 MiB of HBM per device.

v0:
```python
import jax
import jax.numpy as jnp
from jax import lax
from jax.sharding import PartitionSpec as P

TILE = 16
LEVELS = 6
SWEEPS = 2
COARSE_ITERS = 12


def extended(block, sides, width):
    for axis, dim in sides:
        count = lax.axis_size(axis)
        forward = [(i, i + 1) for i in range(count - 1)]
        backward = [(target, source) for source, target in forward]
        low = lax.ppermute(
            lax.slice_in_dim(block, block.shape[dim] - width, None, axis=dim), axis, forward
        )
        high = lax.ppermute(lax.slice_in_dim(block, 0, width, axis=dim), axis, backward)
        block = jnp.concatenate([low, block, high], axis=dim)
    return block


def previous(values, dimension):
    widths = [(0, 0)] * values.ndim
    widths[dimension] = (1, 0)
    return lax.slice_in_dim(jnp.pad(values, widths), 0, values.shape[dimension], axis=dimension)


def following(values, dimension):
    widths = [(0, 0)] * values.ndim
    widths[dimension] = (0, 1)
    return lax.slice_in_dim(jnp.pad(values, widths), 1, values.shape[dimension] + 1, axis=dimension)


def stencil(lateral, vertical, capacity_diagonal, inside, factor):
    row_before = factor * 0.5 * (lateral + previous(lateral, 1))
    row_after = factor * 0.5 * (lateral + following(lateral, 1))
    col_before = factor * 0.5 * (lateral + previous(lateral, 2))
    col_after = factor * 0.5 * (lateral + following(lateral, 2))
    faces = 0.5 * (vertical[1:] + vertical[:-1])
    no_face = jnp.zeros_like(vertical[:1])
    layer_below = jnp.concatenate([no_face, faces], 0)
    layer_above = jnp.concatenate([faces, no_face], 0)
    diagonal = (
        capacity_diagonal
        + row_before
        + row_after
        + col_before
        + col_after
        + layer_below
        + layer_above
    )
    diagonal = jnp.where(inside > 0, diagonal, 1.0)
    return (row_before, row_after, col_before, col_after, layer_below, layer_above, diagonal)


def coupled(values, weights):
    summed = weights[0] * previous(values, 1) + weights[1] * following(values, 1)
    summed = summed + weights[2] * previous(values, 2) + weights[3] * following(values, 2)
    return summed + weights[4] * previous(values, 0) + weights[5] * following(values, 0)


def parity(extent):
    summed = lax.broadcasted_iota(jnp.int32, extent, 0) + lax.broadcasted_iota(jnp.int32, extent, 1)
    return (summed + lax.broadcasted_iota(jnp.int32, extent, 2)) % 2


def restrict(values):
    layers, height, breadth = values.shape
    blocks = values.reshape(layers, height // 2, 2, breadth // 2, 2)
    return (
        blocks[:, :, 0, :, 0]
        + blocks[:, :, 1, :, 0]
        + blocks[:, :, 0, :, 1]
        + blocks[:, :, 1, :, 1]
    ) * 0.25


def prolong(values):
    return jnp.repeat(jnp.repeat(values, 2, axis=1), 2, axis=2)


def lookup(labels, entries):
    summed = jnp.zeros(labels.shape, entries.dtype)
    for number in range(entries.shape[0]):
        summed = summed + jnp.where(labels == number, entries[number], 0.0)
    return summed


def conjugate(source_vector, weights):
    solution = jnp.zeros_like(source_vector)
    residue = source_vector
    precond = residue / weights[6]
    search = precond
    inner = jnp.sum(residue * precond)
    for step_index in range(COARSE_ITERS):
        image = weights[6] * search - coupled(search, weights)
        alpha_step = inner / jnp.sum(search * image)
        solution = solution + alpha_step * search
        residue = residue - alpha_step * image
        precond = residue / weights[6]
        inner_next = jnp.sum(residue * precond)
        search = precond + inner_next / inner * search
        inner = inner_next
    return solution


def update(beside_all, rhs_pad, weights, colours, inside, colour, margin):
    extent = beside_all.shape
    row_index = lax.broadcasted_iota(jnp.int32, extent, 1)
    col_index = lax.broadcasted_iota(jnp.int32, extent, 2)
    region = (row_index >= margin) & (row_index < extent[1] - margin)
    region = region & (col_index >= margin) & (col_index < extent[2] - margin)
    candidate = (rhs_pad + coupled(beside_all, weights)) / weights[6]
    chosen = (colours == colour) & region & (inside > 0)
    return jnp.where(chosen, candidate, beside_all)


def smooth(present_guess, rhs_pad, level_data):
    wide, narrow, colours_wide, inside_wide = level_data
    for sweep_index in range(SWEEPS):
        beside_all = extended(present_guess, (("gx", 1), ("gy", 2)), 2)
        beside_all = update(beside_all, rhs_pad, wide, colours_wide, inside_wide, 0, 1)
        beside_all = update(beside_all, rhs_pad, wide, colours_wide, inside_wide, 1, 2)
        present_guess = beside_all[:, 2:-2, 2:-2]
    return present_guess


def on_device(
    earlier_heat_field,
    substance_per_voxel,
    patch_wattage_category,
    planar_coupling,
    vertical_coupling_per_substance,
    heat_mass_ratio,
    wattage_per_category,
):
    lateral = lookup(substance_per_voxel, planar_coupling)
    vertical = lookup(substance_per_voxel, vertical_coupling_per_substance)
    capacity_diagonal = lookup(substance_per_voxel, heat_mass_ratio)
    heat = jnp.repeat(
        jnp.repeat(lookup(patch_wattage_category, wattage_per_category), TILE, axis=0), TILE, axis=1
    )
    source_vector = capacity_diagonal * earlier_heat_field
    source_vector = jnp.concatenate([source_vector[:1] + heat[None], source_vector[1:]], 0)
    coefficients = [(lateral, vertical, capacity_diagonal)]
    for level_index in range(LEVELS):
        last = coefficients[-1]
        coefficients.append((restrict(last[0]), restrict(last[1]), restrict(last[2])))
    coarse_lateral, coarse_vertical, coarse_storage = coefficients[LEVELS]
    stencils = []
    for level_index in range(LEVELS):
        level_coef = coefficients[level_index]
        padded = (
            extended(level_coef[0], (("gx", 1), ("gy", 2)), 2),
            extended(level_coef[1], (("gx", 1), ("gy", 2)), 2),
            extended(level_coef[2], (("gx", 1), ("gy", 2)), 2),
            extended(jnp.ones_like(level_coef[0]), (("gx", 1), ("gy", 2)), 2),
        )
        wide = stencil(padded[0], padded[1], padded[2], padded[3], 0.25**level_index)
        narrow = tuple((member[:, 1:-1, 1:-1] for member in wide))
        stencils.append((wide, narrow, parity(padded[0].shape), padded[3]))
    present_guess = earlier_heat_field
    saved = []
    for level_index in range(LEVELS):
        narrow = stencils[level_index][1]
        rhs_pad = extended(source_vector, (("gx", 1), ("gy", 2)), 2)
        present_guess = smooth(present_guess, rhs_pad, stencils[level_index])
        beside_all = extended(present_guess, (("gx", 1), ("gy", 2)), 1)
        residual = (
            source_vector - (narrow[6] * beside_all - coupled(beside_all, narrow))[:, 1:-1, 1:-1]
        )
        saved.append((present_guess, rhs_pad))
        source_vector = restrict(residual)
        present_guess = jnp.zeros_like(source_vector)
    whole = (
        lax.all_gather(source_vector, "gx", axis=1, tiled=True),
        lax.all_gather(coarse_lateral, "gx", axis=1, tiled=True),
        lax.all_gather(coarse_vertical, "gx", axis=1, tiled=True),
        lax.all_gather(coarse_storage, "gx", axis=1, tiled=True),
    )
    whole = (
        lax.all_gather(whole[0], "gy", axis=2, tiled=True),
        lax.all_gather(whole[1], "gy", axis=2, tiled=True),
        lax.all_gather(whole[2], "gy", axis=2, tiled=True),
        lax.all_gather(whole[3], "gy", axis=2, tiled=True),
    )
    whole_rhs = whole[0]
    whole_coef = (whole[1], whole[2], whole[3])
    coarse_weights = stencil(
        whole_coef[0], whole_coef[1], whole_coef[2], jnp.ones_like(whole_rhs), 0.25**LEVELS
    )
    solution = conjugate(whole_rhs, coarse_weights)
    start_row = lax.axis_index("gx") * source_vector.shape[1]
    start_col = lax.axis_index("gy") * source_vector.shape[2]
    correction = lax.dynamic_slice(
        solution, (jnp.int32(0), start_row, start_col), source_vector.shape
    )
    for level_index in reversed(range(LEVELS)):
        present_guess, rhs_pad = saved[level_index]
        present_guess = smooth(present_guess + prolong(correction), rhs_pad, stencils[level_index])
        correction = present_guess
    return correction


def solution(mesh):
    placed = (P(None, "gx", "gy"), P(None, "gx", "gy"), P("gx", "gy"), P(), P(), P(), P())
    return jax.shard_map(
        on_device, mesh=mesh, in_specs=placed, out_specs=P(None, "gx", "gy"), check_vma=False
    )
```

profile of v0, /device:TPU:0, one launch (start us, length us, event | category | flops | bytes accessed | tf_op | source)
XLA Modules:
  0.0 1525.3 jit_solution(2888406218585985499)
XLA Ops:
  10.8 6.4 fusion.553
  22.4 7.6 copy.1151
  30.0 12.5 fusion.554
  81.2 7.6 copy.1164
  88.8 12.5 fusion.555
  148.4 7.6 copy.1159
  172.1 12.5 fusion.557
  221.5 13.1 all-gather.6
  234.6 8.2 all-gather.7
  243.5 39.8 %select_add_fusion.3 = f32[8,8]{1,0:T(8,128)S(1)} fusion(s32[8,8]{1,0:T(8,128)S(1)} %copy-done.288, f32[]{:T(128)} %bitcast.71, f32[]{:T(128)} %bitcast.70, f32[]{:T(128)} %bitcast.69, f32[]{:T(128)} %bitcast.68, f32[]{:T(128)} %bitcast.67, f32[]{:T(128)} %bitcast.66, f32[]{:T(128)} %bitcast.65, f32[]{:T(128)} %bitcast.64, f32[]{:T(128)} %bitcast.63, ...), kind=kLoop, calls=%fused_computation.1216 | loop fusion | flops 12224 | bytes 768 | tf_op jit(solution)/shard_map/add | solution.py:88
  291.9 12.8 all-gather.4
  304.8 8.2 all-gather.5
  313.6 12.9 all-gather.2
  326.6 7.9 all-gather.3
  507.5 5.9 collective-permute-start.20
  560.2 6.2 collective-permute-start.42
  568.0 6.5 fusion.4
  642.8 8.5 copy.1146
  651.2 12.5 fusion.556
  663.8 5.6 copy.1277
  669.4 5.6 copy.1278
  675.0 5.6 copy.1279
  680.6 5.6 copy.1280
  755.7 6.7 collective-permute-done.59
  785.7 6.8 collective-permute-done.67
  874.2 5.7 collective-permute-done.91
  1008.6 5.8 collective-permute-start.126
  1154.9 13.4 all-gather
  1169.7 8.8 all-gather.1
  1450.4 5.8 collective-permute-done.227
  1470.8 5.8 collective-permute-done.231
  1500.5 6.5 collective-permute-start.236
  (1640 shorter events, 1191.9 us)
Async XLA Ops:
  0.8 530.3 %collective-permute-start = (f32[6,2,128]{1,2,0:T(8,128)}, f32[6,2,128]{1,2,0:T(8,128)}, u32[]{:S(2)}, u32[]{:S(2)}) collective-permute-start(f32[6,2,128]{1,2,0:T(8,128)} %broadcast.1280), channel_id=1, source_target_pairs={{0,4},{4,8},{8,12},{12,16},{16,20},{20,24},{24,28},{1,5},{5,9},{9,... | collective-permute-start | bytes 18440 | tf_op jit(solution)/shard_map/ppermute | solution.py:17
  3.9 532.0 %collective-permute-start.1 = (f32[6,2,128]{1,2,0:T(8,128)}, f32[6,2,128]{1,2,0:T(8,128)}, u32[]{:S(2)}, u32[]{:S(2)}) collective-permute-start(f32[6,2,128]{1,2,0:T(8,128)} %broadcast.1280), channel_id=1, source_target_pairs={{4,0},{8,4},{12,8},{16,12},{20,16},{24,20},{28,24},{5,1},{9,5},{13... | collective-permute-start | bytes 18440 | tf_op jit(solution)/shard_map/ppermute | solution.py:20
  74.7 261.4 %collective-permute-start.168 = (f32[6,2,4]{0,2,1:T(4,128)}, f32[6,2,4]{0,2,1:T(4,128)}, u32[]{:S(2)}, u32[]{:S(2)}) collective-permute-start(f32[6,2,4]{0,2,1:T(4,128)} %get-tuple-element.495), channel_id=1, source_target_pairs={{0,4},{4,8},{8,12},{12,16},{16,20},{20,24},{24,28},{1,5},{5,9},{9,... | collective-permute-start | bytes 584 | tf_op jit(solution)/shard_map/ppermute | solution.py:17
  79.7 258.1 %collective-permute-start.169 = (f32[6,2,4]{0,2,1:T(4,128)S(1)}, f32[6,2,4]{0,2,1:T(4,128)}, u32[]{:S(2)}, u32[]{:S(2)}) collective-permute-start(f32[6,2,4]{0,2,1:T(4,128)S(1)} %get-tuple-element.496), channel_id=1, source_target_pairs={{4,0},{8,4},{12,8},{16,12},{20,16},{24,20},{28,24},{5,1},{9,5},{13... | collective-permute-start | bytes 584 | tf_op jit(solution)/shard_map/ppermute | solution.py:20
  134.7 207.5 %collective-permute-start.180 = (f32[6,2,4]{0,2,1:T(4,128)}, f32[6,2,4]{0,2,1:T(4,128)S(1)}, u32[]{:S(2)}, u32[]{:S(2)}) collective-permute-start(f32[6,2,4]{0,2,1:T(4,128)} %get-tuple-element.497), channel_id=1, source_target_pairs={{0,4},{4,8},{8,12},{12,16},{16,20},{20,24},{24,28},{1,5},{5,9},{9,... | collective-permute-start | bytes 584 | tf_op jit(solution)/shard_map/ppermute | solution.py:17
  520.6 24.7 %collective-permute-start.10 = (f32[6,132,2]{1,2,0:T(2,128)S(1)}, f32[6,132,2]{1,2,0:T(2,128)S(1)}, u32[]{:S(2)}, u32[]{:S(2)}) collective-permute-start(f32[6,132,2]{1,2,0:T(2,128)S(1)} %get-tuple-element.173), channel_id=1, source_target_pairs={{0,1},{1,2},{2,3},{4,5},{5,6},{6,7},{8,9},{9,10},{10,11},{12,13},{... | collective-permute-start | bytes 19016 | tf_op jit(solution)/shard_map/ppermute | solution.py:17
  525.0 25.3 %collective-permute-start.11 = (f32[6,132,2]{1,2,0:T(2,128)S(1)}, f32[6,132,2]{1,2,0:T(2,128)S(1)}, u32[]{:S(2)}, u32[]{:S(2)}) collective-permute-start(f32[6,132,2]{1,2,0:T(2,128)S(1)} %get-tuple-element.174), channel_id=1, source_target_pairs={{1,0},{2,1},{3,2},{5,4},{6,5},{7,6},{9,8},{10,9},{11,10},{13,12},{... | collective-permute-start | bytes 19016 | tf_op jit(solution)/shard_map/ppermute | solution.py:20
  526.4 25.7 %collective-permute-start.6 = (f32[6,132,2]{1,2,0:T(2,128)S(1)}, f32[6,132,2]{1,2,0:T(2,128)S(1)}, u32[]{:S(2)}, u32[]{:S(2)}) collective-permute-start(f32[6,132,2]{1,2,0:T(2,128)S(1)} %get-tuple-element.177), channel_id=1, source_target_pairs={{0,1},{1,2},{2,3},{4,5},{5,6},{6,7},{8,9},{9,10},{10,11},{12,13},{... | collective-permute-start | bytes 19016 | tf_op jit(solution)/shard_map/ppermute | solution.py:17
  541.6 24.8 %collective-permute-start.22 = (f32[6,132,2]{1,2,0:T(2,128)S(1)}, f32[6,132,2]{1,2,0:T(2,128)S(1)}, u32[]{:S(2)}, u32[]{:S(2)}) collective-permute-start(f32[6,132,2]{1,2,0:T(2,128)S(1)} %get-tuple-element.175), channel_id=1, source_target_pairs={{0,1},{1,2},{2,3},{4,5},{5,6},{6,7},{8,9},{9,10},{10,11},{12,13},{... | collective-permute-start | bytes 19016 | tf_op jit(solution)/shard_map/ppermute | solution.py:17
  560.2 141.0 %collective-permute-start.42 = (f32[6,68,2]{2,1,0:T(8,128)}, f32[6,68,2]{2,1,0:T(8,128)}, u32[]{:S(2)}, u32[]{:S(2)}) collective-permute-start(f32[6,68,2]{2,1,0:T(8,128)} %get-tuple-element.253), channel_id=1, source_target_pairs={{0,1},{1,2},{2,3},{4,5},{5,6},{6,7},{8,9},{9,10},{10,11},{12,13},{... | collective-permute-start | bytes 9800 | tf_op jit(solution)/shard_map/ppermute | solution.py:17
  566.4 35.7 %collective-permute-start.51 = (f32[6,68,2]{2,1,0:T(8,128)}, f32[6,68,2]{2,1,0:T(8,128)}, u32[]{:S(2)}, u32[]{:S(2)}) collective-permute-start(f32[6,68,2]{2,1,0:T(8,128)} %get-tuple-element.260), channel_id=1, source_target_pairs={{1,0},{2,1},{3,2},{5,4},{6,5},{7,6},{9,8},{10,9},{11,10},{13,12},{... | collective-permute-start | bytes 9800 | tf_op jit(solution)/shard_map/ppermute | solution.py:20
  590.4 27.4 %collective-permute-start.46 = (f32[6,68,2]{1,2,0:T(2,128)S(1)}, f32[6,68,2]{1,2,0:T(2,128)S(1)}, u32[]{:S(2)}, u32[]{:S(2)}) collective-permute-start(f32[6,68,2]{1,2,0:T(2,128)S(1)} %copy-done.287), channel_id=1, source_target_pairs={{0,1},{1,2},{2,3},{4,5},{5,6},{6,7},{8,9},{9,10},{10,11},{12,13},{... | collective-permute-start | bytes 9800 | tf_op jit(solution)/shard_map/ppermute | solution.py:17
  617.8 84.7 %collective-permute-start.43 = (f32[6,68,2]{2,1,0:T(8,128)}, f32[6,68,2]{2,1,0:T(8,128)}, u32[]{:S(2)}, u32[]{:S(2)}) collective-permute-start(f32[6,68,2]{2,1,0:T(8,128)} %get-tuple-element.254), channel_id=1, source_target_pairs={{1,0},{2,1},{3,2},{5,4},{6,5},{7,6},{9,8},{10,9},{11,10},{13,12},{... | collective-permute-start | bytes 9800 | tf_op jit(solution)/shard_map/ppermute | solution.py:20
  619.9 98.5 %collective-permute-start.54 = (f32[6,68,2]{2,1,0:T(8,128)}, f32[6,68,2]{2,1,0:T(8,128)}, u32[]{:S(2)}, u32[]{:S(2)}) collective-permute-start(f32[6,68,2]{2,1,0:T(8,128)} %get-tuple-element.255), channel_id=1, source_target_pairs={{0,1},{1,2},{2,3},{4,5},{5,6},{6,7},{8,9},{9,10},{10,11},{12,13},{... | collective-permute-start | bytes 9800 | tf_op jit(solution)/shard_map/ppermute | solution.py:17
  712.2 112.2 %collective-permute-start.74 = (f32[6,36,2]{2,1,0:T(8,128)}, f32[6,36,2]{2,1,0:T(8,128)}, u32[]{:S(2)}, u32[]{:S(2)}) collective-permute-start(f32[6,36,2]{2,1,0:T(8,128)} %get-tuple-element.313), channel_id=1, source_target_pairs={{0,1},{1,2},{2,3},{4,5},{5,6},{6,7},{8,9},{9,10},{10,11},{12,13},{... | collective-permute-start | bytes 5192 | tf_op jit(solution)/shard_map/ppermute | solution.py:17
  739.4 29.8 %collective-permute-start.78 = (f32[6,36,2]{1,2,0:T(2,128)}, f32[6,36,2]{1,2,0:T(2,128)}, u32[]{:S(2)}, u32[]{:S(2)}) collective-permute-start(f32[6,36,2]{1,2,0:T(2,128)} %get-tuple-element.347), channel_id=1, source_target_pairs={{0,1},{1,2},{2,3},{4,5},{5,6},{6,7},{8,9},{9,10},{10,11},{12,13},{... | collective-permute-start | bytes 5192 | tf_op jit(solution)/shard_map/ppermute | solution.py:17
  744.6 27.5 %collective-permute-start.79 = (f32[6,36,2]{1,2,0:T(2,128)}, f32[6,36,2]{1,2,0:T(2,128)}, u32[]{:S(2)}, u32[]{:S(2)}) collective-permute-start(f32[6,36,2]{1,2,0:T(2,128)} %get-tuple-element.348), channel_id=1, source_target_pairs={{1,0},{2,1},{3,2},{5,4},{6,5},{7,6},{9,8},{10,9},{11,10},{13,12},{... | collective-permute-start | bytes 5192 | tf_op jit(solution)/shard_map/ppermute | solution.py:20
  769.3 56.3 %collective-permute-start.75 = (f32[6,36,2]{2,1,0:T(8,128)}, f32[6,36,2]{2,1,0:T(8,128)}, u32[]{:S(2)}, u32[]{:S(2)}) collective-permute-start(f32[6,36,2]{2,1,0:T(8,128)} %get-tuple-element.314), channel_id=1, source_target_pairs={{1,0},{2,1},{3,2},{5,4},{6,5},{7,6},{9,8},{10,9},{11,10},{13,12},{... | collective-permute-start | bytes 5192 | tf_op jit(solution)/shard_map/ppermute | solution.py:20
  772.0 68.6 %collective-permute-start.86 = (f32[6,36,2]{2,1,0:T(8,128)}, f32[6,36,2]{2,1,0:T(8,128)}, u32[]{:S(2)}, u32[]{:S(2)}) collective-permute-start(f32[6,36,2]{2,1,0:T(8,128)} %get-tuple-element.315), channel_id=1, source_target_pairs={{0,1},{1,2},{2,3},{4,5},{5,6},{6,7},{8,9},{9,10},{10,11},{12,13},{... | collective-permute-start | bytes 5192 | tf_op jit(solution)/shard_map/ppermute | solution.py:17
  834.7 102.9 %collective-permute-start.106 = (f32[6,20,2]{2,1,0:T(8,128)}, f32[6,20,2]{2,1,0:T(8,128)}, u32[]{:S(2)}, u32[]{:S(2)}) collective-permute-start(f32[6,20,2]{2,1,0:T(8,128)} %get-tuple-element.379), channel_id=1, source_target_pairs={{0,1},{1,2},{2,3},{4,5},{5,6},{6,7},{8,9},{9,10},{10,11},{12,13},{... | collective-permute-start | bytes 2888 | tf_op jit(solution)/shard_map/ppermute | solution.py:17
  860.6 25.6 %collective-permute-start.110 = (f32[6,20,2]{1,2,0:T(2,128)}, f32[6,20,2]{1,2,0:T(2,128)}, u32[]{:S(2)}, u32[]{:S(2)}) collective-permute-start(f32[6,20,2]{1,2,0:T(2,128)} %get-tuple-element.419), channel_id=1, source_target_pairs={{0,1},{1,2},{2,3},{4,5},{5,6},{6,7},{8,9},{9,10},{10,11},{12,13},{... | collective-permute-start | bytes 2888 | tf_op jit(solution)/shard_map/ppermute | solution.py:17
  886.2 52.6 %collective-permute-start.107 = (f32[6,20,2]{2,1,0:T(8,128)}, f32[6,20,2]{2,1,0:T(8,128)}, u32[]{:S(2)}, u32[]{:S(2)}) collective-permute-start(f32[6,20,2]{2,1,0:T(8,128)} %get-tuple-element.380), channel_id=1, source_target_pairs={{1,0},{2,1},{3,2},{5,4},{6,5},{7,6},{9,8},{10,9},{11,10},{13,12},{... | collective-permute-start | bytes 2888 | tf_op jit(solution)/shard_map/ppermute | solution.py:20
  889.0 66.1 %collective-permute-start.118 = (f32[6,20,2]{2,1,0:T(8,128)}, f32[6,20,2]{2,1,0:T(8,128)}, u32[]{:S(2)}, u32[]{:S(2)}) collective-permute-start(f32[6,20,2]{2,1,0:T(8,128)} %get-tuple-element.381), channel_id=1, source_target_pairs={{0,1},{1,2},{2,3},{4,5},{5,6},{6,7},{8,9},{9,10},{10,11},{12,13},{... | collective-permute-start | bytes 2888 | tf_op jit(solution)/shard_map/ppermute | solution.py:17
  930.1 29.1 %collective-permute-start.119 = (f32[6,20,2]{2,1,0:T(8,128)}, f32[6,20,2]{2,1,0:T(8,128)}, u32[]{:S(2)}, u32[]{:S(2)}) collective-permute-start(f32[6,20,2]{2,1,0:T(8,128)} %get-tuple-element.382), channel_id=1, source_target_pairs={{1,0},{2,1},{3,2},{5,4},{6,5},{7,6},{9,8},{10,9},{11,10},{13,12},{... | collective-permute-start | bytes 2888 | tf_op jit(solution)/shard_map/ppermute | solution.py:20
  948.5 141.1 %collective-permute-start.170 = (f32[6,8,2]{0,2,1:T(2,128)}, f32[6,8,2]{0,2,1:T(2,128)}, u32[]{:S(2)}, u32[]{:S(2)}) collective-permute-start(f32[6,8,2]{0,2,1:T(2,128)} %get-tuple-element.481), channel_id=1, source_target_pairs={{0,1},{1,2},{2,3},{4,5},{5,6},{6,7},{8,9},{9,10},{10,11},{12,13},{... | collective-permute-start | bytes 1160 | tf_op jit(solution)/shard_map/ppermute | solution.py:17
  955.1 39.0 %collective-permute-start.138 = (f32[6,12,2]{0,2,1:T(2,128)}, f32[6,12,2]{0,2,1:T(2,128)S(1)}, u32[]{:S(2)}, u32[]{:S(2)}) collective-permute-start(f32[6,12,2]{0,2,1:T(2,128)} %get-tuple-element.401), channel_id=1, source_target_pairs={{0,1},{1,2},{2,3},{4,5},{5,6},{6,7},{8,9},{9,10},{10,11},{12,13},{... | collective-permute-start | bytes 1736 | tf_op jit(solution)/shard_map/ppermute | solution.py:17
  959.2 38.1 %collective-permute-start.139 = (f32[6,12,2]{0,2,1:T(2,128)}, f32[6,12,2]{0,2,1:T(2,128)S(1)}, u32[]{:S(2)}, u32[]{:S(2)}) collective-permute-start(f32[6,12,2]{0,2,1:T(2,128)} %get-tuple-element.402), channel_id=1, source_target_pairs={{1,0},{2,1},{3,2},{5,4},{6,5},{7,6},{9,8},{10,9},{11,10},{13,12},{... | collective-permute-start | bytes 1736 | tf_op jit(solution)/shard_map/ppermute | solution.py:20
  986.1 33.5 %collective-permute-start.150 = (f32[6,12,2]{0,2,1:T(2,128)}, f32[6,12,2]{0,2,1:T(2,128)S(1)}, u32[]{:S(2)}, u32[]{:S(2)}) collective-permute-start(f32[6,12,2]{0,2,1:T(2,128)} %get-tuple-element.405), channel_id=1, source_target_pairs={{0,1},{1,2},{2,3},{4,5},{5,6},{6,7},{8,9},{9,10},{10,11},{12,13},{... | collective-permute-start | bytes 1736 | tf_op jit(solution)/shard_map/ppermute | solution.py:17
  990.5 30.4 %collective-permute-start.151 = (f32[6,12,2]{0,2,1:T(2,128)}, f32[6,12,2]{0,2,1:T(2,128)S(1)}, u32[]{:S(2)}, u32[]{:S(2)}) collective-permute-start(f32[6,12,2]{0,2,1:T(2,128)} %get-tuple-element.406), channel_id=1, source_target_pairs={{1,0},{2,1},{3,2},{5,4},{6,5},{7,6},{9,8},{10,9},{11,10},{13,12},{... | collective-permute-start | bytes 1736 | tf_op jit(solution)/shard_map/ppermute | solution.py:20
  1019.6 73.0 %collective-permute-start.171 = (f32[6,8,2]{0,2,1:T(2,128)}, f32[6,8,2]{0,2,1:T(2,128)S(1)}, u32[]{:S(2)}, u32[]{:S(2)}) collective-permute-start(f32[6,8,2]{0,2,1:T(2,128)} %get-tuple-element.482), channel_id=1, source_target_pairs={{1,0},{2,1},{3,2},{5,4},{6,5},{7,6},{9,8},{10,9},{11,10},{13,12},{... | collective-permute-start | bytes 1160 | tf_op jit(solution)/shard_map/ppermute | solution.py:20
  1020.9 80.7 %collective-permute-start.182 = (f32[6,8,2]{0,2,1:T(2,128)}, f32[6,8,2]{0,2,1:T(2,128)S(1)}, u32[]{:S(2)}, u32[]{:S(2)}) collective-permute-start(f32[6,8,2]{0,2,1:T(2,128)} %get-tuple-element.483), channel_id=1, source_target_pairs={{0,1},{1,2},{2,3},{4,5},{5,6},{6,7},{8,9},{9,10},{10,11},{12,13},{... | collective-permute-start | bytes 1160 | tf_op jit(solution)/shard_map/ppermute | solution.py:17
  1082.3 27.7 %collective-permute-start.183 = (f32[6,8,2]{0,2,1:T(2,128)S(1)}, f32[6,8,2]{0,2,1:T(2,128)S(1)}, u32[]{:S(2)}, u32[]{:S(2)}) collective-permute-start(f32[6,8,2]{0,2,1:T(2,128)S(1)} %copy-done.280), channel_id=1, source_target_pairs={{1,0},{2,1},{3,2},{5,4},{6,5},{7,6},{9,8},{10,9},{11,10},{13,12},{... | collective-permute-start | bytes 1160 | tf_op jit(solution)/shard_map/ppermute | solution.py:20
  (512 other events, 13995.4 us)
where the time goes:
time: 1550 us; the launch traced here: 1530 us
  starting transfers between devices  622 us (40%)
  local copies, waits for them, and re-layouts  344 us (22%)
  other arithmetic  254 us (16%)
  waiting for transfers between devices  183 us (12%)
  blocking collectives  85.3 us (6%)
  between operations  36.7 us (2%)
    ppermute x120, starting transfers between devices, extended(): lax.ppermute(lax.slice_in_dim(block, block.shape[dim] - width, None, axis...  465 us
    ppermute x120, waiting for transfers between devices, extended(): lax.ppermute(lax.slice_in_dim(block, 0, width, axis=dim), axis, backward)  168 us
    ppermute x120, starting transfers between devices, extended(): lax.ppermute(lax.slice_in_dim(block, 0, width, axis=dim), axis, backward)  157 us
    unnamed x658, local copies, waits for them, and re-layouts  122 us
    slice x19, local copies, waits for them, and re-layouts, restrict(): blocks[:, :, 1, :, 0]  77 us
    select_n x48, other arithmetic, update(): return jnp.where(chosen, candidate, beside_all)  54.1 us
    add x3, other arithmetic, lookup(): summed = summed + jnp.where(labels == number, entries[number], 0.0)  50.2 us
    concatenate x83, other arithmetic, extended(): block = jnp.concatenate([low, block, high], axis=dim)  36 us
  transfers between devices with their start and end apart: 240, of which 66 were waited for; matrix products, arithmetic and copies ran while one was open for 31% of the time, Pallas kernels for 0%

commit v1 on v0

v1 whole, which is shorter than its diff:
```python
import functools

import jax
import jax.numpy as jnp
from jax import lax
from jax.experimental import pallas as pl
from jax.experimental.pallas import tpu as pltpu
from jax.sharding import PartitionSpec as P

TILE = 16
LEVELS = 6
LOCAL = 3
COARSE_ITERS = 12
LANES = 128
PAD = 8
HI = lax.Precision.HIGHEST
F32 = jnp.float32
VMEM = pl.BlockSpec(memory_space=pltpu.VMEM)
SMEM = pl.BlockSpec(memory_space=pltpu.SMEM)
PARAMS = pltpu.CompilerParams(vmem_limit_bytes=60 * 1024 * 1024)


def up8(n):
    return -(-n // 8) * 8


def halo_cells():
    need, above = [], 0
    for level in range(LOCAL):
        need.append(above + 4)
        above = -(-need[-1] // 2)
    f = 0
    for level in reversed(range(LOCAL)):
        inner = max(need[level], 2 * f + 1)
        f = inner + (4 if level == 0 else 3)
    unit = 2**LOCAL
    return -(-f // unit) * unit


def iota(shape, axis):
    return lax.broadcasted_iota(jnp.int32, shape, axis)


def rows(t, off=0):
    return pl.ds(pl.multiple_of(t * 8, 8) + (PAD + off), 8)


def dot(a, b):
    return jnp.dot(a, b, precision=HI, preferred_element_type=F32)


def prep_kernel(par, watt, cat_ref, u_ref, sub_ref, heat_ref, a_ref, b_ref, *, halo):
    layers, height, width = u_ref.shape
    cat = cat_ref[...]
    power = jnp.zeros(cat.shape, F32)
    for n in range(watt.shape[0]):
        power = power + jnp.where(cat == n, watt[n], 0.0)
    spread_r = (iota((height, cat.shape[0]), 0) // TILE == iota((height, cat.shape[0]), 1)).astype(F32)
    spread_c = (iota((cat.shape[1], width), 1) // TILE == iota((cat.shape[1], width), 0)).astype(F32)
    heat_ref[...] = dot(dot(spread_r, power), spread_c)
    even = par[0] == 0
    for q in range(2 * layers + 1):
        if q < layers:
            plane = u_ref[q]
        elif q < 2 * layers:
            plane = (sub_ref[q - layers] + 1).astype(F32)
        else:
            plane = heat_ref[...]
        turned = plane.T
        low, high = turned[:halo], turned[width - halo :]
        a_ref[q] = jnp.where(even, high, low)
        b_ref[q] = jnp.where(even, low, high)


def split_kernel(par, u_ref, sub_ref, heat_ref, ra, rb, out, a_ref, b_ref, scr, *, halo):
    layers, height, width = u_ref.shape
    even_y, even_x = par[0] == 0, par[1] == 0
    half, hh = height // 2, halo // 2
    source, target = iota((width + LANES, 2 * LANES), 0), iota((width + LANES, 2 * LANES), 1)
    cell = 2 * (target % LANES) + target // LANES
    want = jnp.where(
        cell < halo, width + cell, jnp.where(cell < halo + width, cell - halo, cell)
    )
    pick = ((source == want) & (cell < 2 * halo + width)).astype(F32)
    for q in range(2 * layers + 1):
        if q < layers:
            plane = u_ref[q]
        elif q < 2 * layers:
            plane = (sub_ref[q - layers] + 1).astype(F32)
        else:
            plane = heat_ref[...]
        left = jnp.where(even_y, rb[q], ra[q])
        right = jnp.where(even_y, ra[q], rb[q])
        sides = jnp.concatenate([left, right, jnp.zeros((LANES - 2 * halo, height), F32)], 0).T
        both = dot(jnp.concatenate([plane, sides], 1), pick)
        scr[0] = both[:, :LANES]
        scr[1] = both[:, LANES:]
        for p in range(2):
            for j in range(2):
                z = scr[j, pl.ds(p, half, stride=2), :]
                out[q, 2 * p + j] = z
                at = (4 * q + 2 * p + j) * hh
                first, last = z[:hh], z[half - hh :]
                a_ref[at : at + hh] = jnp.where(even_x, last, first)
                b_ref[at : at + hh] = jnp.where(even_x, first, last)


def split_sum(s, p, j, k, t, layers):
    u = s["u"]
    at = rows(t)
    total = s["fri"][j, k, at] * u[2 * (1 - p) + j, k, at]
    if p == 0:
        total += s["fro"][j, k, at] * u[2 + j, k, rows(t, -1)]
    else:
        total += s["fro"][j, k, rows(t, 1)] * u[j, k, rows(t, 1)]
    total += s["fci"][p, k, at] * u[2 * p + 1 - j, k, at]
    if j == 0:
        total += s["fco"][p, k, at] * pltpu.roll(u[2 * p + 1, k, at], 1, 1)
    else:
        total += s["fcr"][p, k, at] * pltpu.roll(u[2 * p, k, at], LANES - 1, 1)
    pj = 2 * p + j
    if k > 0:
        total += s["fl"][pj, k, at] * u[pj, k - 1, at]
    if k < layers - 1:
        total += s["fl"][pj, k + 1, at] * u[pj, k + 1, at]
    return total


def split_half(s, colour, lo, hi, layers):
    def body(t, carry):
        for k in range(layers):
            for p in range(2):
                for j in range(2):
                    if (p + j + k) % 2 == colour:
                        pj = 2 * p + j
                        total = s["f"][pj, k, rows(t)] + split_sum(s, p, j, k, t, layers)
                        s["u"][pj, k, rows(t)] = total * s["invd"][pj, k, rows(t)]
        return carry

    lax.fori_loop(lo, hi, body, 0)


def sides_of(tiles, lane):
    count = len(tiles)
    turned_r = [pltpu.roll(x, 1, 1) for x in tiles]
    turned_l = [pltpu.roll(x, LANES - 1, 1) for x in tiles]
    left = [
        jnp.where(lane == 0, turned_r[i - 1] if i else 0.0, turned_r[i]) for i in range(count)
    ]
    right = [
        jnp.where(lane == LANES - 1, turned_l[i + 1] if i < count - 1 else 0.0, turned_l[i])
        for i in range(count)
    ]
    return left, right


def nat_setup(s, factor):
    tiles, layers, height, _ = s["lat"].shape
    lane = iota((8, LANES), 1)
    c = 0.5 * factor

    def body(t, carry):
        for k in range(layers):
            lat = [s["lat"][i, k, rows(t)] for i in range(tiles)]
            left, right = sides_of(lat, lane)
            for i in range(tiles):
                stor = s["stor"][i, k, rows(t)]
                above = c * (lat[i] + s["lat"][i, k, rows(t, -1)])
                below = c * (lat[i] + s["lat"][i, k, rows(t, 1)])
                before, after = c * (lat[i] + left[i]), c * (lat[i] + right[i])
                diag = stor + above + below + before + after
                vert = s["vert"][i, k, rows(t)]
                if k > 0:
                    face = 0.5 * (vert + s["vert"][i, k - 1, rows(t)])
                    s["wl"][i, k, rows(t)] = face
                    diag += face
                if k < layers - 1:
                    diag += 0.5 * (vert + s["vert"][i, k + 1, rows(t)])
                inside = stor > 0.0
                s["wr"][i, k, rows(t)] = above
                s["wc"][i, k, rows(t)] = before
                s["wcr"][i, k, rows(t)] = after
                s["diag"][i, k, rows(t)] = diag
                s["invd"][i, k, rows(t)] = jnp.where(inside, 1.0 / jnp.where(inside, diag, 1.0), 0.0)
        return carry

    s["wr"][:, :, height - PAD :] = jnp.zeros((tiles, layers, PAD, LANES), F32)
    lax.fori_loop(0, (height - 2 * PAD) // 8, body, 0)


def nat_sum(s, mid, sides, i, k, t, layers):
    u = s["u"]
    total = s["wr"][i, k, rows(t)] * u[i, k, rows(t, -1)]
    total += s["wr"][i, k, rows(t, 1)] * u[i, k, rows(t, 1)]
    total += s["wc"][i, k, rows(t)] * sides[k][0][i] + s["wcr"][i, k, rows(t)] * sides[k][1][i]
    if k > 0:
        total += s["wl"][i, k, rows(t)] * mid[k - 1][i]
    if k < layers - 1:
        total += s["wl"][i, k + 1, rows(t)] * mid[k + 1][i]
    return total


def nat_half(s, colour, lo, hi):
    tiles, layers = s["u"].shape[:2]
    lane = iota((8, LANES), 1)
    odd = (iota((8, LANES), 0) + lane) % 2

    def body(t, carry):
        mid = [[s["u"][i, k, rows(t)] for i in range(tiles)] for k in range(layers)]
        sides = [sides_of(m, lane) for m in mid]
        for k in range(layers):
            chosen = odd == (colour + k) % 2
            for i in range(tiles):
                total = s["f"][i, k, rows(t)] + nat_sum(s, mid, sides, i, k, t, layers)
                s["u"][i, k, rows(t)] = jnp.where(chosen, total * s["invd"][i, k, rows(t)], mid[k][i])
        return carry

    lax.fori_loop(lo, hi, body, 0)


def nat_first(s, lo, hi):
    tiles, layers, height, _ = s["u"].shape
    odd = (iota((8, LANES), 0) + iota((8, LANES), 1)) % 2
    zeros = jnp.zeros((tiles, layers, PAD, LANES), F32)
    s["u"][:, :, :PAD] = zeros
    s["u"][:, :, height - PAD :] = zeros

    def body(t, carry):
        for k in range(layers):
            for i in range(tiles):
                value = s["f"][i, k, rows(t)] * s["invd"][i, k, rows(t)]
                s["u"][i, k, rows(t)] = jnp.where(odd == k % 2, value, 0.0)
        return carry

    lax.fori_loop(lo, hi, body, 0)


def nat_residual(s, res, lo, hi):
    tiles, layers = s["u"].shape[:2]
    lane = iota((8, LANES), 1)

    def body(t, carry):
        mid = [[s["u"][i, k, rows(t)] for i in range(tiles)] for k in range(layers)]
        sides = [sides_of(m, lane) for m in mid]
        for k in range(layers):
            for i in range(tiles):
                total = s["f"][i, k, rows(t)] + nat_sum(s, mid, sides, i, k, t, layers)
                res[i, k, rows(t)] = total - s["diag"][i, k, rows(t)] * mid[k][i]
        return carry

    lax.fori_loop(lo, hi, body, 0)


def nat_down(s, res, steps):
    nat_first(s, 0, steps)
    for colour in (1, 0, 1):
        nat_half(s, colour, 0, steps)
    nat_residual(s, res, 0, steps)


def restrict_to(source, target):
    tiles, layers = source.shape[:2]
    count, height = target.shape[0], target.shape[2] - 2 * PAD
    zeros = jnp.zeros((count, layers, PAD, LANES), F32)
    target[:, :, :PAD] = zeros
    target[:, :, PAD + height :] = zeros
    cell = iota((LANES, LANES), 0) // 2
    for k in range(layers):
        parts = [
            source[i, k, pl.ds(PAD, height, stride=2), :]
            + source[i, k, pl.ds(PAD + 1, height, stride=2), :]
            for i in range(tiles)
        ]
        for o in range(count):
            total = None
            for i in range(tiles):
                shift = LANES // 2 * i - LANES * o
                if -LANES < shift < LANES:
                    pick = jnp.where(cell + shift == iota((LANES, LANES), 1), 0.25, 0.0)
                    part = dot(parts[i], pick)
                    total = part if total is None else total + part
            target[o, k, PAD : PAD + height] = total


def prolong_into(s, u_in, coarse, mask):
    tiles, layers, height, _ = s["u"].shape
    n = (height - 2 * PAD) // 2
    cell = iota((LANES, LANES), 1) // 2
    for i in range(tiles):
        o = i // 2
        shift = LANES // 2 * (i % 2)
        pick = (cell + shift == iota((LANES, LANES), 0)).astype(F32)
        for k in range(layers):
            wide = dot(coarse(o, k)[:n], pick)
            for p in range(2):
                at = pl.ds(PAD + p, n, stride=2)
                add = wide
                if mask:
                    add = jnp.where(s["invd"][i, k, at, :] > 0.0, wide, 0.0)
                s["u"][i, k, at, :] = u_in[i, k, at, :] + add


def nat_up(s, lo, hi):
    for sweep in range(2):
        nat_half(s, 0, lo, hi)
        nat_half(s, 1, lo, hi)


SPLIT_KEPT = ("u", "f", "invd", "fri", "fro", "fci", "fco", "fcr", "fl")
NAT_KEPT = ("u", "f", "invd", "wr", "wc", "wcr", "wl")
NAT_OTHER = ("lat", "vert", "stor", "diag")


def down_kernel(par, tables, *refs, halo, half, kinds):
    refs = list(refs)
    sp, ra, rb = refs[:3]
    refs = refs[3:]
    s = dict(zip(SPLIT_KEPT, refs[: len(SPLIT_KEPT)]))
    refs = refs[len(SPLIT_KEPT) :]
    nats = []
    for level in range(1, LOCAL):
        nats.append(dict(zip(NAT_KEPT, refs[: len(NAT_KEPT)])))
        refs = refs[len(NAT_KEPT) :]
    payload = refs.pop(0)
    for name in ("lat", "vert", "stor"):
        s[name] = refs.pop(0)
    heat = refs.pop(0)
    for level in range(1, LOCAL):
        for name in NAT_OTHER:
            nats[level - 1][name] = refs.pop(0)
    ress = [refs.pop(0) for level in range(1, LOCAL)]
    layers = s["u"].shape[1]
    height = s["u"].shape[2]
    hh = halo // 2
    steps = (height - 2 * PAD) // 8
    even = par[0] == 0
    zeros = jnp.zeros((PAD, LANES), F32)

    def place(ref, index, q, pj):
        at = (4 * q + pj) * hh
        first, second = ra[at : at + hh], rb[at : at + hh]
        ref[index + (slice(PAD, PAD + hh),)] = jnp.where(even, second, first)
        ref[index + (slice(PAD + hh, PAD + hh + half),)] = sp[q, pj]
        ref[index + (slice(PAD + hh + half, PAD + 2 * hh + half),)] = jnp.where(even, first, second)

    for pj in range(4):
        for k in range(layers):
            for name in ("u", "lat"):
                s[name][pj, k, :PAD] = zeros
                s[name][pj, k, height - PAD :] = zeros
            place(s["u"], (pj, k), k, pj)
            place(s["stor"], (pj, k), layers + k, pj)
        place(heat, (pj,), 2 * layers, pj)
    for j in range(2):
        for k in range(layers):
            s["fro"][j, k, height - PAD :] = zeros

    first = nats[0]
    clear = [first[name] for name in ("lat", "vert", "stor", "f")] + ress
    for ref in clear:
        for k in range(layers):
            ref[0, k, :PAD] = zeros
            ref[0, k, ref.shape[2] - PAD :] = zeros

    def look(t, carry):
        for k in range(layers):
            sums = [None, None, None]
            for pj in range(4):
                at = (pj, k, rows(t))
                label = s["stor"][at]
                value = [jnp.zeros_like(label)] * 3
                for n in range(kinds):
                    hit = label == float(n + 1)
                    value = [jnp.where(hit, tables[i * kinds + n], value[i]) for i in range(3)]
                for i, name in enumerate(("lat", "vert", "stor")):
                    s[name][at] = value[i]
                    sums[i] = value[i] if sums[i] is None else sums[i] + value[i]
                f = value[2] * s["u"][at]
                if k == 0:
                    f = f + heat[pj, rows(t)]
                s["f"][at] = f
            for i, name in enumerate(("lat", "vert", "stor")):
                first[name][0, k, rows(t)] = sums[i] * 0.25
        return carry

    lax.fori_loop(0, steps, look, 0)

    def faces(t, carry):
        at = rows(t)
        for k in range(layers):
            lat = [s["lat"][pj, k, at] for pj in range(4)]
            inner_r = [0.5 * (lat[j] + lat[2 + j]) for j in range(2)]
            before_r = [0.5 * (s["lat"][2 + j, k, rows(t, -1)] + lat[j]) for j in range(2)]
            after_r = [0.5 * (lat[2 + j] + s["lat"][j, k, rows(t, 1)]) for j in range(2)]
            inner_c = [0.5 * (lat[2 * p] + lat[2 * p + 1]) for p in range(2)]
            before_c = [0.5 * (pltpu.roll(lat[2 * p + 1], 1, 1) + lat[2 * p]) for p in range(2)]
            after_c = [0.5 * (lat[2 * p + 1] + pltpu.roll(lat[2 * p], LANES - 1, 1)) for p in range(2)]
            for x in range(2):
                s["fri"][x, k, at] = inner_r[x]
                s["fro"][x, k, at] = before_r[x]
                s["fci"][x, k, at] = inner_c[x]
                s["fco"][x, k, at] = before_c[x]
                s["fcr"][x, k, at] = after_c[x]
            for p in range(2):
                for j in range(2):
                    pj = 2 * p + j
                    stor = s["stor"][pj, k, at]
                    diag = stor + inner_r[j] + (after_r[j] if p else before_r[j])
                    diag += inner_c[p] + (after_c[p] if j else before_c[p])
                    vert = s["vert"][pj, k, at]
                    if k > 0:
                        face = 0.5 * (vert + s["vert"][pj, k - 1, at])
                        s["fl"][pj, k, at] = face
                        diag += face
                    if k < layers - 1:
                        diag += 0.5 * (vert + s["vert"][pj, k + 1, at])
                    inside = stor > 0.0
                    s["invd"][pj, k, at] = jnp.where(inside, 1.0 / jnp.where(inside, diag, 1.0), 0.0)
                    s["stor"][pj, k, at] = diag
        return carry

    lax.fori_loop(0, steps, faces, 0)
    for sweep in range(2):
        split_half(s, 0, 0, steps, layers)
        split_half(s, 1, 0, steps, layers)

    def remain(t, carry):
        for k in range(layers):
            total = None
            for p in range(2):
                for j in range(2):
                    if (p + j + k) % 2 == 0:
                        pj = 2 * p + j
                        r = s["f"][pj, k, rows(t)] + split_sum(s, p, j, k, t, layers)
                        r -= s["stor"][pj, k, rows(t)] * s["u"][pj, k, rows(t)]
                        total = r if total is None else total + r
            first["f"][0, k, rows(t)] = total * 0.25
        return carry

    lax.fori_loop(0, steps, remain, 0)

    for level in range(1, LOCAL):
        now = nats[level - 1]
        nat_setup(now, 0.25**level)
        count = (now["u"].shape[2] - 2 * PAD) // 8
        nat_down(now, ress[level - 1], count)
        if level < LOCAL - 1:
            below = nats[level]
            for name in ("lat", "vert", "stor"):
                restrict_to(now[name], below[name])
            restrict_to(ress[level - 1], below["f"])

    last, res = nats[-1], ress[-1]
    mine = 2 * half >> LOCAL
    off = halo >> (LOCAL - 1)
    group = 4 * mine
    per = LANES // group
    quantities = (res, last["lat"], last["vert"], last["stor"])
    source, target = iota((LANES, LANES), 0), iota((LANES, LANES), 1)
    for pair in range(-(-layers // per)):
        total = jnp.zeros((mine, LANES), F32)
        for inner in range(per):
            k = pair * per + inner
            if k < layers:
                for n, ref in enumerate(quantities):
                    base = inner * group + n * mine
                    hit = (target >= base) & (target < base + mine)
                    hit &= (source - off >= 0) & ((source - off) // 2 == target - base)
                    pick = jnp.where(hit, 0.25, 0.0)
                    part = ref[0, k, pl.ds(PAD + off, mine, stride=2), :]
                    part += ref[0, k, pl.ds(PAD + off + 1, mine, stride=2), :]
                    total += dot(part, pick)
        payload[pair * mine : (pair + 1) * mine] = total


def conjugate(s):
    tiles, layers, height, _ = s["u"].shape
    n = height - 2 * PAD
    row, lane = iota((n, LANES), 0), iota((n, LANES), 1)
    spots = [(i, k) for k in range(layers) for i in range(tiles)]
    body_rows = slice(PAD, PAD + n)

    def apply(v):
        out = []
        for k in range(layers):
            tiles_of = [v[k * tiles + i] for i in range(tiles)]
            left, right = sides_of(tiles_of, lane)
            for i in range(tiles):
                mid = tiles_of[i]
                wr = s["wr"][i, k, body_rows]
                wr_next = s["wr"][i, k, slice(PAD + 1, PAD + 1 + n)]
                total = wr * jnp.where(row == 0, 0.0, pltpu.roll(mid, 1, 0))
                total += wr_next * jnp.where(row == n - 1, 0.0, pltpu.roll(mid, n - 1, 0))
                total += s["wc"][i, k, body_rows] * left[i] + s["wcr"][i, k, body_rows] * right[i]
                if k > 0:
                    total += s["wl"][i, k, body_rows] * v[(k - 1) * tiles + i]
                if k < layers - 1:
                    total += s["wl"][i, k + 1, body_rows] * v[(k + 1) * tiles + i]
                out.append(s["diag"][i, k, body_rows] * mid - total)
        return out

    def inner(a, b):
        total = a[0] * b[0]
        for x, y in zip(a[1:], b[1:]):
            total += x * y
        total = jnp.sum(total, axis=0, keepdims=True)
        return jnp.sum(total, axis=1, keepdims=True)

    inv = [s["invd"][i, k, body_rows] for i, k in spots]
    inside = [x > 0.0 for x in inv]
    r = [jnp.where(inside[m], s["f"][i, k, body_rows], 0.0) for m, (i, k) in enumerate(spots)]
    z = [x * y for x, y in zip(r, inv)]
    count = len(spots)

    def step(_, carry):
        e, r, p, rz = carry[:count], carry[count : 2 * count], carry[2 * count : 3 * count], carry[-1]
        q = apply(p)
        alpha = rz / inner(p, q)
        e = [x + alpha * y for x, y in zip(e, p)]
        r = [jnp.where(m, x - alpha * y, 0.0) for m, x, y in zip(inside, r, q)]
        z = [x * s["invd"][i, k, body_rows] for x, (i, k) in zip(r, spots)]
        fresh = inner(r, z)
        beta = fresh / rz
        p = [x + beta * y for x, y in zip(z, p)]
        return (*e, *r, *p, fresh)

    start = (*[jnp.zeros_like(x) for x in r], *r, *z, inner(r, z))
    out = lax.fori_loop(0, COARSE_ITERS, step, start)
    for (i, k), value in zip(spots, out[:count]):
        s["u"][i, k, body_rows] = value


WHOLE = ("u", "f", "invd", "wr", "wc", "wcr", "wl", "lat", "vert", "stor", "diag")


def up_kernel(place, *refs, halo, half, spans):
    refs = list(refs)
    gathered = refs.pop(0)
    s = dict(zip(SPLIT_KEPT, refs[: len(SPLIT_KEPT)]))
    refs = refs[len(SPLIT_KEPT) :]
    nats = []
    for level in range(1, LOCAL):
        nats.append(dict(zip(NAT_KEPT, refs[: len(NAT_KEPT)])))
        refs = refs[len(NAT_KEPT) :]
    out = refs.pop(0)
    wholes = []
    for level in range(LOCAL, LEVELS + 1):
        wholes.append(dict(zip(WHOLE, refs[: len(WHOLE)])))
        refs = refs[len(WHOLE) :]
    ress = [refs.pop(0) for level in range(LOCAL, LEVELS)]
    fresh = [refs.pop(0) for level in range(LOCAL)]
    wider = refs.pop(0)
    nx, ny = spans
    layers = s["u"].shape[1]
    top = wholes[0]
    tiles, _, tall, _ = top["u"].shape
    mine = 2 * half >> LOCAL
    group = 4 * mine
    per = LANES // group
    lane = iota((mine, LANES), 1)

    for whole in wholes:
        count, _, height, _ = whole["u"].shape
        for name in ("u", "lat"):
            zeros = jnp.zeros((count, layers, PAD, LANES), F32)
            whole[name][:, :, :PAD] = zeros
            whole[name][:, :, height - PAD :] = zeros

    def gather(x, carry):
        at = pl.ds(pl.multiple_of(x * mine, 8) + PAD, mine)
        for k in range(layers):
            for n, name in enumerate(("f", "lat", "vert", "stor")):
                base = (k % per) * group + n * mine
                lines = slice((k // per) * mine, (k // per + 1) * mine)
                for i in range(tiles):
                    total = jnp.zeros((mine, LANES), F32)
                    for y in range(ny):
                        if y * mine // LANES == i:
                            to = y * mine % LANES
                            part = gathered[x * ny + y, lines]
                            if to != base:
                                part = pltpu.roll(part, (to - base) % LANES, 1)
                            total = jnp.where((lane >= to) & (lane < to + mine), part, total)
                    top[name][i, k, at] = total
        return carry

    lax.fori_loop(0, nx, gather, 0)

    for n, level in enumerate(range(LOCAL, LEVELS)):
        now, below = wholes[n], wholes[n + 1]
        nat_setup(now, 0.25**level)
        nat_down(now, ress[n], (now["u"].shape[2] - 2 * PAD) // 8)
        for name in ("lat", "vert", "stor"):
            restrict_to(now[name], below[name])
        restrict_to(ress[n], below["f"])
    nat_setup(wholes[-1], 0.25**LEVELS)
    conjugate(wholes[-1])
    for n in reversed(range(len(wholes) - 1)):
        now, below = wholes[n], wholes[n + 1]
        prolong_into(now, now["u"], lambda o, k: below["u"][o, k, PAD : below["u"].shape[2] - PAD], False)
        nat_up(now, 0, (now["u"].shape[2] - 2 * PAD) // 8)

    x, y = place[0], place[1]
    reach = halo >> LOCAL
    need = (nats[-1]["u"].shape[2] - 2 * PAD) // 2
    height = top["u"].shape[2]
    for i in range(tiles):
        for k in range(layers):
            wider[i, k, :height] = top["u"][i, k]
            wider[i, k, height:] = jnp.zeros((PAD, LANES), F32)
    begin = PAD + x * mine - reach
    shift = y * mine - reach

    def window(o, k):
        parts = [wider[i, k, pl.ds(begin, need)] for i in range(tiles)]
        turn = lax.rem(4 * LANES - shift, LANES)
        lanes = iota((need, LANES), 1)
        first = lax.div(shift + LANES, LANES) - 1
        value = jnp.zeros((need, LANES), F32)
        for i in range(tiles):
            moved = pltpu.roll(parts[i], turn, 1)
            value = jnp.where((first == i) & (lanes < turn) | (first == i) & (turn == 0), moved, value)
            value = jnp.where((first == i - 1) & (lanes >= turn) & (turn != 0), moved, value)
        return value

    coarse = window
    for level in reversed(range(1, LOCAL)):
        now = dict(nats[level - 1])
        before = now["u"]
        now["u"] = fresh[level]
        height = before.shape[2]
        for i in range(before.shape[0]):
            for k in range(layers):
                now["u"][i, k, :PAD] = jnp.zeros((PAD, LANES), F32)
                now["u"][i, k, height - PAD :] = jnp.zeros((PAD, LANES), F32)
        prolong_into(now, before, coarse, level == LOCAL - 1)
        side = halo >> level
        own = 2 * half >> level
        margin = {0: 4, 1: 6, 2: 7}.get(level, 8)
        nat_up(now, (side - margin) // 8, min(-(-(side + own + margin) // 8), (height - 2 * PAD) // 8))
        coarse = functools.partial(lambda ref, o, k: ref[o, k, PAD : ref.shape[2] - PAD], now["u"])

    now = dict(s)
    now["u"] = fresh[0]
    hh = halo // 2
    lo, hi = (hh - 2) // 8, -(-(hh + half + 2) // 8)
    steps = (s["u"].shape[2] - 2 * PAD) // 8

    def add(t, carry):
        for k in range(layers):
            value = fresh[1][0, k, rows(t)]
            for pj in range(4):
                now["u"][pj, k, rows(t)] = s["u"][pj, k, rows(t)] + value
        return carry

    lax.fori_loop(lo - 1, min(hi + 1, steps), add, 0)
    for sweep in range(2):
        split_half(now, 0, lo, hi, layers)
        split_half(now, 1, lo, hi, layers)
    source, target = iota((2 * LANES, 2 * half), 0), iota((2 * LANES, 2 * half), 1)
    pick = ((source % LANES == hh + target // 2) & (source // LANES == target % 2)).astype(F32)
    for k in range(layers):
        for p in range(2):
            body_rows = slice(PAD + hh, PAD + hh + half)
            both = jnp.concatenate([now["u"][2 * p, k, body_rows], now["u"][2 * p + 1, k, body_rows]], 1)
            out[k, pl.ds(p, half, stride=2), :] = dot(both, pick)


def swap(values, axis, first):
    count = lax.axis_size(axis)
    pairs = [(i, i + 1) for i in range(first, count - 1, 2)]
    return lax.ppermute(values, axis, pairs + [(b, a) for a, b in pairs])


def shape(*dims):
    return jax.ShapeDtypeStruct(dims, F32)


def on_device(u0, sub, cat, planar, vertical, ratio, watt):
    nx, ny = lax.axis_size("gx"), lax.axis_size("gy")
    gx, gy = lax.axis_index("gx"), lax.axis_index("gy")
    layers, height, width = u0.shape
    halo = halo_cells()
    half, hh = height // 2, halo // 2
    planes = 2 * layers + 1
    assert height == width == LANES and 2 * halo <= LANES and halo + half <= LANES
    par = jnp.stack([gy % 2, gx % 2]).astype(jnp.int32)

    heat, a, b = pl.pallas_call(
        functools.partial(prep_kernel, halo=halo),
        out_shape=(shape(height, width), shape(planes, halo, height), shape(planes, halo, height)),
        in_specs=[SMEM, SMEM, VMEM, VMEM, VMEM],
        out_specs=(VMEM,) * 3,
        compiler_params=PARAMS,
        name="prep",
    )(par, watt, cat, u0, sub)
    a, b = swap(a, "gy", 0), swap(b, "gy", 1)

    lines = planes * 4 * hh
    sp, a, b = pl.pallas_call(
        functools.partial(split_kernel, halo=halo),
        out_shape=(shape(planes, 4, half, LANES), shape(lines, LANES), shape(lines, LANES)),
        in_specs=[SMEM] + [VMEM] * 5,
        out_specs=(VMEM,) * 3,
        scratch_shapes=[pltpu.VMEM((2, height, LANES), F32)],
        compiler_params=PARAMS,
        name="split",
    )(par, u0, sub, heat, a, b)
    a, b = swap(a, "gx", 0), swap(b, "gx", 1)

    tall = up8(half + 2 * hh) + 2 * PAD
    four, two = (4, layers, tall, LANES), (2, layers, tall, LANES)
    split_shapes = [four if name in ("u", "f", "invd", "fl") else two for name in SPLIT_KEPT]
    nat_shapes = [
        (1, layers, up8((height + 2 * halo) >> level) + 2 * PAD, LANES) for level in range(1, LOCAL)
    ]
    mine = height >> LOCAL
    per = LANES // (4 * mine)
    pairs = -(-layers // per)
    kept = [shape(*d) for d in split_shapes]
    for d in nat_shapes:
        kept += [shape(*d)] * len(NAT_KEPT)
    scratch = [pltpu.VMEM(four, F32)] * 3 + [pltpu.VMEM((4, tall, LANES), F32)]
    for d in nat_shapes:
        scratch += [pltpu.VMEM(d, F32)] * len(NAT_OTHER)
    scratch += [pltpu.VMEM(d, F32) for d in nat_shapes]
    tables = jnp.concatenate([planar, vertical, ratio])
    *saved, payload = pl.pallas_call(
        functools.partial(
            down_kernel, halo=halo, half=half, kinds=planar.shape[0]
        ),
        out_shape=(*kept, shape(pairs * mine, LANES)),
        in_specs=[SMEM, SMEM, VMEM, VMEM, VMEM],
        out_specs=(VMEM,) * (len(kept) + 1),
        scratch_shapes=scratch,
        compiler_params=PARAMS,
        name="down",
    )(par[1:], tables, sp, a, b)

    sent = jnp.broadcast_to(payload[None], (nx * ny,) + payload.shape)
    gathered = lax.all_to_all(sent, ("gx", "gy"), 0, 0)

    scratch = []
    for level in range(LOCAL, LEVELS + 1):
        wide = -(-(ny * width >> level) // LANES)
        d = (wide, layers, up8(nx * height >> level) + 2 * PAD, LANES)
        scratch += [pltpu.VMEM(d, F32)] * len(WHOLE)
    for level in range(LOCAL, LEVELS):
        wide = -(-(ny * width >> level) // LANES)
        scratch.append(pltpu.VMEM((wide, layers, up8(nx * height >> level) + 2 * PAD, LANES), F32))
    scratch += [pltpu.VMEM(four, F32)] + [pltpu.VMEM(d, F32) for d in nat_shapes]
    wide, count, rows_of, _ = scratch[0].shape
    scratch.append(pltpu.VMEM((wide, count, rows_of + PAD, LANES), F32))
    return pl.pallas_call(
        functools.partial(up_kernel, halo=halo, half=half, spans=(nx, ny)),
        out_shape=shape(layers, height, width),
        in_specs=[SMEM] + [VMEM] * (1 + len(kept)),
        out_specs=VMEM,
        scratch_shapes=scratch,
        compiler_params=PARAMS,
        name="up",
    )(jnp.stack([gx, gy]).astype(jnp.int32), gathered, *saved)


def solution(mesh):
    placed = (P(None, "gx", "gy"), P(None, "gx", "gy"), P("gx", "gy"), P(), P(), P(), P())
    return jax.shard_map(
        on_device, mesh=mesh, in_specs=placed, out_specs=P(None, "gx", "gy"), check_vma=False
    )
```

time: 1550 us -> 155 us (0.10); the launches traced: 1530 us -> 154 us
  starting transfers between devices: 622 us -> 28 us
  local copies, waits for them, and re-layouts: 344 us -> 4.61 us
  other arithmetic: 254 us -> 1.84 us
  waiting for transfers between devices: 183 us -> 30.8 us
  Pallas kernels: 0 us -> 89.1 us
  blocking collectives: 85.3 us -> 0 us
  between operations: 36.7 us -> 0.06 us
    ppermute x240 -> x4, starting transfers between devices: 622 us -> 4.36 us  [swap(): return lax.ppermute(values, axis, pairs + [(b, a) for a, b in pairs])]
    ppermute x240 -> x4, waiting for transfers between devices: 183 us -> 10.1 us  [swap(): return lax.ppermute(values, axis, pairs + [(b, a) for a, b in pairs])]
    slice x161 -> x0, local copies, waits for them, and re-layouts: 136 us -> none  [the longest x19 77 us: restrict(): blocks[:, :, 1, :, 0]]
    unnamed x658 -> x16, local copies, waits for them, and re-layouts: 122 us -> 2.92 us
    pallas_call x0 -> x4, Pallas kernels: none -> 89.1 us  [the longest x1 51.7 us: on_device(): pl.pallas_call(functools.partial(up_kernel, halo=halo, half=half, spans=(...]
    all_gather x8 -> x0, blocking collectives: 85.3 us -> none  [the longest x1 13.4 us: on_device(): lax.all_gather(source_vector, 'gx', axis=1, tiled=True)]
    add x27 -> x0, other arithmetic: 70.4 us -> none  [the longest x3 50.2 us: lookup(): summed = summed + jnp.where(labels == number, entries[number], 0.0)]
    select_n x49 -> x0, other arithmetic: 55.6 us -> none  [the longest x48 54.1 us: update(): return jnp.where(chosen, candidate, beside_all)]
  transfers between devices with their start and end apart: 240 -> 5, of which waited for: 66 -> 3; matrix products, arithmetic and copies ran while one was open for 31% -> 1% of each run, Pallas kernels for 0% -> 0%
where the time goes in v1:
time: 155 us; the launch traced here: 154 us
  Pallas kernels  89.1 us (57%)
  waiting for transfers between devices  30.8 us (20%)
  starting transfers between devices  28 us (18%)
  local copies, waits for them, and re-layouts  4.61 us (3%)
  other arithmetic  1.84 us (1%)
    pallas_call x1, Pallas kernels, on_device(): pl.pallas_call(functools.partial(up_kernel, halo=halo, half=half, spans=(...  51.7 us
    pallas_call x1, Pallas kernels, on_device(): pl.pallas_call(functools.partial(down_kernel, halo=halo, half=half, kinds...  29.9 us
    all_to_all x1, starting transfers between devices, on_device(): gathered = lax.all_to_all(sent, ('gx', 'gy'), 0, 0)  23.7 us
    all_to_all x1, waiting for transfers between devices, on_device(): gathered = lax.all_to_all(sent, ('gx', 'gy'), 0, 0)  20.7 us
    ppermute x4, waiting for transfers between devices, swap(): return lax.ppermute(values, axis, pairs + [(b, a) for a, b in pairs])  10.1 us
    pallas_call x1, Pallas kernels, on_device(): pl.pallas_call(functools.partial(split_kernel, halo=halo), out_shape=(sha...  4.9 us
    ppermute x4, starting transfers between devices, swap(): return lax.ppermute(values, axis, pairs + [(b, a) for a, b in pairs])  4.36 us
  transfers between devices with their start and end apart: 5, of which 3 were waited for; matrix products, arithmetic and copies ran while one was open for 1% of the time, Pallas kernels for 0%

profile of v1, /device:TPU:0, one launch (start us, length us, event | category | flops | bytes accessed | tf_op | source)
XLA Modules:
  0.0 154.4 jit_solution(15424628054161496760)
XLA Ops:
  0.0 0.0 copy-start.5
  0.0 0.0 copy-start.6
  0.0 0.0 copy-start.7
  0.0 0.6 pad_add_fusion.1.par
  0.6 2.6 %prep.1 = (f32[128,128]{1,0:T(8,128)}, f32[13,56,128]{2,1,0:T(8,128)}, f32[13,56,128]{2,1,0:T(8,128)}) custom-call(s32[2]{0:T(128)} %pad_add_fusion.1.par, f32[64]{0:T(128)} %watt.1, s32[8,8]{1,0:T(8,128)} %cat_ref.1, f32[6,128,128]{2,1,0:T(8,128)} %u_ref.3, s32[6,128,128]{2,1,0:T(8,128)} %sub_ref.3), custom_call_target="tpu_custom_call" | custom-call | tf_op jit(solution)/shard_map/prep/pallas_call | solution.py:689
  3.2 3.0 %collective-permute-start = (f32[13,56,128]{2,1,0:T(8,128)}, f32[13,56,128]{2,1,0:T(8,128)S(1)}, u32[]{:S(2)}, u32[]{:S(2)}) collective-permute-start(f32[13,56,128]{2,1,0:T(8,128)} %get-tuple-element.36), channel_id=1, source_target_pairs={{0,1},{2,3},{1,0},{3,2},{4,5},{6,7},{5,4},{7,6},{8,9},{10,11},{9,8... | collective-permute-start | bytes 1118216 | tf_op jit(solution)/shard_map/ppermute | solution.py:672
  6.2 0.7 collective-permute-start.1
  6.9 9.1 %collective-permute-done.ra = f32[13,56,128]{2,1,0:T(8,128)S(1)} collective-permute-done((f32[13,56,128]{2,1,0:T(8,128)}, f32[13,56,128]{2,1,0:T(8,128)S(1)}, u32[]{:S(2)}, u32[]{:S(2)}) %collective-permute-start) | collective-permute-done | bytes 372768 | tf_op jit(solution)/shard_map/ppermute | solution.py:672
  15.9 0.0 copy-start.3
  15.9 0.0 collective-permute-done.1.rb
  15.9 0.0 copy-start.4
  15.9 0.7 copy-done.3
  16.7 0.1 copy-done.4
  16.8 4.9 %split.1 = (f32[13,4,64,128]{3,2,1,0:T(8,128)}, f32[1456,128]{1,0:T(8,128)}, f32[1456,128]{1,0:T(8,128)}) custom-call(s32[2]{0:T(128)} %pad_add_fusion.1.par, f32[6,128,128]{2,1,0:T(8,128)} %u_ref.3, s32[6,128,128]{2,1,0:T(8,128)} %sub_ref.3, f32[128,128]{1,0:T(8,128)} %get-tuple-element.35.heat_ref, f32[13,56,128]{2,1,0:T(8,128)} %copy-done.3, ...), custom_call_target="tpu_custom_call" | custom-call | tf_op jit(solution)/shard_map/split/pallas_call | solution.py:700
  21.7 0.0 collective-permute-start.2
  21.7 0.7 collective-permute-start.3
  22.4 0.0 copy-done.5
  22.4 0.0 copy-done.6
  22.4 0.0 copy-done.7
  22.4 0.6 pad_maximum_fusion.tables
  23.1 1.1 collective-permute-done.2.refs_1_
  24.1 0.0 copy-start.1
  24.1 0.0 collective-permute-done.3.refs_2_
  24.1 0.9 copy-done.1
  25.1 0.2 copy-done.2
  25.3 29.9 %down.1 = (f32[4,6,136,128]{3,2,1,0:T(8,128)}, f32[4,6,136,128]{3,2,1,0:T(8,128)}, f32[4,6,136,128]{3,2,1,0:T(8,128)}, f32[2,6,136,128]{3,2,1,0:T(8,128)}, f32[2...) custom-call(s32[1]{0:T(128)} %bitcast.2.par, ...), custom_call_target="tpu_custom_call" | custom-call | tf_op jit(solution)/shard_map/down/pallas_call | solution.py:728
  55.2 1.7 %broadcast_in_dim.2 = f32[32,48,128]{2,1,0:T(8,128)} broadcast(f32[48,128]{1,0:T(8,128)} %get-tuple-element.41), dimensions={1,2} | broadcast | bytes 811008 | tf_op jit(solution)/shard_map/broadcast_in_dim | solution.py:740
  56.9 23.7 %all-to-all-start = ((f32[32,48,128]{2,1,0:T(8,128)}), f32[32,48,128]{2,1,0:T(8,128)S(1)}, u32[]{:S(2)}, u32[]{:S(2)}) async-start(f32[32,48,128]{2,1,0:T(8,128)} %broadcast_in_dim.2), calls=%async_computation | async-start | bytes 1572864 | tf_op jit(solution)/shard_map/all_to_all | solution.py:741
  80.6 0.6 pad_add_fusion.place
  81.2 20.7 %all-to-all-done.refs_0_ = f32[32,48,128]{2,1,0:T(8,128)S(1)} async-done(((f32[32,48,128]{2,1,0:T(8,128)}), f32[32,48,128]{2,1,0:T(8,128)S(1)}, u32[]{:S(2)}, u32[]{:S(2)}) %all-to-all-start) | async-done | bytes 786464 | tf_op jit(solution)/shard_map/all_to_all | solution.py:741
  101.8 0.9 copy-done
  102.7 51.7 %up.1 = f32[6,128,128]{2,1,0:T(8,128)} custom-call(s32[2]{0:T(128)} %pad_add_fusion.place, f32[32,48,128]{2,1,0:T(8,128)} %copy-done, f32[4,6,136,128]{3,2,1,0:T(8,128)} %get-tuple-element.42.refs_1_, f32[4,6,136,128]{3,2,1,0:T(8,128)} %get-tuple-element.43.refs_2_, f32[4,6,136,128]{3,2,1,0:T(8,128)} %get-tuple-element.44.refs_3_, ...), custom_call_target="tpu_custom_call" | custom-call | tf_op jit(solution)/shard_map/up/pallas_call | solution.py:754
  (2 shorter events, 0.0 us)
Async XLA Ops:
  0.0 22.4 %copy-start.5 = (f32[8]{0:T(128)S(1)}, f32[8]{0:T(128)}, u32[]{:S(2)}) copy-start(f32[8]{0:T(128)} %param.12) | copy-start | bytes 100
  0.0 22.4 %copy-start.6 = (f32[8]{0:T(128)S(1)}, f32[8]{0:T(128)}, u32[]{:S(2)}) copy-start(f32[8]{0:T(128)} %param.11) | copy-start | bytes 100
  0.0 22.4 %copy-start.7 = (f32[8]{0:T(128)S(1)}, f32[8]{0:T(128)}, u32[]{:S(2)}) copy-start(f32[8]{0:T(128)} %param.10) | copy-start | bytes 100
  3.2 12.7 %collective-permute-start = (f32[13,56,128]{2,1,0:T(8,128)}, f32[13,56,128]{2,1,0:T(8,128)S(1)}, u32[]{:S(2)}, u32[]{:S(2)}) collective-permute-start(f32[13,56,128]{2,1,0:T(8,128)} %get-tuple-element.36), channel_id=1, source_target_pairs={{0,1},{2,3},{1,0},{3,2},{4,5},{6,7},{5,4},{7,6},{8,9},{10,11},{9,8... | collective-permute-start | bytes 1118216 | tf_op jit(solution)/shard_map/ppermute | solution.py:672
  6.2 9.7 %collective-permute-start.1 = (f32[13,56,128]{2,1,0:T(8,128)}, f32[13,56,128]{2,1,0:T(8,128)S(1)}, u32[]{:S(2)}, u32[]{:S(2)}) collective-permute-start(f32[13,56,128]{2,1,0:T(8,128)} %get-tuple-element.37), channel_id=1, source_target_pairs={{1,2},{2,1},{5,6},{6,5},{9,10},{10,9},{13,14},{14,13},{17,18},{18,... | collective-permute-start | bytes 1118216 | tf_op jit(solution)/shard_map/ppermute | solution.py:672
  15.9 0.7 copy-start.3
  15.9 0.9 copy-start.4
  21.7 2.4 %collective-permute-start.2 = (f32[1456,128]{1,0:T(8,128)}, f32[1456,128]{1,0:T(8,128)S(1)}, u32[]{:S(2)}, u32[]{:S(2)}) collective-permute-start(f32[1456,128]{1,0:T(8,128)} %get-tuple-element.39), channel_id=1, source_target_pairs={{0,4},{8,12},{16,20},{24,28},{4,0},{12,8},{20,16},{28,24},{1,5},{9... | collective-permute-start | bytes 2236424 | tf_op jit(solution)/shard_map/ppermute | solution.py:672
  21.7 2.4 %collective-permute-start.3 = (f32[1456,128]{1,0:T(8,128)}, f32[1456,128]{1,0:T(8,128)S(1)}, u32[]{:S(2)}, u32[]{:S(2)}) collective-permute-start(f32[1456,128]{1,0:T(8,128)} %get-tuple-element.40), channel_id=1, source_target_pairs={{4,8},{12,16},{20,24},{8,4},{16,12},{24,20},{5,9},{13,17},{21,25},... | collective-permute-start | bytes 2236424 | tf_op jit(solution)/shard_map/ppermute | solution.py:672
  24.1 0.9 copy-start.1
  24.1 1.1 copy-start.2
  56.9 44.9 %all-to-all-start = ((f32[32,48,128]{2,1,0:T(8,128)}), f32[32,48,128]{2,1,0:T(8,128)S(1)}, u32[]{:S(2)}, u32[]{:S(2)}) async-start(f32[32,48,128]{2,1,0:T(8,128)} %broadcast_in_dim.2), calls=%async_computation | async-start | bytes 1572864 | tf_op jit(solution)/shard_map/all_to_all | solution.py:741
  101.8 0.9 copy-start

commit v2 on v1

--- a/solution.py
+++ b/solution.py
@@ -1,4 +1,5 @@
 import functools
+import math
 
 import jax
 import jax.numpy as jnp
@@ -13,11 +14,16 @@
 COARSE_ITERS = 12
 LANES = 128
 PAD = 8
+MOST = dict(split=3, nat=4, first=4, residual=4, setup=4, look=2, faces=2, remain=3, add=4)
 HI = lax.Precision.HIGHEST
 F32 = jnp.float32
 VMEM = pl.BlockSpec(memory_space=pltpu.VMEM)
 SMEM = pl.BlockSpec(memory_space=pltpu.SMEM)
-PARAMS = pltpu.CompilerParams(vmem_limit_bytes=60 * 1024 * 1024)
+
+
+def limit(mib, scratch=()):
+    held = sum(4 * math.prod(ref.shape) for ref in scratch)
+    return pltpu.CompilerParams(vmem_limit_bytes=mib * 1024 * 1024 + held + held // 4)
 
 
 def up8(n):
@@ -42,14 +48,42 @@
 
 
 def rows(t, off=0):
-    return pl.ds(pl.multiple_of(t * 8, 8) + (PAD + off), 8)
+    first, count = t
+    start = first * 8 if isinstance(first, int) else pl.multiple_of(first * 8, 8)
+    return pl.ds(start + (PAD + off), 8 * count)
+
+
+def over(lo, hi, most, body):
+    steps = -(-(hi - lo) // most)
+    size = -(-(hi - lo) // steps)
+    if steps == 1:
+        body((lo, size))
+        return
+
+    def step(i, carry):
+        body((jnp.minimum(lo + i * size, hi - size), size))
+        return carry
+
+    lax.fori_loop(0, steps, step, 0)
 
 
 def dot(a, b):
     return jnp.dot(a, b, precision=HI, preferred_element_type=F32)
 
 
-def prep_kernel(par, watt, cat_ref, u_ref, sub_ref, heat_ref, a_ref, b_ref, *, halo):
+def pick_dot(x, pick, pieces=3):
+    pick = pick.astype(jnp.bfloat16)
+    total = None
+    for n in range(pieces):
+        piece = x.astype(jnp.bfloat16)
+        part = jnp.dot(piece, pick, preferred_element_type=F32)
+        total = part if total is None else total + part
+        if n < pieces - 1:
+            x = x - piece.astype(F32)
+    return total
+
+
+def prep_kernel(watt, cat_ref, u_ref, sub_ref, heat_ref, a_ref, b_ref, *, halo):
     layers, height, width = u_ref.shape
     cat = cat_ref[...]
     power = jnp.zeros(cat.shape, F32)
@@ -58,7 +92,7 @@
     spread_r = (iota((height, cat.shape[0]), 0) // TILE == iota((height, cat.shape[0]), 1)).astype(F32)
     spread_c = (iota((cat.shape[1], width), 1) // TILE == iota((cat.shape[1], width), 0)).astype(F32)
     heat_ref[...] = dot(dot(spread_r, power), spread_c)
-    even = par[0] == 0
+    even = lax.axis_index("gy") % 2 == 0
     for q in range(2 * layers + 1):
         if q < layers:
             plane = u_ref[q]
@@ -72,9 +106,9 @@
         b_ref[q] = jnp.where(even, low, high)
 
 
-def split_kernel(par, u_ref, sub_ref, heat_ref, ra, rb, out, a_ref, b_ref, scr, *, halo):
+def split_kernel(u_ref, sub_ref, heat_ref, ra, rb, out, a_ref, b_ref, scr, *, halo):
     layers, height, width = u_ref.shape
-    even_y, even_x = par[0] == 0, par[1] == 0
+    even_y, even_x = lax.axis_index("gy") % 2 == 0, lax.axis_index("gx") % 2 == 0
     half, hh = height // 2, halo // 2
     source, target = iota((width + LANES, 2 * LANES), 0), iota((width + LANES, 2 * LANES), 1)
     cell = 2 * (target % LANES) + target // LANES
@@ -82,6 +116,7 @@
         cell < halo, width + cell, jnp.where(cell < halo + width, cell - halo, cell)
     )
     pick = ((source == want) & (cell < 2 * halo + width)).astype(F32)
+    planes = []
     for q in range(2 * layers + 1):
         if q < layers:
             plane = u_ref[q]
@@ -92,17 +127,25 @@
         left = jnp.where(even_y, rb[q], ra[q])
         right = jnp.where(even_y, ra[q], rb[q])
         sides = jnp.concatenate([left, right, jnp.zeros((LANES - 2 * halo, height), F32)], 0).T
-        both = dot(jnp.concatenate([plane, sides], 1), pick)
-        scr[0] = both[:, :LANES]
-        scr[1] = both[:, LANES:]
+        planes.append(jnp.concatenate([plane, sides], 1))
+    first = pick_dot(jnp.concatenate(planes[:layers] + planes[2 * layers :], 0), pick)
+    second = pick_dot(jnp.concatenate(planes[layers : 2 * layers], 0), pick, 1)
+    for q in range(2 * layers + 1):
+        if layers <= q < 2 * layers:
+            both = second[(q - layers) * height : (q - layers + 1) * height]
+        else:
+            at = q if q < layers else layers
+            both = first[at * height : (at + 1) * height]
+        scr[q % 2, 0] = both[:, :LANES]
+        scr[q % 2, 1] = both[:, LANES:]
         for p in range(2):
             for j in range(2):
-                z = scr[j, pl.ds(p, half, stride=2), :]
+                z = scr[q % 2, j, pl.ds(p, half, stride=2), :]
                 out[q, 2 * p + j] = z
                 at = (4 * q + 2 * p + j) * hh
-                first, last = z[:hh], z[half - hh :]
-                a_ref[at : at + hh] = jnp.where(even_x, last, first)
-                b_ref[at : at + hh] = jnp.where(even_x, first, last)
+                first_rows, last_rows = z[:hh], z[half - hh :]
+                a_ref[at : at + hh] = jnp.where(even_x, last_rows, first_rows)
+                b_ref[at : at + hh] = jnp.where(even_x, first_rows, last_rows)
 
 
 def split_sum(s, p, j, k, t, layers):
@@ -127,7 +170,7 @@
 
 
 def split_half(s, colour, lo, hi, layers):
-    def body(t, carry):
+    def body(t):
         for k in range(layers):
             for p in range(2):
                 for j in range(2):
@@ -135,9 +178,8 @@
                         pj = 2 * p + j
                         total = s["f"][pj, k, rows(t)] + split_sum(s, p, j, k, t, layers)
                         s["u"][pj, k, rows(t)] = total * s["invd"][pj, k, rows(t)]
-        return carry
-
-    lax.fori_loop(lo, hi, body, 0)
+
+    over(lo, hi, MOST["split"], body)
 
 
 def sides_of(tiles, lane):
@@ -156,10 +198,10 @@
 
 def nat_setup(s, factor):
     tiles, layers, height, _ = s["lat"].shape
-    lane = iota((8, LANES), 1)
     c = 0.5 * factor
 
-    def body(t, carry):
+    def body(t):
+        lane = iota((8 * t[1], LANES), 1)
         for k in range(layers):
             lat = [s["lat"][i, k, rows(t)] for i in range(tiles)]
             left, right = sides_of(lat, lane)
@@ -182,10 +224,9 @@
                 s["wcr"][i, k, rows(t)] = after
                 s["diag"][i, k, rows(t)] = diag
                 s["invd"][i, k, rows(t)] = jnp.where(inside, 1.0 / jnp.where(inside, diag, 1.0), 0.0)
-        return carry
 
     s["wr"][:, :, height - PAD :] = jnp.zeros((tiles, layers, PAD, LANES), F32)
-    lax.fori_loop(0, (height - 2 * PAD) // 8, body, 0)
+    over(0, (height - 2 * PAD) // 8, MOST["setup"], body)
 
 
 def nat_sum(s, mid, sides, i, k, t, layers):
@@ -202,10 +243,10 @@
 
 def nat_half(s, colour, lo, hi):
     tiles, layers = s["u"].shape[:2]
-    lane = iota((8, LANES), 1)
-    odd = (iota((8, LANES), 0) + lane) % 2
-
-    def body(t, carry):
+
+    def body(t):
+        lane = iota((8 * t[1], LANES), 1)
+        odd = (iota((8 * t[1], LANES), 0) + lane) % 2
         mid = [[s["u"][i, k, rows(t)] for i in range(tiles)] for k in range(layers)]
         sides = [sides_of(m, lane) for m in mid]
         for k in range(layers):
@@ -213,42 +254,39 @@
             for i in range(tiles):
                 total = s["f"][i, k, rows(t)] + nat_sum(s, mid, sides, i, k, t, layers)
                 s["u"][i, k, rows(t)] = jnp.where(chosen, total * s["invd"][i, k, rows(t)], mid[k][i])
-        return carry
-
-    lax.fori_loop(lo, hi, body, 0)
+
+    over(lo, hi, MOST["nat"], body)
 
 
 def nat_first(s, lo, hi):
     tiles, layers, height, _ = s["u"].shape
-    odd = (iota((8, LANES), 0) + iota((8, LANES), 1)) % 2
     zeros = jnp.zeros((tiles, layers, PAD, LANES), F32)
     s["u"][:, :, :PAD] = zeros
     s["u"][:, :, height - PAD :] = zeros
 
-    def body(t, carry):
+    def body(t):
+        odd = (iota((8 * t[1], LANES), 0) + iota((8 * t[1], LANES), 1)) % 2
         for k in range(layers):
             for i in range(tiles):
                 value = s["f"][i, k, rows(t)] * s["invd"][i, k, rows(t)]
                 s["u"][i, k, rows(t)] = jnp.where(odd == k % 2, value, 0.0)
-        return carry
-
-    lax.fori_loop(lo, hi, body, 0)
+
+    over(lo, hi, MOST["first"], body)
 
 
 def nat_residual(s, res, lo, hi):
     tiles, layers = s["u"].shape[:2]
-    lane = iota((8, LANES), 1)
-
-    def body(t, carry):
+
+    def body(t):
+        lane = iota((8 * t[1], LANES), 1)
         mid = [[s["u"][i, k, rows(t)] for i in range(tiles)] for k in range(layers)]
         sides = [sides_of(m, lane) for m in mid]
         for k in range(layers):
             for i in range(tiles):
                 total = s["f"][i, k, rows(t)] + nat_sum(s, mid, sides, i, k, t, layers)
                 res[i, k, rows(t)] = total - s["diag"][i, k, rows(t)] * mid[k][i]
-        return carry
-
-    lax.fori_loop(lo, hi, body, 0)
+
+    over(lo, hi, MOST["residual"], body)
 
 
 def nat_down(s, res, steps):
@@ -258,40 +296,46 @@
     nat_residual(s, res, 0, steps)
 
 
-def restrict_to(source, target):
-    tiles, layers = source.shape[:2]
-    count, height = target.shape[0], target.shape[2] - 2 * PAD
+def restrict_all(pairs):
+    tiles, layers = pairs[0][0].shape[:2]
+    count, height = pairs[0][1].shape[0], pairs[0][1].shape[2] - 2 * PAD
     zeros = jnp.zeros((count, layers, PAD, LANES), F32)
-    target[:, :, :PAD] = zeros
-    target[:, :, PAD + height :] = zeros
+    parts = [[] for i in range(tiles)]
+    for source, target in pairs:
+        target[:, :, :PAD] = zeros
+        target[:, :, PAD + height :] = zeros
+        for k in range(layers):
+            for i in range(tiles):
+                part = source[i, k, pl.ds(PAD, height, stride=2), :]
+                parts[i].append(part + source[i, k, pl.ds(PAD + 1, height, stride=2), :])
+    parts = [jnp.concatenate(p, 0) for p in parts]
     cell = iota((LANES, LANES), 0) // 2
-    for k in range(layers):
-        parts = [
-            source[i, k, pl.ds(PAD, height, stride=2), :]
-            + source[i, k, pl.ds(PAD + 1, height, stride=2), :]
-            for i in range(tiles)
-        ]
-        for o in range(count):
-            total = None
-            for i in range(tiles):
-                shift = LANES // 2 * i - LANES * o
-                if -LANES < shift < LANES:
-                    pick = jnp.where(cell + shift == iota((LANES, LANES), 1), 0.25, 0.0)
-                    part = dot(parts[i], pick)
-                    total = part if total is None else total + part
-            target[o, k, PAD : PAD + height] = total
+    for o in range(count):
+        total = None
+        for i in range(tiles):
+            shift = LANES // 2 * i - LANES * o
+            if -LANES < shift < LANES:
+                pick = jnp.where(cell + shift == iota((LANES, LANES), 1), 0.25, 0.0)
+                part = pick_dot(parts[i], pick)
+                total = part if total is None else total + part
+        for n, (_, target) in enumerate(pairs):
+            for k in range(layers):
+                at = (n * layers + k) * height
+                target[o, k, PAD : PAD + height] = total[at : at + height]
 
 
 def prolong_into(s, u_in, coarse, mask):
     tiles, layers, height, _ = s["u"].shape
     n = (height - 2 * PAD) // 2
+    tall = up8(n)
     cell = iota((LANES, LANES), 1) // 2
     for i in range(tiles):
         o = i // 2
         shift = LANES // 2 * (i % 2)
         pick = (cell + shift == iota((LANES, LANES), 0)).astype(F32)
-        for k in range(layers):
-            wide = dot(coarse(o, k)[:n], pick)
+        every = pick_dot(jnp.concatenate([coarse(o, k)[:tall] for k in range(layers)], 0), pick)
+        for k in range(layers):
+            wide = every[k * tall : k * tall + n]
             for p in range(2):
                 at = pl.ds(PAD + p, n, stride=2)
                 add = wide
@@ -311,10 +355,9 @@
 NAT_OTHER = ("lat", "vert", "stor", "diag")
 
 
-def down_kernel(par, tables, *refs, halo, half, kinds):
-    refs = list(refs)
-    sp, ra, rb = refs[:3]
-    refs = refs[3:]
+def down_kernel(*refs, halo, half, kinds):
+    tables, (sp, ra, rb) = refs[:3], refs[3:6]
+    refs = list(refs[6:])
     s = dict(zip(SPLIT_KEPT, refs[: len(SPLIT_KEPT)]))
     refs = refs[len(SPLIT_KEPT) :]
     nats = []
@@ -333,7 +376,7 @@
     height = s["u"].shape[2]
     hh = halo // 2
     steps = (height - 2 * PAD) // 8
-    even = par[0] == 0
+    even = lax.axis_index("gx") % 2 == 0
     zeros = jnp.zeros((PAD, LANES), F32)
 
     def place(ref, index, q, pj):
@@ -362,7 +405,7 @@
             ref[0, k, :PAD] = zeros
             ref[0, k, ref.shape[2] - PAD :] = zeros
 
-    def look(t, carry):
+    def look(t):
         for k in range(layers):
             sums = [None, None, None]
             for pj in range(4):
@@ -371,7 +414,7 @@
                 value = [jnp.zeros_like(label)] * 3
                 for n in range(kinds):
                     hit = label == float(n + 1)
-                    value = [jnp.where(hit, tables[i * kinds + n], value[i]) for i in range(3)]
+                    value = [jnp.where(hit, tables[i][n], value[i]) for i in range(3)]
                 for i, name in enumerate(("lat", "vert", "stor")):
                     s[name][at] = value[i]
                     sums[i] = value[i] if sums[i] is None else sums[i] + value[i]
@@ -381,11 +424,10 @@
                 s["f"][at] = f
             for i, name in enumerate(("lat", "vert", "stor")):
                 first[name][0, k, rows(t)] = sums[i] * 0.25
-        return carry
-
-    lax.fori_loop(0, steps, look, 0)
-
-    def faces(t, carry):
+
+    over(0, steps, MOST["look"], look)
+
+    def faces(t):
         at = rows(t)
         for k in range(layers):
             lat = [s["lat"][pj, k, at] for pj in range(4)]
@@ -417,14 +459,13 @@
                     inside = stor > 0.0
                     s["invd"][pj, k, at] = jnp.where(inside, 1.0 / jnp.where(inside, diag, 1.0), 0.0)
                     s["stor"][pj, k, at] = diag
-        return carry
-
-    lax.fori_loop(0, steps, faces, 0)
+
+    over(0, steps, MOST["faces"], faces)
     for sweep in range(2):
         split_half(s, 0, 0, steps, layers)
         split_half(s, 1, 0, steps, layers)
 
-    def remain(t, carry):
+    def remain(t):
         for k in range(layers):
             total = None
             for p in range(2):
@@ -435,9 +476,8 @@
                         r -= s["stor"][pj, k, rows(t)] * s["u"][pj, k, rows(t)]
                         total = r if total is None else total + r
             first["f"][0, k, rows(t)] = total * 0.25
-        return carry
-
-    lax.fori_loop(0, steps, remain, 0)
+
+    over(0, steps, MOST["remain"], remain)
 
     for level in range(1, LOCAL):
         now = nats[level - 1]
@@ -446,9 +486,8 @@
         nat_down(now, ress[level - 1], count)
         if level < LOCAL - 1:
             below = nats[level]
-            for name in ("lat", "vert", "stor"):
-                restrict_to(now[name], below[name])
-            restrict_to(ress[level - 1], below["f"])
+            pairs = [(now[name], below[name]) for name in ("lat", "vert", "stor")]
+            restrict_all(pairs + [(ress[level - 1], below["f"])])
 
     last, res = nats[-1], ress[-1]
     mine = 2 * half >> LOCAL
@@ -456,20 +495,19 @@
     group = 4 * mine
     per = LANES // group
     quantities = (res, last["lat"], last["vert"], last["stor"])
+    parts = []
+    for k in range(layers):
+        for ref in quantities:
+            part = ref[0, k, pl.ds(PAD + off, mine, stride=2), :]
+            parts.append(part + ref[0, k, pl.ds(PAD + off + 1, mine, stride=2), :])
     source, target = iota((LANES, LANES), 0), iota((LANES, LANES), 1)
+    hit = (source >= off) & ((source - off) // 2 == target) & (target < mine)
+    packed = pick_dot(jnp.concatenate(parts, 0), jnp.where(hit, 0.25, 0.0))
     for pair in range(-(-layers // per)):
         total = jnp.zeros((mine, LANES), F32)
-        for inner in range(per):
-            k = pair * per + inner
-            if k < layers:
-                for n, ref in enumerate(quantities):
-                    base = inner * group + n * mine
-                    hit = (target >= base) & (target < base + mine)
-                    hit &= (source - off >= 0) & ((source - off) // 2 == target - base)
-                    pick = jnp.where(hit, 0.25, 0.0)
-                    part = ref[0, k, pl.ds(PAD + off, mine, stride=2), :]
-                    part += ref[0, k, pl.ds(PAD + off + 1, mine, stride=2), :]
-                    total += dot(part, pick)
+        for n in range(pair * per * 4, min(layers, (pair + 1) * per) * 4):
+            part, base = packed[n * mine : (n + 1) * mine], (n - pair * per * 4) * mine
+            total += pltpu.roll(part, base, 1) if base else part
         payload[pair * mine : (pair + 1) * mine] = total
 
 
@@ -533,7 +571,7 @@
 WHOLE = ("u", "f", "invd", "wr", "wc", "wcr", "wl", "lat", "vert", "stor", "diag")
 
 
-def up_kernel(place, *refs, halo, half, spans):
+def up_kernel(*refs, halo, half, spans):
     refs = list(refs)
     gathered = refs.pop(0)
     s = dict(zip(SPLIT_KEPT, refs[: len(SPLIT_KEPT)]))
@@ -590,9 +628,8 @@
         now, below = wholes[n], wholes[n + 1]
         nat_setup(now, 0.25**level)
         nat_down(now, ress[n], (now["u"].shape[2] - 2 * PAD) // 8)
-        for name in ("lat", "vert", "stor"):
-            restrict_to(now[name], below[name])
-        restrict_to(ress[n], below["f"])
+        pairs = [(now[name], below[name]) for name in ("lat", "vert", "stor")]
+        restrict_all(pairs + [(ress[n], below["f"])])
     nat_setup(wholes[-1], 0.25**LEVELS)
     conjugate(wholes[-1])
     for n in reversed(range(len(wholes) - 1)):
@@ -600,7 +637,7 @@
         prolong_into(now, now["u"], lambda o, k: below["u"][o, k, PAD : below["u"].shape[2] - PAD], False)
         nat_up(now, 0, (now["u"].shape[2] - 2 * PAD) // 8)
 
-    x, y = place[0], place[1]
+    x, y = lax.axis_index("gx"), lax.axis_index("gy")
     reach = halo >> LOCAL
     need = (nats[-1]["u"].shape[2] - 2 * PAD) // 2
     height = top["u"].shape[2]
@@ -646,24 +683,26 @@
     lo, hi = (hh - 2) // 8, -(-(hh + half + 2) // 8)
     steps = (s["u"].shape[2] - 2 * PAD) // 8
 
-    def add(t, carry):
+    def add(t):
         for k in range(layers):
             value = fresh[1][0, k, rows(t)]
             for pj in range(4):
                 now["u"][pj, k, rows(t)] = s["u"][pj, k, rows(t)] + value
-        return carry
-
-    lax.fori_loop(lo - 1, min(hi + 1, steps), add, 0)
+
+    over(lo - 1, min(hi + 1, steps), MOST["add"], add)
     for sweep in range(2):
         split_half(now, 0, lo, hi, layers)
         split_half(now, 1, lo, hi, layers)
     source, target = iota((2 * LANES, 2 * half), 0), iota((2 * LANES, 2 * half), 1)
     pick = ((source % LANES == hh + target // 2) & (source // LANES == target % 2)).astype(F32)
-    for k in range(layers):
-        for p in range(2):
-            body_rows = slice(PAD + hh, PAD + hh + half)
-            both = jnp.concatenate([now["u"][2 * p, k, body_rows], now["u"][2 * p + 1, k, body_rows]], 1)
-            out[k, pl.ds(p, half, stride=2), :] = dot(both, pick)
+    body_rows = slice(PAD + hh, PAD + hh + half)
+    spots = [(k, p) for k in range(layers) for p in range(2)]
+    both = [
+        jnp.concatenate([now["u"][2 * p + j, k, body_rows] for k, p in spots], 0) for j in range(2)
+    ]
+    every = pick_dot(jnp.concatenate(both, 1), pick)
+    for n, (k, p) in enumerate(spots):
+        out[k, pl.ds(p, half, stride=2), :] = every[n * half : (n + 1) * half]
 
 
 def swap(values, axis, first):
@@ -678,34 +717,32 @@
 
 def on_device(u0, sub, cat, planar, vertical, ratio, watt):
     nx, ny = lax.axis_size("gx"), lax.axis_size("gy")
-    gx, gy = lax.axis_index("gx"), lax.axis_index("gy")
     layers, height, width = u0.shape
     halo = halo_cells()
     half, hh = height // 2, halo // 2
     planes = 2 * layers + 1
     assert height == width == LANES and 2 * halo <= LANES and halo + half <= LANES
-    par = jnp.stack([gy % 2, gx % 2]).astype(jnp.int32)
 
     heat, a, b = pl.pallas_call(
         functools.partial(prep_kernel, halo=halo),
         out_shape=(shape(height, width), shape(planes, halo, height), shape(planes, halo, height)),
-        in_specs=[SMEM, SMEM, VMEM, VMEM, VMEM],
+        in_specs=[SMEM, VMEM, VMEM, VMEM],
         out_specs=(VMEM,) * 3,
-        compiler_params=PARAMS,
+        compiler_params=limit(8),
         name="prep",
-    )(par, watt, cat, u0, sub)
+    )(watt, cat, u0, sub)
     a, b = swap(a, "gy", 0), swap(b, "gy", 1)
 
     lines = planes * 4 * hh
     sp, a, b = pl.pallas_call(
         functools.partial(split_kernel, halo=halo),
         out_shape=(shape(planes, 4, half, LANES), shape(lines, LANES), shape(lines, LANES)),
-        in_specs=[SMEM] + [VMEM] * 5,
+        in_specs=[VMEM] * 5,
         out_specs=(VMEM,) * 3,
-        scratch_shapes=[pltpu.VMEM((2, height, LANES), F32)],
-        compiler_params=PARAMS,
+        scratch_shapes=[pltpu.VMEM((2, 2, height, LANES), F32)],
+        compiler_params=limit(20),
         name="split",
-    )(par, u0, sub, heat, a, b)
+    )(u0, sub, heat, a, b)
     a, b = swap(a, "gx", 0), swap(b, "gx", 1)
 
     tall = up8(half + 2 * hh) + 2 * PAD
@@ -724,18 +761,17 @@
     for d in nat_shapes:
         scratch += [pltpu.VMEM(d, F32)] * len(NAT_OTHER)
     scratch += [pltpu.VMEM(d, F32) for d in nat_shapes]
-    tables = jnp.concatenate([planar, vertical, ratio])
     *saved, payload = pl.pallas_call(
         functools.partial(
             down_kernel, halo=halo, half=half, kinds=planar.shape[0]
         ),
         out_shape=(*kept, shape(pairs * mine, LANES)),
-        in_specs=[SMEM, SMEM, VMEM, VMEM, VMEM],
+        in_specs=[SMEM] * 3 + [VMEM] * 3,
         out_specs=(VMEM,) * (len(kept) + 1),
         scratch_shapes=scratch,
-        compiler_params=PARAMS,
+        compiler_params=limit(36),
         name="down",
-    )(par[1:], tables, sp, a, b)
+    )(planar, vertical, ratio, sp, a, b)
 
     sent = jnp.broadcast_to(payload[None], (nx * ny,) + payload.shape)
     gathered = lax.all_to_all(sent, ("gx", "gy"), 0, 0)
@@ -754,12 +790,12 @@
     return pl.pallas_call(
         functools.partial(up_kernel, halo=halo, half=half, spans=(nx, ny)),
         out_shape=shape(layers, height, width),
-        in_specs=[SMEM] + [VMEM] * (1 + len(kept)),
+        in_specs=[VMEM] * (1 + len(kept)),
         out_specs=VMEM,
         scratch_shapes=scratch,
-        compiler_params=PARAMS,
+        compiler_params=limit(20, scratch),
         name="up",
-    )(jnp.stack([gx, gy]).astype(jnp.int32), gathered, *saved)
+    )(gathered, *saved)
 
 
 def solution(mesh):

time: 155 us -> 103 us (0.66)
  Pallas kernels: 89.1 us -> 37 us
  blocking collectives: 0 us -> 45.1 us
  starting transfers between devices: 28 us -> 4.48 us
  waiting for transfers between devices: 30.8 us -> 10.3 us
  other arithmetic: 1.84 us -> 0 us
    all_to_all x0 -> x1, blocking collectives: none -> 45.1 us  [on_device(): gathered = lax.all_to_all(sent, ('gx', 'gy'), 0, 0)]
    pallas_call x1, Pallas kernels: 51.7 us -> 22.1 us  [on_device(): pl.pallas_call(functools.partial(up_kernel, halo=halo, half=half, spans=(...]
    all_to_all x1 -> x0, starting transfers between devices: 23.7 us -> none  [on_device(): gathered = lax.all_to_all(sent, ('gx', 'gy'), 0, 0)]
    all_to_all x1 -> x0, waiting for transfers between devices: 20.7 us -> none  [on_device(): gathered = lax.all_to_all(sent, ('gx', 'gy'), 0, 0)]
    pallas_call x1, Pallas kernels: 29.9 us -> 12.8 us  [on_device(): pl.pallas_call(functools.partial(down_kernel, halo=halo, half=half, kinds...]
    pallas_call x1, Pallas kernels: 4.9 us -> 1 us  [on_device(): pl.pallas_call(functools.partial(split_kernel, halo=halo), out_shape=(sha...]
    unnamed x16 -> x18, local copies, waits for them, and re-layouts: 2.92 us -> 5.33 us
    broadcast_in_dim x1, local copies, waits for them, and re-layouts: 1.69 us -> 0.05 us  [on_device(): sent = jnp.broadcast_to(payload[None], (nx * ny,) + payload.shape)]
  transfers between devices with their start and end apart: 5 -> 4, of which waited for: 3 -> 2; matrix products, arithmetic and copies ran while one was open for 1% -> 0% of each run, Pallas kernels for 0% -> 0%
where the time goes in v2:
time: 103 us; the launch traced here: 102 us
  blocking collectives  45.1 us (44%)
  Pallas kernels  37 us (36%)
  waiting for transfers between devices  10.3 us (10%)
  local copies, waits for them, and re-layouts  5.39 us (5%)
  starting transfers between devices  4.48 us (4%)
    all_to_all x1, blocking collectives, on_device(): gathered = lax.all_to_all(sent, ('gx', 'gy'), 0, 0)  45.1 us
    pallas_call x1, Pallas kernels, on_device(): pl.pallas_call(functools.partial(up_kernel, halo=halo, half=half, spans=(...  22.1 us
    pallas_call x1, Pallas kernels, on_device(): pl.pallas_call(functools.partial(down_kernel, halo=halo, half=half, kinds...  12.8 us
    ppermute x4, waiting for transfers between devices, swap(): return lax.ppermute(values, axis, pairs + [(b, a) for a, b in pairs])  10.3 us
    unnamed x18, local copies, waits for them, and re-layouts  5.33 us
    ppermute x4, starting transfers between devices, swap(): return lax.ppermute(values, axis, pairs + [(b, a) for a, b in pairs])  4.48 us
  transfers between devices with their start and end apart: 4, of which 2 were waited for; matrix products, arithmetic and copies ran while one was open for 0% of the time, Pallas kernels for 0%

profile of v2, /device:TPU:0, one launch (start us, length us, event | category | flops | bytes accessed | tf_op | source)
XLA Modules:
  0.0 102.4 jit_solution(1930170959399448797)
XLA Ops:
  0.0 0.0 copy-start
  0.0 1.0 copy-done
  1.0 0.0 copy-start.2
  1.0 1.0 copy-done.2
  2.0 0.0 copy-start.4
  2.0 0.7 copy-done.4
  2.7 0.0 copy-start.8
  2.7 0.7 copy-done.8
  3.3 0.0 copy-start.5
  3.3 0.0 copy-start.6
  3.3 0.0 copy-start.7
  3.3 1.1 %prep.1 = (f32[128,128]{1,0:T(8,128)S(1)}, f32[13,56,128]{2,1,0:T(8,128)S(1)}, f32[13,56,128]{2,1,0:T(8,128)S(1)}) custom-call(f32[64]{0:T(128)S(1)} %copy-done.8, s32[8,8]{1,0:T(8,128)S(1)} %copy-done.4, f32[6,128,128]{2,1,0:T(8,128)S(1)} %copy-done, s32[6,128,128]{2,1,0:T(8,128)S(1)} %copy-done.2), custom_call_target="tpu_custom_call" | custom-call | tf_op jit(solution)/shard_map/prep/pallas_call | solution.py:726
  4.5 3.0 %collective-permute-start = (f32[13,56,128]{2,1,0:T(8,128)S(1)}, f32[13,56,128]{2,1,0:T(8,128)S(1)}, u32[]{:S(2)}, u32[]{:S(2)}) collective-permute-start(f32[13,56,128]{2,1,0:T(8,128)S(1)} %get-tuple-element.36), channel_id=1, source_target_pairs={{0,1},{2,3},{1,0},{3,2},{4,5},{6,7},{5,4},{7,6},{8,9},{10,11},{9,8... | collective-permute-start | bytes 1118216 | tf_op jit(solution)/shard_map/ppermute | solution.py:711
  7.5 0.7 collective-permute-start.1
  8.2 8.8 %collective-permute-done.ra = f32[13,56,128]{2,1,0:T(8,128)S(1)} collective-permute-done((f32[13,56,128]{2,1,0:T(8,128)S(1)}, f32[13,56,128]{2,1,0:T(8,128)S(1)}, u32[]{:S(2)}, u32[]{:S(2)}) %collective-permute-start) | collective-permute-done | bytes 372768 | tf_op jit(solution)/shard_map/ppermute | solution.py:711
  17.0 0.0 collective-permute-done.1.rb
  17.0 0.0 copy-start.1
  17.0 1.0 copy-done.1
  18.0 0.0 copy-start.3
  18.0 1.0 copy-done.3
  19.0 1.0 split.1
  20.0 0.1 collective-permute-start.2
  20.1 0.7 collective-permute-start.3
  20.8 1.5 %collective-permute-done.2.refs_4_ = f32[1456,128]{1,0:T(8,128)S(1)} collective-permute-done((f32[1456,128]{1,0:T(8,128)S(1)}, f32[1456,128]{1,0:T(8,128)S(1)}, u32[]{:S(2)}, u32[]{:S(2)}) %collective-permute-start.2) | collective-permute-done | bytes 745504 | tf_op jit(solution)/shard_map/ppermute | solution.py:711
  22.3 0.0 collective-permute-done.3.refs_5_
  22.3 0.0 copy-done.5
  22.3 0.0 copy-done.6
  22.3 0.0 copy-done.7
  22.3 12.8 %down.1 = (f32[4,6,136,128]{3,2,1,0:T(8,128)S(1)}, f32[4,6,136,128]{3,2,1,0:T(8,128)S(1)}, f32[4,6,136,128]{3,2,1,0:T(8,128)S(1)}, f32[2,6,136,128]{3,2,1,0:T(8,...) custom-call(f32[8]{0:T(128)S(1)} %copy-done.5, ...), custom_call_target="tpu_custom_call" | custom-call | tf_op jit(solution)/shard_map/down/pallas_call | solution.py:764
  35.1 0.1 broadcast_in_dim.2
  35.2 45.1 %all_to_all.5.refs_0_ = f32[32,48,128]{2,1,0:T(8,128)S(1)} all-to-all(f32[32,48,128]{2,1,0:T(8,128)S(1)} %broadcast_in_dim.2), channel_id=1, replica_groups=mesh['gx'=8,'gy'=4] {'gx','gy'}, dimensions={0} | all-to-all | bytes 1572864 | tf_op jit(solution)/shard_map/all_to_all | solution.py:777
  80.3 22.1 %up.1 = f32[6,128,128]{2,1,0:T(8,128)} custom-call(f32[32,48,128]{2,1,0:T(8,128)S(1)} %all_to_all.5.refs_0_, f32[4,6,136,128]{3,2,1,0:T(8,128)S(1)} %get-tuple-element.42.refs_1_, f32[4,6,136,128]{3,2,1,0:T(8,128)S(1)} %get-tuple-element.43.refs_2_, f32[4,6,136,128]{3,2,1,0:T(8,128)S(1)} %get-tuple-element.44.refs_3_, ...), custom_call_target="tpu_custom_call" | custom-call | tf_op jit(solution)/shard_map/up/pallas_call | solution.py:790
Async XLA Ops:
  0.0 1.0 copy-start
  1.0 1.0 copy-start.2
  2.0 0.7 copy-start.4
  2.7 0.7 copy-start.8
  3.3 19.0 %copy-start.5 = (f32[8]{0:T(128)S(1)}, f32[8]{0:T(128)}, u32[]{:S(2)}) copy-start(f32[8]{0:T(128)} %refs_0_.1) | copy-start | bytes 100
  3.3 19.0 %copy-start.6 = (f32[8]{0:T(128)S(1)}, f32[8]{0:T(128)}, u32[]{:S(2)}) copy-start(f32[8]{0:T(128)} %refs_1_.1) | copy-start | bytes 100
  3.3 19.0 %copy-start.7 = (f32[8]{0:T(128)S(1)}, f32[8]{0:T(128)}, u32[]{:S(2)}) copy-start(f32[8]{0:T(128)} %refs_2_.1) | copy-start | bytes 100
  4.5 12.6 %collective-permute-start = (f32[13,56,128]{2,1,0:T(8,128)S(1)}, f32[13,56,128]{2,1,0:T(8,128)S(1)}, u32[]{:S(2)}, u32[]{:S(2)}) collective-permute-start(f32[13,56,128]{2,1,0:T(8,128)S(1)} %get-tuple-element.36), channel_id=1, source_target_pairs={{0,1},{2,3},{1,0},{3,2},{4,5},{6,7},{5,4},{7,6},{8,9},{10,11},{9,8... | collective-permute-start | bytes 1118216 | tf_op jit(solution)/shard_map/ppermute | solution.py:711
  7.5 9.5 %collective-permute-start.1 = (f32[13,56,128]{2,1,0:T(8,128)S(1)}, f32[13,56,128]{2,1,0:T(8,128)S(1)}, u32[]{:S(2)}, u32[]{:S(2)}) collective-permute-start(f32[13,56,128]{2,1,0:T(8,128)S(1)} %get-tuple-element.37), channel_id=1, source_target_pairs={{1,2},{2,1},{5,6},{6,5},{9,10},{10,9},{13,14},{14,13},{17,18},{18,... | collective-permute-start | bytes 1118216 | tf_op jit(solution)/shard_map/ppermute | solution.py:711
  17.0 1.0 copy-start.1
  18.0 1.0 copy-start.3
  20.0 2.3 %collective-permute-start.2 = (f32[1456,128]{1,0:T(8,128)S(1)}, f32[1456,128]{1,0:T(8,128)S(1)}, u32[]{:S(2)}, u32[]{:S(2)}) collective-permute-start(f32[1456,128]{1,0:T(8,128)S(1)} %get-tuple-element.39), channel_id=1, source_target_pairs={{0,4},{8,12},{16,20},{24,28},{4,0},{12,8},{20,16},{28,24},{1,5},{9... | collective-permute-start | bytes 2236424 | tf_op jit(solution)/shard_map/ppermute | solution.py:711
  20.1 2.2 %collective-permute-start.3 = (f32[1456,128]{1,0:T(8,128)S(1)}, f32[1456,128]{1,0:T(8,128)S(1)}, u32[]{:S(2)}, u32[]{:S(2)}) collective-permute-start(f32[1456,128]{1,0:T(8,128)S(1)} %get-tuple-element.40), channel_id=1, source_target_pairs={{4,8},{12,16},{20,24},{8,4},{16,12},{24,20},{5,9},{13,17},{21,25},... | collective-permute-start | bytes 2236424 | tf_op jit(solution)/shard_map/ppermute | solution.py:711

commit v3 on v2

--- a/solution.py
+++ b/solution.py
@@ -10,7 +10,8 @@
 
 TILE = 16
 LEVELS = 6
-LOCAL = 3
+FIRST = 2
+LOCAL = 4
 COARSE_ITERS = 12
 LANES = 128
 PAD = 8
@@ -19,6 +20,7 @@
 F32 = jnp.float32
 VMEM = pl.BlockSpec(memory_space=pltpu.VMEM)
 SMEM = pl.BlockSpec(memory_space=pltpu.SMEM)
+HBM = pl.BlockSpec(memory_space=pltpu.HBM)
 
 
 def limit(mib, scratch=()):
@@ -32,14 +34,14 @@
 
 def halo_cells():
     need, above = [], 0
-    for level in range(LOCAL):
+    for level in range(FIRST):
         need.append(above + 4)
         above = -(-need[-1] // 2)
     f = 0
-    for level in reversed(range(LOCAL)):
+    for level in reversed(range(FIRST)):
         inner = max(need[level], 2 * f + 1)
         f = inner + (4 if level == 0 else 3)
-    unit = 2**LOCAL
+    unit = 2**FIRST
     return -(-f // unit) * unit
 
 
@@ -83,31 +85,38 @@
     return total
 
 
-def prep_kernel(watt, cat_ref, u_ref, sub_ref, heat_ref, a_ref, b_ref, *, halo):
-    layers, height, width = u_ref.shape
+def prep_kernel(watt_hbm, cat_hbm, u_hbm, sub_hbm, planes, a_ref, b_ref, watt, cat_ref, sub_ref, sems, *, halo):
+    layers, height, width = u_hbm.shape
+    copies = [
+        pltpu.make_async_copy(source, target, sems.at[n])
+        for n, (source, target) in enumerate(
+            ((u_hbm, planes.at[pl.ds(0, layers)]), (sub_hbm, sub_ref), (cat_hbm, cat_ref), (watt_hbm, watt))
+        )
+    ]
+    for copy in copies:
+        copy.start()
+    for copy in copies:
+        copy.wait()
     cat = cat_ref[...]
     power = jnp.zeros(cat.shape, F32)
     for n in range(watt.shape[0]):
         power = power + jnp.where(cat == n, watt[n], 0.0)
     spread_r = (iota((height, cat.shape[0]), 0) // TILE == iota((height, cat.shape[0]), 1)).astype(F32)
     spread_c = (iota((cat.shape[1], width), 1) // TILE == iota((cat.shape[1], width), 0)).astype(F32)
-    heat_ref[...] = dot(dot(spread_r, power), spread_c)
+    planes[2 * layers] = dot(dot(spread_r, power), spread_c)
     even = lax.axis_index("gy") % 2 == 0
     for q in range(2 * layers + 1):
-        if q < layers:
-            plane = u_ref[q]
-        elif q < 2 * layers:
-            plane = (sub_ref[q - layers] + 1).astype(F32)
-        else:
-            plane = heat_ref[...]
-        turned = plane.T
+        if layers <= q < 2 * layers:
+            planes[q] = (sub_ref[q - layers] + 1).astype(F32)
+        turned = planes[q].T
         low, high = turned[:halo], turned[width - halo :]
         a_ref[q] = jnp.where(even, high, low)
         b_ref[q] = jnp.where(even, low, high)
 
 
-def split_kernel(u_ref, sub_ref, heat_ref, ra, rb, out, a_ref, b_ref, scr, *, halo):
-    layers, height, width = u_ref.shape
+def split_kernel(own, ra, rb, out, a_ref, b_ref, scr, *, halo):
+    count, height, width = own.shape
+    layers = count // 2
     even_y, even_x = lax.axis_index("gy") % 2 == 0, lax.axis_index("gx") % 2 == 0
     half, hh = height // 2, halo // 2
     source, target = iota((width + LANES, 2 * LANES), 0), iota((width + LANES, 2 * LANES), 1)
@@ -117,17 +126,11 @@
     )
     pick = ((source == want) & (cell < 2 * halo + width)).astype(F32)
     planes = []
-    for q in range(2 * layers + 1):
-        if q < layers:
-            plane = u_ref[q]
-        elif q < 2 * layers:
-            plane = (sub_ref[q - layers] + 1).astype(F32)
-        else:
-            plane = heat_ref[...]
+    for q in range(count):
         left = jnp.where(even_y, rb[q], ra[q])
         right = jnp.where(even_y, ra[q], rb[q])
         sides = jnp.concatenate([left, right, jnp.zeros((LANES - 2 * halo, height), F32)], 0).T
-        planes.append(jnp.concatenate([plane, sides], 1))
+        planes.append(jnp.concatenate([own[q], sides], 1))
     first = pick_dot(jnp.concatenate(planes[:layers] + planes[2 * layers :], 0), pick)
     second = pick_dot(jnp.concatenate(planes[layers : 2 * layers], 0), pick, 1)
     for q in range(2 * layers + 1):
@@ -182,18 +185,20 @@
     over(lo, hi, MOST["split"], body)
 
 
-def sides_of(tiles, lane):
+def sides_of(tiles, edge):
     count = len(tiles)
-    turned_r = [pltpu.roll(x, 1, 1) for x in tiles]
-    turned_l = [pltpu.roll(x, LANES - 1, 1) for x in tiles]
-    left = [
-        jnp.where(lane == 0, turned_r[i - 1] if i else 0.0, turned_r[i]) for i in range(count)
-    ]
-    right = [
-        jnp.where(lane == LANES - 1, turned_l[i + 1] if i < count - 1 else 0.0, turned_l[i])
-        for i in range(count)
-    ]
-    return left, right
+    left = [pltpu.roll(x, 1, 1) for x in tiles]
+    right = [pltpu.roll(x, LANES - 1, 1) for x in tiles]
+    if count == 1 and not edge:
+        return left, right
+    lane = iota(tiles[0].shape, 1)
+    return (
+        [jnp.where(lane == 0, left[i - 1] if i else 0.0, left[i]) for i in range(count)],
+        [
+            jnp.where(lane == LANES - 1, right[i + 1] if i < count - 1 else 0.0, right[i])
+            for i in range(count)
+        ],
+    )
 
 
 def nat_setup(s, factor):
@@ -201,10 +206,9 @@
     c = 0.5 * factor
 
     def body(t):
-        lane = iota((8 * t[1], LANES), 1)
         for k in range(layers):
             lat = [s["lat"][i, k, rows(t)] for i in range(tiles)]
-            left, right = sides_of(lat, lane)
+            left, right = sides_of(lat, s["edge"])
             for i in range(tiles):
                 stor = s["stor"][i, k, rows(t)]
                 above = c * (lat[i] + s["lat"][i, k, rows(t, -1)])
@@ -245,10 +249,9 @@
     tiles, layers = s["u"].shape[:2]
 
     def body(t):
-        lane = iota((8 * t[1], LANES), 1)
-        odd = (iota((8 * t[1], LANES), 0) + lane) % 2
+        odd = (iota((8 * t[1], LANES), 0) + iota((8 * t[1], LANES), 1)) % 2
         mid = [[s["u"][i, k, rows(t)] for i in range(tiles)] for k in range(layers)]
-        sides = [sides_of(m, lane) for m in mid]
+        sides = [sides_of(m, s["edge"]) for m in mid]
         for k in range(layers):
             chosen = odd == (colour + k) % 2
             for i in range(tiles):
@@ -278,9 +281,8 @@
     tiles, layers = s["u"].shape[:2]
 
     def body(t):
-        lane = iota((8 * t[1], LANES), 1)
         mid = [[s["u"][i, k, rows(t)] for i in range(tiles)] for k in range(layers)]
-        sides = [sides_of(m, lane) for m in mid]
+        sides = [sides_of(m, s["edge"]) for m in mid]
         for k in range(layers):
             for i in range(tiles):
                 total = s["f"][i, k, rows(t)] + nat_sum(s, mid, sides, i, k, t, layers)
@@ -355,23 +357,44 @@
 NAT_OTHER = ("lat", "vert", "stor", "diag")
 
 
+def pack_own(payload, last, res, mine, off):
+    layers = res.shape[1]
+    group = 4 * mine
+    per = LANES // group
+    quantities = (res, last["lat"], last["vert"], last["stor"])
+    parts = []
+    for k in range(layers):
+        for ref in quantities:
+            part = ref[0, k, pl.ds(PAD + off, mine, stride=2), :]
+            parts.append(part + ref[0, k, pl.ds(PAD + off + 1, mine, stride=2), :])
+    source, target = iota((LANES, LANES), 0), iota((LANES, LANES), 1)
+    hit = (source >= off) & ((source - off) // 2 == target) & (target < mine)
+    packed = pick_dot(jnp.concatenate(parts, 0), jnp.where(hit, 0.25, 0.0))
+    for pair in range(-(-layers // per)):
+        total = jnp.zeros((mine, LANES), F32)
+        for n in range(pair * per * 4, min(layers, (pair + 1) * per) * 4):
+            part, base = packed[n * mine : (n + 1) * mine], (n - pair * per * 4) * mine
+            total += pltpu.roll(part, base, 1) if base else part
+        payload[pair * mine : (pair + 1) * mine] = total
+
+
 def down_kernel(*refs, halo, half, kinds):
     tables, (sp, ra, rb) = refs[:3], refs[3:6]
     refs = list(refs[6:])
     s = dict(zip(SPLIT_KEPT, refs[: len(SPLIT_KEPT)]))
     refs = refs[len(SPLIT_KEPT) :]
     nats = []
-    for level in range(1, LOCAL):
-        nats.append(dict(zip(NAT_KEPT, refs[: len(NAT_KEPT)])))
+    for level in range(1, FIRST):
+        nats.append(dict(zip(NAT_KEPT, refs[: len(NAT_KEPT)]), edge=False))
         refs = refs[len(NAT_KEPT) :]
     payload = refs.pop(0)
-    for name in ("lat", "vert", "stor"):
+    for name in ("lat", "vert", "stor", "diag"):
         s[name] = refs.pop(0)
     heat = refs.pop(0)
-    for level in range(1, LOCAL):
+    for level in range(1, FIRST):
         for name in NAT_OTHER:
             nats[level - 1][name] = refs.pop(0)
-    ress = [refs.pop(0) for level in range(1, LOCAL)]
+    ress = [refs.pop(0) for level in range(1, FIRST)]
     layers = s["u"].shape[1]
     height = s["u"].shape[2]
     hh = halo // 2
@@ -392,7 +415,7 @@
                 s[name][pj, k, :PAD] = zeros
                 s[name][pj, k, height - PAD :] = zeros
             place(s["u"], (pj, k), k, pj)
-            place(s["stor"], (pj, k), layers + k, pj)
+            place(s["diag"], (pj, k), layers + k, pj)
         place(heat, (pj,), 2 * layers, pj)
     for j in range(2):
         for k in range(layers):
@@ -410,7 +433,7 @@
             sums = [None, None, None]
             for pj in range(4):
                 at = (pj, k, rows(t))
-                label = s["stor"][at]
+                label = s["diag"][at]
                 value = [jnp.zeros_like(label)] * 3
                 for n in range(kinds):
                     hit = label == float(n + 1)
@@ -458,7 +481,7 @@
                         diag += 0.5 * (vert + s["vert"][pj, k + 1, at])
                     inside = stor > 0.0
                     s["invd"][pj, k, at] = jnp.where(inside, 1.0 / jnp.where(inside, diag, 1.0), 0.0)
-                    s["stor"][pj, k, at] = diag
+                    s["diag"][pj, k, at] = diag
 
     over(0, steps, MOST["faces"], faces)
     for sweep in range(2):
@@ -473,48 +496,78 @@
                     if (p + j + k) % 2 == 0:
                         pj = 2 * p + j
                         r = s["f"][pj, k, rows(t)] + split_sum(s, p, j, k, t, layers)
-                        r -= s["stor"][pj, k, rows(t)] * s["u"][pj, k, rows(t)]
+                        r -= s["diag"][pj, k, rows(t)] * s["u"][pj, k, rows(t)]
                         total = r if total is None else total + r
             first["f"][0, k, rows(t)] = total * 0.25
 
     over(0, steps, MOST["remain"], remain)
 
-    for level in range(1, LOCAL):
+    for level in range(1, FIRST):
         now = nats[level - 1]
         nat_setup(now, 0.25**level)
         count = (now["u"].shape[2] - 2 * PAD) // 8
         nat_down(now, ress[level - 1], count)
-        if level < LOCAL - 1:
+        if level < FIRST - 1:
             below = nats[level]
             pairs = [(now[name], below[name]) for name in ("lat", "vert", "stor")]
             restrict_all(pairs + [(ress[level - 1], below["f"])])
 
-    last, res = nats[-1], ress[-1]
-    mine = 2 * half >> LOCAL
-    off = halo >> (LOCAL - 1)
-    group = 4 * mine
-    per = LANES // group
-    quantities = (res, last["lat"], last["vert"], last["stor"])
-    parts = []
-    for k in range(layers):
-        for ref in quantities:
-            part = ref[0, k, pl.ds(PAD + off, mine, stride=2), :]
-            parts.append(part + ref[0, k, pl.ds(PAD + off + 1, mine, stride=2), :])
-    source, target = iota((LANES, LANES), 0), iota((LANES, LANES), 1)
-    hit = (source >= off) & ((source - off) // 2 == target) & (target < mine)
-    packed = pick_dot(jnp.concatenate(parts, 0), jnp.where(hit, 0.25, 0.0))
-    for pair in range(-(-layers // per)):
-        total = jnp.zeros((mine, LANES), F32)
-        for n in range(pair * per * 4, min(layers, (pair + 1) * per) * 4):
-            part, base = packed[n * mine : (n + 1) * mine], (n - pair * per * 4) * mine
-            total += pltpu.roll(part, base, 1) if base else part
-        payload[pair * mine : (pair + 1) * mine] = total
+    pack_own(payload, nats[-1], ress[-1], 2 * half >> FIRST, halo >> (FIRST - 1))
+
+
+def mid_kernel(own, ra, rb, ta, tb, *refs):
+    refs = list(refs)
+    count = LOCAL - FIRST
+    nats = []
+    for n in range(count):
+        nats.append(dict(zip(NAT_KEPT, refs[: len(NAT_KEPT)]), edge=False))
+        refs = refs[len(NAT_KEPT) :]
+    payload = refs.pop(0)
+    for n in range(count):
+        for name in NAT_OTHER:
+            nats[n][name] = refs.pop(0)
+    ress = refs
+    layers = nats[0]["u"].shape[1]
+    mine = own.shape[0] // layers
+    even_y, even_x = lax.axis_index("gy") % 2 == 0, lax.axis_index("gx") % 2 == 0
+    zeros = jnp.zeros((PAD, LANES), F32)
+    for now, res in zip(nats, ress):
+        for ref in [now[name] for name in ("lat", "vert", "stor", "f")] + [res]:
+            for k in range(layers):
+                ref[0, k, :PAD] = zeros
+                ref[0, k, ref.shape[2] - PAD :] = zeros
+    group = iota((mine, LANES), 1) // mine
+    for v in range(3):
+        for k in range(layers):
+            lines = slice(k * mine, (k + 1) * mine)
+            if v == 1:
+                middle, a, b = own[lines], ra[lines], rb[lines]
+            else:
+                first, second = (tb, ta) if v == 0 else (ta, tb)
+                middle, a, b = [jnp.where(even_x, first[n, lines], second[n, lines]) for n in range(3)]
+            left, right = jnp.where(even_y, b, a), jnp.where(even_y, a, b)
+            middle, right = pltpu.roll(middle, mine, 1), pltpu.roll(right, 2 * mine, 1)
+            for n, name in enumerate(("f", "lat", "vert", "stor")):
+                value = jnp.where(group == (n + 1) % 4, middle, right)
+                value = jnp.where(group == n, left, value)
+                value = jnp.where(group == (n + 3) % 4, 0.0, value)
+                if n:
+                    value = pltpu.roll(value, LANES - n * mine, 1)
+                nats[0][name][0, k, PAD + v * mine : PAD + (v + 1) * mine] = value
+    for n, level in enumerate(range(FIRST, LOCAL)):
+        now = nats[n]
+        nat_setup(now, 0.25**level)
+        nat_down(now, ress[n], (now["u"].shape[2] - 2 * PAD) // 8)
+        if n < count - 1:
+            pairs = [(now[name], nats[n + 1][name]) for name in ("lat", "vert", "stor")]
+            restrict_all(pairs + [(ress[n], nats[n + 1]["f"])])
+    pack_own(payload, nats[-1], ress[-1], mine >> count, mine >> (count - 1))
 
 
 def conjugate(s):
     tiles, layers, height, _ = s["u"].shape
     n = height - 2 * PAD
-    row, lane = iota((n, LANES), 0), iota((n, LANES), 1)
+    row = iota((n, LANES), 0)
     spots = [(i, k) for k in range(layers) for i in range(tiles)]
     body_rows = slice(PAD, PAD + n)
 
@@ -522,7 +575,7 @@
         out = []
         for k in range(layers):
             tiles_of = [v[k * tiles + i] for i in range(tiles)]
-            left, right = sides_of(tiles_of, lane)
+            left, right = sides_of(tiles_of, s["edge"])
             for i in range(tiles):
                 mid = tiles_of[i]
                 wr = s["wr"][i, k, body_rows]
@@ -578,12 +631,13 @@
     refs = refs[len(SPLIT_KEPT) :]
     nats = []
     for level in range(1, LOCAL):
-        nats.append(dict(zip(NAT_KEPT, refs[: len(NAT_KEPT)])))
+        nats.append(dict(zip(NAT_KEPT, refs[: len(NAT_KEPT)]), edge=False))
         refs = refs[len(NAT_KEPT) :]
     out = refs.pop(0)
     wholes = []
     for level in range(LOCAL, LEVELS + 1):
-        wholes.append(dict(zip(WHOLE, refs[: len(WHOLE)])))
+        edge = (spans[1] * 2 * half >> level) % LANES == 0
+        wholes.append(dict(zip(WHOLE, refs[: len(WHOLE)]), edge=edge))
         refs = refs[len(WHOLE) :]
     ress = [refs.pop(0) for level in range(LOCAL, LEVELS)]
     fresh = [refs.pop(0) for level in range(LOCAL)]
@@ -606,20 +660,23 @@
 
     def gather(x, carry):
         at = pl.ds(pl.multiple_of(x * mine, 8) + PAD, mine)
-        for k in range(layers):
-            for n, name in enumerate(("f", "lat", "vert", "stor")):
-                base = (k % per) * group + n * mine
-                lines = slice((k // per) * mine, (k // per + 1) * mine)
-                for i in range(tiles):
-                    total = jnp.zeros((mine, LANES), F32)
-                    for y in range(ny):
-                        if y * mine // LANES == i:
-                            to = y * mine % LANES
-                            part = gathered[x * ny + y, lines]
-                            if to != base:
-                                part = pltpu.roll(part, (to - base) % LANES, 1)
-                            total = jnp.where((lane >= to) & (lane < to + mine), part, total)
-                    top[name][i, k, at] = total
+        for i in range(tiles):
+            here = [y for y in range(ny) if y * mine // LANES == i]
+            for wide in range(-(-layers // per)):
+                lines = slice(wide * mine, (wide + 1) * mine)
+                parts = []
+                for y in here:
+                    part = gathered[x * ny + y, lines]
+                    to = y * mine % LANES
+                    parts.append(pltpu.roll(part, to, 1) if to else part)
+                for k in range(wide * per, min(layers, (wide + 1) * per)):
+                    for n, name in enumerate(("f", "lat", "vert", "stor")):
+                        base = (k % per) * group + n * mine
+                        total = jnp.zeros((mine, LANES), F32)
+                        for y, part in zip(here, parts):
+                            spot = (base + y * mine) % LANES
+                            total = jnp.where((lane >= spot) & (lane < spot + mine), part, total)
+                        top[name][i, k, at] = pltpu.roll(total, LANES - base, 1) if base else total
         return carry
 
     lax.fori_loop(0, nx, gather, 0)
@@ -638,7 +695,7 @@
         nat_up(now, 0, (now["u"].shape[2] - 2 * PAD) // 8)
 
     x, y = lax.axis_index("gx"), lax.axis_index("gy")
-    reach = halo >> LOCAL
+    reach = (2 * half >> FIRST) >> (LOCAL - FIRST)
     need = (nats[-1]["u"].shape[2] - 2 * PAD) // 2
     height = top["u"].shape[2]
     for i in range(tiles):
@@ -661,6 +718,10 @@
         return value
 
     coarse = window
+    margins, above = [], 0
+    for level in range(LOCAL):
+        margins.append(above + 4)
+        above = -(-margins[-1] // 2)
     for level in reversed(range(1, LOCAL)):
         now = dict(nats[level - 1])
         before = now["u"]
@@ -671,11 +732,19 @@
                 now["u"][i, k, :PAD] = jnp.zeros((PAD, LANES), F32)
                 now["u"][i, k, height - PAD :] = jnp.zeros((PAD, LANES), F32)
         prolong_into(now, before, coarse, level == LOCAL - 1)
-        side = halo >> level
         own = 2 * half >> level
-        margin = {0: 4, 1: 6, 2: 7}.get(level, 8)
-        nat_up(now, (side - margin) // 8, min(-(-(side + own + margin) // 8), (height - 2 * PAD) // 8))
+        side = halo >> level if level < FIRST else (2 * half >> FIRST) >> (level - FIRST)
+        reach = margins[level]
+        nat_up(now, (side - reach) // 8, min(-(-(side + own + reach) // 8), (height - 2 * PAD) // 8))
         coarse = functools.partial(lambda ref, o, k: ref[o, k, PAD : ref.shape[2] - PAD], now["u"])
+        if level == FIRST:
+            skip = side - (halo >> FIRST)
+            coarse = functools.partial(
+                lambda ref, o, k: pltpu.roll(
+                    ref[o, k, PAD + skip : ref.shape[2] - PAD], LANES - skip, 1
+                ),
+                now["u"],
+            )
 
     now = dict(s)
     now["u"] = fresh[0]
@@ -715,6 +784,22 @@
     return jax.ShapeDtypeStruct(dims, F32)
 
 
+def packed_shape(layers, mine):
+    per = LANES // (4 * mine)
+    return shape(-(-layers // per) * mine, LANES)
+
+
+def whole_shape(level, layers, height, width):
+    return -(-(width >> level) // LANES), layers, up8(height >> level) + 2 * PAD, LANES
+
+
+def other_scratch(shapes):
+    out = []
+    for d in shapes:
+        out += [pltpu.VMEM(d, F32)] * len(NAT_OTHER)
+    return out + [pltpu.VMEM(d, F32) for d in shapes]
+
+
 def on_device(u0, sub, cat, planar, vertical, ratio, watt):
     nx, ny = lax.axis_size("gx"), lax.axis_size("gy")
     layers, height, width = u0.shape
@@ -723,11 +808,17 @@
     planes = 2 * layers + 1
     assert height == width == LANES and 2 * halo <= LANES and halo + half <= LANES
 
-    heat, a, b = pl.pallas_call(
+    own, a, b = pl.pallas_call(
         functools.partial(prep_kernel, halo=halo),
-        out_shape=(shape(height, width), shape(planes, halo, height), shape(planes, halo, height)),
-        in_specs=[SMEM, VMEM, VMEM, VMEM],
+        out_shape=(shape(planes, height, width), shape(planes, halo, height), shape(planes, halo, height)),
+        in_specs=[HBM] * 4,
         out_specs=(VMEM,) * 3,
+        scratch_shapes=[
+            pltpu.SMEM(watt.shape, F32),
+            pltpu.VMEM(cat.shape, jnp.int32),
+            pltpu.VMEM(sub.shape, jnp.int32),
+            pltpu.SemaphoreType.DMA((4,)),
+        ],
         compiler_params=limit(8),
         name="prep",
     )(watt, cat, u0, sub)
@@ -737,63 +828,75 @@
     sp, a, b = pl.pallas_call(
         functools.partial(split_kernel, halo=halo),
         out_shape=(shape(planes, 4, half, LANES), shape(lines, LANES), shape(lines, LANES)),
-        in_specs=[VMEM] * 5,
+        in_specs=[VMEM] * 3,
         out_specs=(VMEM,) * 3,
         scratch_shapes=[pltpu.VMEM((2, 2, height, LANES), F32)],
         compiler_params=limit(20),
         name="split",
-    )(u0, sub, heat, a, b)
+    )(own, a, b)
     a, b = swap(a, "gx", 0), swap(b, "gx", 1)
 
     tall = up8(half + 2 * hh) + 2 * PAD
     four, two = (4, layers, tall, LANES), (2, layers, tall, LANES)
-    split_shapes = [four if name in ("u", "f", "invd", "fl") else two for name in SPLIT_KEPT]
+    kept = [shape(*(four if name in ("u", "f", "invd", "fl") else two)) for name in SPLIT_KEPT]
     nat_shapes = [
-        (1, layers, up8((height + 2 * halo) >> level) + 2 * PAD, LANES) for level in range(1, LOCAL)
+        (1, layers, up8((height + 2 * halo) >> level) + 2 * PAD, LANES) for level in range(1, FIRST)
     ]
-    mine = height >> LOCAL
-    per = LANES // (4 * mine)
-    pairs = -(-layers // per)
-    kept = [shape(*d) for d in split_shapes]
     for d in nat_shapes:
         kept += [shape(*d)] * len(NAT_KEPT)
-    scratch = [pltpu.VMEM(four, F32)] * 3 + [pltpu.VMEM((4, tall, LANES), F32)]
-    for d in nat_shapes:
-        scratch += [pltpu.VMEM(d, F32)] * len(NAT_OTHER)
-    scratch += [pltpu.VMEM(d, F32) for d in nat_shapes]
-    *saved, payload = pl.pallas_call(
-        functools.partial(
-            down_kernel, halo=halo, half=half, kinds=planar.shape[0]
-        ),
-        out_shape=(*kept, shape(pairs * mine, LANES)),
+    scratch = [pltpu.VMEM(four, F32)] * 4 + [pltpu.VMEM((4, tall, LANES), F32)]
+    scratch += other_scratch(nat_shapes)
+    *saved, block = pl.pallas_call(
+        functools.partial(down_kernel, halo=halo, half=half, kinds=planar.shape[0]),
+        out_shape=(*kept, packed_shape(layers, height >> FIRST)),
         in_specs=[SMEM] * 3 + [VMEM] * 3,
         out_specs=(VMEM,) * (len(kept) + 1),
         scratch_shapes=scratch,
-        compiler_params=limit(36),
+        compiler_params=limit(30),
         name="down",
     )(planar, vertical, ratio, sp, a, b)
 
+    a, b = swap(block, "gy", 0), swap(block, "gy", 1)
+    column = jnp.stack([block, a, b])
+    above, below = swap(column, "gx", 0), swap(column, "gx", 1)
+    mine = height >> FIRST
+    assert 4 * mine <= LANES
+    block_shapes = [
+        (1, layers, up8(3 * mine >> n) + 2 * PAD, LANES) for n in range(LOCAL - FIRST)
+    ]
+    kept = []
+    for d in block_shapes:
+        kept += [shape(*d)] * len(NAT_KEPT)
+    *more, payload = pl.pallas_call(
+        mid_kernel,
+        out_shape=(*kept, packed_shape(layers, height >> LOCAL)),
+        in_specs=[VMEM] * 5,
+        out_specs=(VMEM,) * (len(kept) + 1),
+        scratch_shapes=other_scratch(block_shapes),
+        compiler_params=limit(20),
+        name="mid",
+    )(block, a, b, above, below)
+    saved += more
+    nat_shapes += block_shapes
+
     sent = jnp.broadcast_to(payload[None], (nx * ny,) + payload.shape)
     gathered = lax.all_to_all(sent, ("gx", "gy"), 0, 0)
 
     scratch = []
     for level in range(LOCAL, LEVELS + 1):
-        wide = -(-(ny * width >> level) // LANES)
-        d = (wide, layers, up8(nx * height >> level) + 2 * PAD, LANES)
-        scratch += [pltpu.VMEM(d, F32)] * len(WHOLE)
+        scratch += [pltpu.VMEM(whole_shape(level, layers, nx * height, ny * width), F32)] * len(WHOLE)
     for level in range(LOCAL, LEVELS):
-        wide = -(-(ny * width >> level) // LANES)
-        scratch.append(pltpu.VMEM((wide, layers, up8(nx * height >> level) + 2 * PAD, LANES), F32))
+        scratch.append(pltpu.VMEM(whole_shape(level, layers, nx * height, ny * width), F32))
     scratch += [pltpu.VMEM(four, F32)] + [pltpu.VMEM(d, F32) for d in nat_shapes]
     wide, count, rows_of, _ = scratch[0].shape
     scratch.append(pltpu.VMEM((wide, count, rows_of + PAD, LANES), F32))
     return pl.pallas_call(
         functools.partial(up_kernel, halo=halo, half=half, spans=(nx, ny)),
         out_shape=shape(layers, height, width),
-        in_specs=[VMEM] * (1 + len(kept)),
+        in_specs=[VMEM] * (1 + len(saved)),
         out_specs=VMEM,
         scratch_shapes=scratch,
-        compiler_params=limit(20, scratch),
+        compiler_params=limit(16, scratch),
         name="up",
     )(gathered, *saved)
 

time: 103 us -> 88.6 us (0.86)
  blocking collectives: 45.1 us -> 18.1 us
  starting transfers between devices: 4.48 us -> 25.6 us
  Pallas kernels: 37 us -> 32 us
  local copies, waits for them, and re-layouts: 5.39 us -> 3.36 us
  waiting for transfers between devices: 10.3 us -> 9.13 us
    all_to_all x1, blocking collectives: 45.1 us -> 18.1 us  [on_device(): gathered = lax.all_to_all(sent, ('gx', 'gy'), 0, 0)]
    ppermute x4 -> x8, starting transfers between devices: 4.48 us -> 25.6 us  [swap(): return lax.ppermute(values, axis, pairs + [(b, a) for a, b in pairs])]
    pallas_call x1, Pallas kernels: 22.1 us -> 16 us  [on_device(): pl.pallas_call(functools.partial(up_kernel, halo=halo, half=half, spans=(...]
    pallas_call x0 -> x1, Pallas kernels: none -> 5.1 us  [on_device(): pl.pallas_call(mid_kernel, out_shape=(*kept, packed_shape(layers, height...]
    pallas_call x1, Pallas kernels: 12.8 us -> 8.41 us  [on_device(): pl.pallas_call(functools.partial(down_kernel, halo=halo, half=half, kinds...]
    unnamed x18 -> x14, local copies, waits for them, and re-layouts: 5.33 us -> 3.34 us
    ppermute x4 -> x8, waiting for transfers between devices: 10.3 us -> 9.13 us  [swap(): return lax.ppermute(values, axis, pairs + [(b, a) for a, b in pairs])]
  transfers between devices with their start and end apart: 4 -> 8, of which waited for: 2 -> 4; matrix products, arithmetic and copies ran while one was open for 0% -> 0% of each run, Pallas kernels for 0% -> 0%
where the time goes in v3:
time: 88.6 us; the launch traced here: 88.3 us
  Pallas kernels  32 us (36%)
  starting transfers between devices  25.6 us (29%)
  blocking collectives  18.1 us (20%)
  waiting for transfers between devices  9.13 us (10%)
  local copies, waits for them, and re-layouts  3.36 us (4%)
    ppermute x8, starting transfers between devices, swap(): return lax.ppermute(values, axis, pairs + [(b, a) for a, b in pairs])  25.6 us
    all_to_all x1, blocking collectives, on_device(): gathered = lax.all_to_all(sent, ('gx', 'gy'), 0, 0)  18.1 us
    pallas_call x1, Pallas kernels, on_device(): pl.pallas_call(functools.partial(up_kernel, halo=halo, half=half, spans=(...  16 us
    ppermute x8, waiting for transfers between devices, swap(): return lax.ppermute(values, axis, pairs + [(b, a) for a, b in pairs])  9.13 us
    pallas_call x1, Pallas kernels, on_device(): pl.pallas_call(functools.partial(down_kernel, halo=halo, half=half, kinds...  8.41 us
    pallas_call x1, Pallas kernels, on_device(): pl.pallas_call(mid_kernel, out_shape=(*kept, packed_shape(layers, height...  5.1 us
    unnamed x14, local copies, waits for them, and re-layouts  3.34 us
  transfers between devices with their start and end apart: 8, of which 4 were waited for; matrix products, arithmetic and copies ran while one was open for 0% of the time, Pallas kernels for 0%

profile of v3, /device:TPU:0, one launch (start us, length us, event | category | flops | bytes accessed | tf_op | source)
XLA Modules:
  0.0 88.3 jit_solution(16564833689602853398)
XLA Ops:
  0.0 0.0 copy-start
  0.0 1.0 %copy-done = f32[6,128,128]{2,1,0:T(8,128)S(1)} copy-done((f32[6,128,128]{2,1,0:T(8,128)S(1)}, f32[6,128,128]{2,1,0:T(8,128)}, u32[]{:S(2)}) %copy-start) | copy-done | bytes 393240
  1.0 0.0 copy-start.1
  1.0 1.0 %copy-done.1 = s32[6,128,128]{2,1,0:T(8,128)S(1)} copy-done((s32[6,128,128]{2,1,0:T(8,128)S(1)}, s32[6,128,128]{2,1,0:T(8,128)}, u32[]{:S(2)}) %copy-start.1) | copy-done | bytes 393240
  2.0 0.0 copy-start.2
  2.0 0.7 copy-done.2
  2.7 0.7 copy-done.6
  3.3 1.5 %prep.1 = (f32[13,128,128]{2,1,0:T(8,128)S(1)}, f32[13,24,128]{2,1,0:T(8,128)S(1)}, f32[13,24,128]{2,1,0:T(8,128)S(1)}) custom-call(f32[64]{0:T(128)S(1)} %copy-done.6, s32[8,8]{1,0:T(8,128)S(1)} %copy-done.2, f32[6,128,128]{2,1,0:T(8,128)S(1)} %copy-done, s32[6,128,128]{2,1,0:T(8,128)S(1)} %copy-done.1), custom_call_target="tpu_custom_call" | custom-call | tf_op jit(solution)/shard_map/prep/pallas_call | solution.py:811
  4.9 3.0 %collective-permute-start = (f32[13,24,128]{2,1,0:T(8,128)S(1)}, f32[13,24,128]{2,1,0:T(8,128)S(1)}, u32[]{:S(2)}, u32[]{:S(2)}) collective-permute-start(f32[13,24,128]{2,1,0:T(8,128)S(1)} %get-tuple-element.44), channel_id=1, source_target_pairs={{0,1},{2,3},{1,0},{3,2},{4,5},{6,7},{5,4},{7,6},{8,9},{10,11},{9,8... | collective-permute-start | bytes 479240 | tf_op jit(solution)/shard_map/ppermute | solution.py:780
  7.9 0.7 collective-permute-start.1
  8.6 3.4 %collective-permute-done.ra = f32[13,24,128]{2,1,0:T(8,128)S(1)} collective-permute-done((f32[13,24,128]{2,1,0:T(8,128)S(1)}, f32[13,24,128]{2,1,0:T(8,128)S(1)}, u32[]{:S(2)}, u32[]{:S(2)}) %collective-permute-start) | collective-permute-done | bytes 159776 | tf_op jit(solution)/shard_map/ppermute | solution.py:780
  12.0 0.0 collective-permute-done.1.rb
  12.0 0.9 %split.1 = (f32[13,4,64,128]{3,2,1,0:T(8,128)S(1)}, f32[624,128]{1,0:T(8,128)S(1)}, f32[624,128]{1,0:T(8,128)S(1)}) custom-call(f32[13,128,128]{2,1,0:T(8,128)S(1)} %get-tuple-element.43.own, f32[13,24,128]{2,1,0:T(8,128)S(1)} %collective-permute-done.ra, f32[13,24,128]{2,1,0:T(8,128)S(1)} %collective-permute-done.1.rb), custom_call_target="tpu_custom_call" | custom-call | tf_op jit(solution)/shard_map/split/pallas_call | solution.py:828
  12.9 0.1 collective-permute-start.2
  13.0 0.7 collective-permute-start.3
  13.7 0.9 %collective-permute-done.2.refs_4_ = f32[624,128]{1,0:T(8,128)S(1)} collective-permute-done((f32[624,128]{1,0:T(8,128)S(1)}, f32[624,128]{1,0:T(8,128)S(1)}, u32[]{:S(2)}, u32[]{:S(2)}) %collective-permute-start.2) | collective-permute-done | bytes 319520 | tf_op jit(solution)/shard_map/ppermute | solution.py:780
  14.6 0.0 collective-permute-done.3.refs_5_
  14.6 0.0 copy-done.3
  14.6 0.0 copy-done.4
  14.6 0.0 copy-done.5
  14.6 8.4 %down.1 = (f32[4,6,104,128]{3,2,1,0:T(8,128)S(1)}, f32[4,6,104,128]{3,2,1,0:T(8,128)S(1)}, f32[4,6,104,128]{3,2,1,0:T(8,128)S(1)}, f32[2,6,104,128]{3,2,1,0:T(8,...) custom-call(f32[8]{0:T(128)S(1)} %copy-done.3, ...), custom_call_target="tpu_custom_call" | custom-call | tf_op jit(solution)/shard_map/down/pallas_call | solution.py:849
  23.1 0.7 collective-permute-start.5
  23.7 8.5 %collective-permute-start.4 = (f32[192,128]{1,0:T(8,128)S(1)}, f32[192,128]{1,0:T(8,128)S(1)}, u32[]{:S(2)}, u32[]{:S(2)}) collective-permute-start(f32[192,128]{1,0:T(8,128)S(1)} %get-tuple-element.49.own), channel_id=1, source_target_pairs={{0,1},{2,3},{1,0},{3,2},{4,5},{6,7},{5,4},{7,6},{8,9},{10,11},{9,8... | collective-permute-start | bytes 294920 | tf_op jit(solution)/shard_map/ppermute | solution.py:780
  32.3 0.0 collective-permute-done.5.rb
  32.3 3.6 %collective-permute-done.4.ra = f32[192,128]{1,0:T(8,128)S(1)} collective-permute-done((f32[192,128]{1,0:T(8,128)S(1)}, f32[192,128]{1,0:T(8,128)S(1)}, u32[]{:S(2)}, u32[]{:S(2)}) %collective-permute-start.4) | collective-permute-done | bytes 98336 | tf_op jit(solution)/shard_map/ppermute | solution.py:780
  35.8 0.7 collective-permute-start.7
  36.5 11.3 %collective-permute-start.6 = (f32[3,192,128]{2,1,0:T(8,128)S(1)}, f32[3,192,128]{2,1,0:T(8,128)S(1)}, u32[]{:S(2)}, u32[]{:S(2)}) collective-permute-start(f32[3,192,128]{2,1,0:T(8,128)S(1)} %pad_maximum_fusion), channel_id=1, source_target_pairs={{0,4},{8,12},{16,20},{24,28},{4,0},{12,8},{20,16},{28,24},{1,5},{9... | collective-permute-start | bytes 884744 | tf_op jit(solution)/shard_map/ppermute | solution.py:780
  47.8 0.0 collective-permute-done.7.tb
  47.8 1.2 %collective-permute-done.6.ta = f32[3,192,128]{2,1,0:T(8,128)S(1)} collective-permute-done((f32[3,192,128]{2,1,0:T(8,128)S(1)}, f32[3,192,128]{2,1,0:T(8,128)S(1)}, u32[]{:S(2)}, u32[]{:S(2)}) %collective-permute-start.6) | collective-permute-done | bytes 294944 | tf_op jit(solution)/shard_map/ppermute | solution.py:780
  49.0 5.1 %mid.1 = (f32[1,6,112,128]{3,2,1,0:T(8,128)S(1)}, f32[1,6,112,128]{3,2,1,0:T(8,128)S(1)}, f32[1,6,112,128]{3,2,1,0:T(8,128)S(1)}, f32[1,6,112,128]{3,2,1,0:T(8,1...) custom-call(f32[192,128]{1,0:T(8,128)S(1)} %get-tuple-element.49.own, ...), custom_call_target="tpu_custom_call" | custom-call | tf_op jit(solution)/shard_map/mid/pallas_call | solution.py:870
  54.2 18.1 %all_to_all.5.refs_0_ = f32[32,16,128]{2,1,0:T(8,128)S(1)} all-to-all(f32[32,16,128]{2,1,0:T(8,128)S(1)} %broadcast_in_dim.2), channel_id=1, replica_groups=mesh['gx'=8,'gy'=4] {'gx','gy'}, dimensions={0} | all-to-all | bytes 524288 | tf_op jit(solution)/shard_map/all_to_all | solution.py:883
  72.3 16.0 %up.1 = f32[6,128,128]{2,1,0:T(8,128)} custom-call(f32[32,16,128]{2,1,0:T(8,128)S(1)} %all_to_all.5.refs_0_, f32[4,6,104,128]{3,2,1,0:T(8,128)S(1)} %get-tuple-element.51.refs_1_, f32[4,6,104,128]{3,2,1,0:T(8,128)S(1)} %get-tuple-element.52.refs_2_, f32[4,6,104,128]{3,2,1,0:T(8,128)S(1)} %get-tuple-element.53.refs_3_, ...), custom_call_target="tpu_custom_call" | custom-call | tf_op jit(solution)/shard_map/up/pallas_call | solution.py:893
  (6 shorter events, 0.0 us)
Async XLA Ops:
  0.0 1.0 %copy-start = (f32[6,128,128]{2,1,0:T(8,128)S(1)}, f32[6,128,128]{2,1,0:T(8,128)}, u32[]{:S(2)}) copy-start(f32[6,128,128]{2,1,0:T(8,128)} %u_hbm.1) | copy-start | bytes 1179652
  1.0 1.0 %copy-start.1 = (s32[6,128,128]{2,1,0:T(8,128)S(1)}, s32[6,128,128]{2,1,0:T(8,128)}, u32[]{:S(2)}) copy-start(s32[6,128,128]{2,1,0:T(8,128)} %sub_hbm.1) | copy-start | bytes 1179652
  2.0 0.7 copy-start.2
  2.7 0.7 copy-start.6
  3.3 11.3 %copy-start.3 = (f32[8]{0:T(128)S(1)}, f32[8]{0:T(128)}, u32[]{:S(2)}) copy-start(f32[8]{0:T(128)} %refs_0_.1) | copy-start | bytes 100
  3.3 11.3 %copy-start.4 = (f32[8]{0:T(128)S(1)}, f32[8]{0:T(128)}, u32[]{:S(2)}) copy-start(f32[8]{0:T(128)} %refs_1_.1) | copy-start | bytes 100
  3.3 11.3 %copy-start.5 = (f32[8]{0:T(128)S(1)}, f32[8]{0:T(128)}, u32[]{:S(2)}) copy-start(f32[8]{0:T(128)} %refs_2_.1) | copy-start | bytes 100
  4.9 7.1 %collective-permute-start = (f32[13,24,128]{2,1,0:T(8,128)S(1)}, f32[13,24,128]{2,1,0:T(8,128)S(1)}, u32[]{:S(2)}, u32[]{:S(2)}) collective-permute-start(f32[13,24,128]{2,1,0:T(8,128)S(1)} %get-tuple-element.44), channel_id=1, source_target_pairs={{0,1},{2,3},{1,0},{3,2},{4,5},{6,7},{5,4},{7,6},{8,9},{10,11},{9,8... | collective-permute-start | bytes 479240 | tf_op jit(solution)/shard_map/ppermute | solution.py:780
  7.9 4.1 %collective-permute-start.1 = (f32[13,24,128]{2,1,0:T(8,128)S(1)}, f32[13,24,128]{2,1,0:T(8,128)S(1)}, u32[]{:S(2)}, u32[]{:S(2)}) collective-permute-start(f32[13,24,128]{2,1,0:T(8,128)S(1)} %get-tuple-element.45), channel_id=1, source_target_pairs={{1,2},{2,1},{5,6},{6,5},{9,10},{10,9},{13,14},{14,13},{17,18},{18,... | collective-permute-start | bytes 479240 | tf_op jit(solution)/shard_map/ppermute | solution.py:780
  12.9 1.7 %collective-permute-start.2 = (f32[624,128]{1,0:T(8,128)S(1)}, f32[624,128]{1,0:T(8,128)S(1)}, u32[]{:S(2)}, u32[]{:S(2)}) collective-permute-start(f32[624,128]{1,0:T(8,128)S(1)} %get-tuple-element.47), channel_id=1, source_target_pairs={{0,4},{8,12},{16,20},{24,28},{4,0},{12,8},{20,16},{28,24},{1,5},{9... | collective-permute-start | bytes 958472 | tf_op jit(solution)/shard_map/ppermute | solution.py:780
  13.0 1.6 %collective-permute-start.3 = (f32[624,128]{1,0:T(8,128)S(1)}, f32[624,128]{1,0:T(8,128)S(1)}, u32[]{:S(2)}, u32[]{:S(2)}) collective-permute-start(f32[624,128]{1,0:T(8,128)S(1)} %get-tuple-element.48), channel_id=1, source_target_pairs={{4,8},{12,16},{20,24},{8,4},{16,12},{24,20},{5,9},{13,17},{21,25},... | collective-permute-start | bytes 958472 | tf_op jit(solution)/shard_map/ppermute | solution.py:780
  23.1 9.2 %collective-permute-start.5 = (f32[192,128]{1,0:T(8,128)S(1)}, f32[192,128]{1,0:T(8,128)S(1)}, u32[]{:S(2)}, u32[]{:S(2)}) collective-permute-start(f32[192,128]{1,0:T(8,128)S(1)} %get-tuple-element.49.own), channel_id=1, source_target_pairs={{1,2},{2,1},{5,6},{6,5},{9,10},{10,9},{13,14},{14,13},{17,18},{18,... | collective-permute-start | bytes 294920 | tf_op jit(solution)/shard_map/ppermute | solution.py:780
  23.7 12.1 %collective-permute-start.4 = (f32[192,128]{1,0:T(8,128)S(1)}, f32[192,128]{1,0:T(8,128)S(1)}, u32[]{:S(2)}, u32[]{:S(2)}) collective-permute-start(f32[192,128]{1,0:T(8,128)S(1)} %get-tuple-element.49.own), channel_id=1, source_target_pairs={{0,1},{2,3},{1,0},{3,2},{4,5},{6,7},{5,4},{7,6},{8,9},{10,11},{9,8... | collective-permute-start | bytes 294920 | tf_op jit(solution)/shard_map/ppermute | solution.py:780
  35.8 12.0 %collective-permute-start.7 = (f32[3,192,128]{2,1,0:T(8,128)S(1)}, f32[3,192,128]{2,1,0:T(8,128)S(1)}, u32[]{:S(2)}, u32[]{:S(2)}) collective-permute-start(f32[3,192,128]{2,1,0:T(8,128)S(1)} %pad_maximum_fusion), channel_id=1, source_target_pairs={{4,8},{12,16},{20,24},{8,4},{16,12},{24,20},{5,9},{13,17},{21,25},... | collective-permute-start | bytes 884744 | tf_op jit(solution)/shard_map/ppermute | solution.py:780
  36.5 12.5 %collective-permute-start.6 = (f32[3,192,128]{2,1,0:T(8,128)S(1)}, f32[3,192,128]{2,1,0:T(8,128)S(1)}, u32[]{:S(2)}, u32[]{:S(2)}) collective-permute-start(f32[3,192,128]{2,1,0:T(8,128)S(1)} %pad_maximum_fusion), channel_id=1, source_target_pairs={{0,4},{8,12},{16,20},{24,28},{4,0},{12,8},{20,16},{28,24},{1,5},{9... | collective-permute-start | bytes 884744 | tf_op jit(solution)/shard_map/ppermute | solution.py:780

commit v4 on v3

--- a/solution.py
+++ b/solution.py
@@ -15,7 +15,7 @@
 COARSE_ITERS = 12
 LANES = 128
 PAD = 8
-MOST = dict(split=3, nat=4, first=4, residual=4, setup=4, look=2, faces=2, remain=3, add=4)
+MOST = dict(split=6, nat=12, first=12, residual=12, setup=6, look=1, faces=4, remain=6, add=4)
 HI = lax.Precision.HIGHEST
 F32 = jnp.float32
 VMEM = pl.BlockSpec(memory_space=pltpu.VMEM)
@@ -151,36 +151,43 @@
                 b_ref[at : at + hh] = jnp.where(even_x, first_rows, last_rows)
 
 
-def split_sum(s, p, j, k, t, layers):
-    u = s["u"]
-    at = rows(t)
-    total = s["fri"][j, k, at] * u[2 * (1 - p) + j, k, at]
-    if p == 0:
-        total += s["fro"][j, k, at] * u[2 + j, k, rows(t, -1)]
-    else:
-        total += s["fro"][j, k, rows(t, 1)] * u[j, k, rows(t, 1)]
-    total += s["fci"][p, k, at] * u[2 * p + 1 - j, k, at]
-    if j == 0:
-        total += s["fco"][p, k, at] * pltpu.roll(u[2 * p + 1, k, at], 1, 1)
-    else:
-        total += s["fcr"][p, k, at] * pltpu.roll(u[2 * p, k, at], LANES - 1, 1)
-    pj = 2 * p + j
-    if k > 0:
-        total += s["fl"][pj, k, at] * u[pj, k - 1, at]
-    if k < layers - 1:
-        total += s["fl"][pj, k + 1, at] * u[pj, k + 1, at]
-    return total
+def split_block(s, colour, t, layers):
+    u, at = s["u"], rows(t)
+    other = {
+        (p, j, k): u[2 * p + j, k, at]
+        for k in range(layers)
+        for p in range(2)
+        for j in range(2)
+        if (p + j + k) % 2 != colour
+    }
+    for k in range(layers):
+        for p in range(2):
+            for j in range(2):
+                if (p + j + k) % 2 != colour:
+                    continue
+                pj = 2 * p + j
+                total = s["f"][pj, k, at] + s["fri"][j, k, at] * other[1 - p, j, k]
+                if p == 0:
+                    total += s["fro"][j, k, at] * u[2 + j, k, rows(t, -1)]
+                else:
+                    total += s["fro"][j, k, rows(t, 1)] * u[j, k, rows(t, 1)]
+                beside = other[p, 1 - j, k]
+                total += s["fci"][p, k, at] * beside
+                if j == 0:
+                    total += s["fco"][p, k, at] * pltpu.roll(beside, 1, 1)
+                else:
+                    total += s["fcr"][p, k, at] * pltpu.roll(beside, LANES - 1, 1)
+                if k > 0:
+                    total += s["fl"][pj, k, at] * other[p, j, k - 1]
+                if k < layers - 1:
+                    total += s["fl"][pj, k + 1, at] * other[p, j, k + 1]
+                yield pj, k, total
 
 
 def split_half(s, colour, lo, hi, layers):
     def body(t):
-        for k in range(layers):
-            for p in range(2):
-                for j in range(2):
-                    if (p + j + k) % 2 == colour:
-                        pj = 2 * p + j
-                        total = s["f"][pj, k, rows(t)] + split_sum(s, p, j, k, t, layers)
-                        s["u"][pj, k, rows(t)] = total * s["invd"][pj, k, rows(t)]
+        for pj, k, total in split_block(s, colour, t, layers):
+            s["u"][pj, k, rows(t)] = total * s["invd"][pj, k, rows(t)]
 
     over(lo, hi, MOST["split"], body)
 
@@ -233,30 +240,31 @@
     over(0, (height - 2 * PAD) // 8, MOST["setup"], body)
 
 
-def nat_sum(s, mid, sides, i, k, t, layers):
-    u = s["u"]
-    total = s["wr"][i, k, rows(t)] * u[i, k, rows(t, -1)]
-    total += s["wr"][i, k, rows(t, 1)] * u[i, k, rows(t, 1)]
-    total += s["wc"][i, k, rows(t)] * sides[k][0][i] + s["wcr"][i, k, rows(t)] * sides[k][1][i]
-    if k > 0:
-        total += s["wl"][i, k, rows(t)] * mid[k - 1][i]
-    if k < layers - 1:
-        total += s["wl"][i, k + 1, rows(t)] * mid[k + 1][i]
-    return total
+def nat_block(s, t):
+    u, at = s["u"], rows(t)
+    tiles, layers = u.shape[:2]
+    mid = [[u[i, k, at] for i in range(tiles)] for k in range(layers)]
+    wl = [None] * tiles
+    for k in range(layers):
+        left, right = sides_of(mid[k], s["edge"])
+        for i in range(tiles):
+            total = s["f"][i, k, at] + s["wr"][i, k, at] * u[i, k, rows(t, -1)]
+            total += s["wr"][i, k, rows(t, 1)] * u[i, k, rows(t, 1)]
+            total += s["wc"][i, k, at] * left[i] + s["wcr"][i, k, at] * right[i]
+            if k > 0:
+                total += wl[i] * mid[k - 1][i]
+            if k < layers - 1:
+                wl[i] = s["wl"][i, k + 1, at]
+                total += wl[i] * mid[k + 1][i]
+            yield i, k, total, mid[k][i]
 
 
 def nat_half(s, colour, lo, hi):
-    tiles, layers = s["u"].shape[:2]
-
     def body(t):
         odd = (iota((8 * t[1], LANES), 0) + iota((8 * t[1], LANES), 1)) % 2
-        mid = [[s["u"][i, k, rows(t)] for i in range(tiles)] for k in range(layers)]
-        sides = [sides_of(m, s["edge"]) for m in mid]
-        for k in range(layers):
-            chosen = odd == (colour + k) % 2
-            for i in range(tiles):
-                total = s["f"][i, k, rows(t)] + nat_sum(s, mid, sides, i, k, t, layers)
-                s["u"][i, k, rows(t)] = jnp.where(chosen, total * s["invd"][i, k, rows(t)], mid[k][i])
+        for i, k, total, old in nat_block(s, t):
+            value = total * s["invd"][i, k, rows(t)]
+            s["u"][i, k, rows(t)] = jnp.where(odd == (colour + k) % 2, value, old)
 
     over(lo, hi, MOST["nat"], body)
 
@@ -278,15 +286,9 @@
 
 
 def nat_residual(s, res, lo, hi):
-    tiles, layers = s["u"].shape[:2]
-
     def body(t):
-        mid = [[s["u"][i, k, rows(t)] for i in range(tiles)] for k in range(layers)]
-        sides = [sides_of(m, s["edge"]) for m in mid]
-        for k in range(layers):
-            for i in range(tiles):
-                total = s["f"][i, k, rows(t)] + nat_sum(s, mid, sides, i, k, t, layers)
-                res[i, k, rows(t)] = total - s["diag"][i, k, rows(t)] * mid[k][i]
+        for i, k, total, old in nat_block(s, t):
+            res[i, k, rows(t)] = total - s["diag"][i, k, rows(t)] * old
 
     over(lo, hi, MOST["residual"], body)
 
@@ -489,16 +491,12 @@
         split_half(s, 1, 0, steps, layers)
 
     def remain(t):
-        for k in range(layers):
-            total = None
-            for p in range(2):
-                for j in range(2):
-                    if (p + j + k) % 2 == 0:
-                        pj = 2 * p + j
-                        r = s["f"][pj, k, rows(t)] + split_sum(s, p, j, k, t, layers)
-                        r -= s["diag"][pj, k, rows(t)] * s["u"][pj, k, rows(t)]
-                        total = r if total is None else total + r
-            first["f"][0, k, rows(t)] = total * 0.25
+        sums = {}
+        for pj, k, total in split_block(s, 0, t, layers):
+            r = total - s["diag"][pj, k, rows(t)] * s["u"][pj, k, rows(t)]
+            sums[k] = sums[k] + r if k in sums else r
+            if pj >= 2:
+                first["f"][0, k, rows(t)] = sums[k] * 0.25
 
     over(0, steps, MOST["remain"], remain)
 
@@ -564,61 +562,76 @@
     pack_own(payload, nats[-1], ress[-1], mine >> count, mine >> (count - 1))
 
 
-def conjugate(s):
+def conjugate(s, width):
     tiles, layers, height, _ = s["u"].shape
+    assert tiles == 1
     n = height - 2 * PAD
-    row = iota((n, LANES), 0)
-    spots = [(i, k) for k in range(layers) for i in range(tiles)]
-    body_rows = slice(PAD, PAD + n)
+    fold = max(f for f in range(1, layers + 1) if layers % f == 0 and f * width <= LANES)
+    deep = layers // fold
+    row, lane = iota((n, LANES), 0), iota((n, LANES), 1)
+    here, after = slice(PAD, PAD + n), slice(PAD + 1, PAD + 1 + n)
+
+    def folded(get, keep):
+        out = []
+        for k in range(deep):
+            total = None
+            for g in range(fold):
+                value = get(g * deep + k)
+                if value is None:
+                    continue
+                value = jnp.where(keep, value, 0.0)
+                if g:
+                    value = pltpu.roll(value, g * width, 1)
+                total = value if total is None else total + value
+            out.append(jnp.zeros((n, LANES), F32) if total is None else total)
+        return out
+
+    used = lane < width
+    above = folded(lambda k: s["wr"][0, k, here], used & (row > 0))
+    below = folded(lambda k: s["wr"][0, k, after], used & (row < n - 1))
+    before = folded(lambda k: s["wc"][0, k, here], used & (lane > 0))
+    behind = folded(lambda k: s["wcr"][0, k, here], lane < width - 1)
+    under = folded(lambda k: s["wl"][0, k, here] if k else None, used)
+    over_ = folded(lambda k: s["wl"][0, k + 1, here] if k < layers - 1 else None, used)
+    diag = folded(lambda k: s["diag"][0, k, here], used)
+    inv = folded(lambda k: s["invd"][0, k, here], used)
+    r = folded(lambda k: s["f"][0, k, here], used)
 
     def apply(v):
         out = []
-        for k in range(layers):
-            tiles_of = [v[k * tiles + i] for i in range(tiles)]
-            left, right = sides_of(tiles_of, s["edge"])
-            for i in range(tiles):
-                mid = tiles_of[i]
-                wr = s["wr"][i, k, body_rows]
-                wr_next = s["wr"][i, k, slice(PAD + 1, PAD + 1 + n)]
-                total = wr * jnp.where(row == 0, 0.0, pltpu.roll(mid, 1, 0))
-                total += wr_next * jnp.where(row == n - 1, 0.0, pltpu.roll(mid, n - 1, 0))
-                total += s["wc"][i, k, body_rows] * left[i] + s["wcr"][i, k, body_rows] * right[i]
-                if k > 0:
-                    total += s["wl"][i, k, body_rows] * v[(k - 1) * tiles + i]
-                if k < layers - 1:
-                    total += s["wl"][i, k + 1, body_rows] * v[(k + 1) * tiles + i]
-                out.append(s["diag"][i, k, body_rows] * mid - total)
+        for k in range(deep):
+            total = above[k] * pltpu.roll(v[k], 1, 0) + below[k] * pltpu.roll(v[k], n - 1, 0)
+            total += before[k] * pltpu.roll(v[k], 1, 1) + behind[k] * pltpu.roll(v[k], LANES - 1, 1)
+            lower = v[k - 1] if k else pltpu.roll(v[deep - 1], width, 1)
+            upper = v[k + 1] if k < deep - 1 else pltpu.roll(v[0], LANES - width, 1)
+            out.append(diag[k] * v[k] - (total + under[k] * lower + over_[k] * upper))
         return out
 
     def inner(a, b):
         total = a[0] * b[0]
         for x, y in zip(a[1:], b[1:]):
             total += x * y
-        total = jnp.sum(total, axis=0, keepdims=True)
-        return jnp.sum(total, axis=1, keepdims=True)
-
-    inv = [s["invd"][i, k, body_rows] for i, k in spots]
-    inside = [x > 0.0 for x in inv]
-    r = [jnp.where(inside[m], s["f"][i, k, body_rows], 0.0) for m, (i, k) in enumerate(spots)]
-    z = [x * y for x, y in zip(r, inv)]
-    count = len(spots)
+        return jnp.sum(jnp.sum(total, axis=0, keepdims=True), axis=1, keepdims=True)
 
     def step(_, carry):
-        e, r, p, rz = carry[:count], carry[count : 2 * count], carry[2 * count : 3 * count], carry[-1]
+        e, r, p = carry[:deep], carry[deep : 2 * deep], carry[2 * deep :]
         q = apply(p)
-        alpha = rz / inner(p, q)
+        z = [x * y for x, y in zip(r, inv)]
+        w = [x * y for x, y in zip(q, inv)]
+        rz, pq, zq, wq = inner(r, z), inner(p, q), inner(z, q), inner(w, q)
+        alpha = rz / pq
+        beta = (rz + alpha * (alpha * wq - 2.0 * zq)) / rz
         e = [x + alpha * y for x, y in zip(e, p)]
-        r = [jnp.where(m, x - alpha * y, 0.0) for m, x, y in zip(inside, r, q)]
-        z = [x * s["invd"][i, k, body_rows] for x, (i, k) in zip(r, spots)]
-        fresh = inner(r, z)
-        beta = fresh / rz
-        p = [x + beta * y for x, y in zip(z, p)]
-        return (*e, *r, *p, fresh)
-
-    start = (*[jnp.zeros_like(x) for x in r], *r, *z, inner(r, z))
+        r = [x - alpha * y for x, y in zip(r, q)]
+        p = [x - alpha * y + beta * d for x, y, d in zip(z, w, p)]
+        return (*e, *r, *p)
+
+    start = (*[jnp.zeros((n, LANES), F32)] * deep, *r, *[x * y for x, y in zip(r, inv)])
     out = lax.fori_loop(0, COARSE_ITERS, step, start)
-    for (i, k), value in zip(spots, out[:count]):
-        s["u"][i, k, body_rows] = value
+    for g in range(fold):
+        for k in range(deep):
+            value = pltpu.roll(out[k], LANES - g * width, 1) if g else out[k]
+            s["u"][0, g * deep + k, here] = jnp.where(used, value, 0.0)
 
 
 WHOLE = ("u", "f", "invd", "wr", "wc", "wcr", "wl", "lat", "vert", "stor", "diag")
@@ -658,7 +671,7 @@
             whole[name][:, :, :PAD] = zeros
             whole[name][:, :, height - PAD :] = zeros
 
-    def gather(x, carry):
+    def gather(x):
         at = pl.ds(pl.multiple_of(x * mine, 8) + PAD, mine)
         for i in range(tiles):
             here = [y for y in range(ny) if y * mine // LANES == i]
@@ -677,9 +690,13 @@
                             spot = (base + y * mine) % LANES
                             total = jnp.where((lane >= spot) & (lane < spot + mine), part, total)
                         top[name][i, k, at] = pltpu.roll(total, LANES - base, 1) if base else total
+
+    def gather_some(step, carry):
+        for n in range(4):
+            gather(jnp.minimum(4 * step + n, nx - 1))
         return carry
 
-    lax.fori_loop(0, nx, gather, 0)
+    lax.fori_loop(0, -(-nx // 4), gather_some, 0)
 
     for n, level in enumerate(range(LOCAL, LEVELS)):
         now, below = wholes[n], wholes[n + 1]
@@ -688,7 +705,7 @@
         pairs = [(now[name], below[name]) for name in ("lat", "vert", "stor")]
         restrict_all(pairs + [(ress[n], below["f"])])
     nat_setup(wholes[-1], 0.25**LEVELS)
-    conjugate(wholes[-1])
+    conjugate(wholes[-1], spans[1] * 2 * half >> LEVELS)
     for n in reversed(range(len(wholes) - 1)):
         now, below = wholes[n], wholes[n + 1]
         prolong_into(now, now["u"], lambda o, k: below["u"][o, k, PAD : below["u"].shape[2] - PAD], False)
@@ -821,7 +838,7 @@
         ],
         compiler_params=limit(8),
         name="prep",
-    )(watt, cat, u0, sub)
+    )(*[pltpu.with_memory_space_constraint(x, pltpu.HBM) for x in (watt, cat, u0, sub)])
     a, b = swap(a, "gy", 0), swap(b, "gy", 1)
 
     lines = planes * 4 * hh

time: 88.6 us -> 78.6 us (0.89)
  Pallas kernels: 32 us -> 25.4 us
  local copies, waits for them, and re-layouts: 3.36 us -> 0.03 us
    pallas_call x1, Pallas kernels: 16 us -> 11.6 us  [on_device(): pl.pallas_call(functools.partial(up_kernel, halo=halo, half=half, spans=(...]
    unnamed x14 -> x6, local copies, waits for them, and re-layouts: 3.34 us -> 0.01 us
    pallas_call x1, Pallas kernels: 5.1 us -> 3.74 us  [on_device(): pl.pallas_call(mid_kernel, out_shape=(*kept, packed_shape(layers, height...]
    pallas_call x1, Pallas kernels: 8.41 us -> 7.38 us  [on_device(): pl.pallas_call(functools.partial(down_kernel, halo=halo, half=half, kinds...]
where the time goes in v4:
time: 78.6 us; the launch traced here: 78.4 us
  starting transfers between devices  25.6 us (33%)
  Pallas kernels  25.4 us (32%)
  blocking collectives  18.1 us (23%)
  waiting for transfers between devices  9.13 us (12%)
    ppermute x8, starting transfers between devices, swap(): return lax.ppermute(values, axis, pairs + [(b, a) for a, b in pairs])  25.6 us
    all_to_all x1, blocking collectives, on_device(): gathered = lax.all_to_all(sent, ('gx', 'gy'), 0, 0)  18.1 us
    pallas_call x1, Pallas kernels, on_device(): pl.pallas_call(functools.partial(up_kernel, halo=halo, half=half, spans=(...  11.6 us
    ppermute x8, waiting for transfers between devices, swap(): return lax.ppermute(values, axis, pairs + [(b, a) for a, b in pairs])  9.13 us
    pallas_call x1, Pallas kernels, on_device(): pl.pallas_call(functools.partial(down_kernel, halo=halo, half=half, kinds...  7.38 us
    pallas_call x1, Pallas kernels, on_device(): pl.pallas_call(mid_kernel, out_shape=(*kept, packed_shape(layers, height...  3.74 us
    pallas_call x1, Pallas kernels, on_device(): pl.pallas_call(functools.partial(prep_kernel, halo=halo), out_shape=(shap...  1.78 us
  transfers between devices with their start and end apart: 8, of which 4 were waited for; matrix products, arithmetic and copies ran while one was open for 0% of the time, Pallas kernels for 0%

profile of v4, /device:TPU:0, one launch (start us, length us, event | category | flops | bytes accessed | tf_op | source)
XLA Modules:
  0.0 78.4 jit_solution(15081875849338308116)
XLA Ops:
  0.0 0.0 copy-start.2
  0.0 0.0 copy-start.1
  0.0 0.0 copy-start
  0.0 1.8 %prep.1 = (f32[13,128,128]{2,1,0:T(8,128)S(1)}, f32[13,24,128]{2,1,0:T(8,128)S(1)}, f32[13,24,128]{2,1,0:T(8,128)S(1)}) custom-call(f32[64]{0:T(128)} %watt_hbm.1, s32[8,8]{1,0:T(8,128)} %cat_hbm.1, f32[6,128,128]{2,1,0:T(8,128)} %u_hbm.1, s32[6,128,128]{2,1,0:T(8,128)} %sub_hbm.1), custom_call_target="tpu_custom_call" | custom-call | tf_op jit(solution)/shard_map/prep/pallas_call | solution.py:828
  1.8 3.0 %collective-permute-start = (f32[13,24,128]{2,1,0:T(8,128)S(1)}, f32[13,24,128]{2,1,0:T(8,128)S(1)}, u32[]{:S(2)}, u32[]{:S(2)}) collective-permute-start(f32[13,24,128]{2,1,0:T(8,128)S(1)} %get-tuple-element.44), channel_id=1, source_target_pairs={{0,1},{2,3},{1,0},{3,2},{4,5},{6,7},{5,4},{7,6},{8,9},{10,11},{9,8... | collective-permute-start | bytes 479240 | tf_op jit(solution)/shard_map/ppermute | solution.py:797
  4.8 0.7 collective-permute-start.1
  5.5 3.4 %collective-permute-done.ra = f32[13,24,128]{2,1,0:T(8,128)S(1)} collective-permute-done((f32[13,24,128]{2,1,0:T(8,128)S(1)}, f32[13,24,128]{2,1,0:T(8,128)S(1)}, u32[]{:S(2)}, u32[]{:S(2)}) %collective-permute-start) | collective-permute-done | bytes 159776 | tf_op jit(solution)/shard_map/ppermute | solution.py:797
  8.9 0.0 collective-permute-done.1.rb
  8.9 0.9 %split.1 = (f32[13,4,64,128]{3,2,1,0:T(8,128)S(1)}, f32[624,128]{1,0:T(8,128)S(1)}, f32[624,128]{1,0:T(8,128)S(1)}) custom-call(f32[13,128,128]{2,1,0:T(8,128)S(1)} %get-tuple-element.43.own, f32[13,24,128]{2,1,0:T(8,128)S(1)} %collective-permute-done.ra, f32[13,24,128]{2,1,0:T(8,128)S(1)} %collective-permute-done.1.rb), custom_call_target="tpu_custom_call" | custom-call | tf_op jit(solution)/shard_map/split/pallas_call | solution.py:845
  9.9 0.1 collective-permute-start.2
  9.9 0.7 collective-permute-start.3
  10.6 0.9 %collective-permute-done.2.refs_4_ = f32[624,128]{1,0:T(8,128)S(1)} collective-permute-done((f32[624,128]{1,0:T(8,128)S(1)}, f32[624,128]{1,0:T(8,128)S(1)}, u32[]{:S(2)}, u32[]{:S(2)}) %collective-permute-start.2) | collective-permute-done | bytes 319520 | tf_op jit(solution)/shard_map/ppermute | solution.py:797
  11.5 0.0 collective-permute-done.3.refs_5_
  11.5 0.0 copy-done.2
  11.5 0.0 copy-done.1
  11.5 0.0 copy-done
  11.6 7.4 %down.1 = (f32[4,6,104,128]{3,2,1,0:T(8,128)S(1)}, f32[4,6,104,128]{3,2,1,0:T(8,128)S(1)}, f32[4,6,104,128]{3,2,1,0:T(8,128)S(1)}, f32[2,6,104,128]{3,2,1,0:T(8,...) custom-call(f32[8]{0:T(128)S(1)} %copy-done, ...), custom_call_target="tpu_custom_call" | custom-call | tf_op jit(solution)/shard_map/down/pallas_call | solution.py:866
  18.9 0.7 collective-permute-start.5
  19.6 8.5 %collective-permute-start.4 = (f32[192,128]{1,0:T(8,128)S(1)}, f32[192,128]{1,0:T(8,128)S(1)}, u32[]{:S(2)}, u32[]{:S(2)}) collective-permute-start(f32[192,128]{1,0:T(8,128)S(1)} %get-tuple-element.49.own), channel_id=1, source_target_pairs={{0,1},{2,3},{1,0},{3,2},{4,5},{6,7},{5,4},{7,6},{8,9},{10,11},{9,8... | collective-permute-start | bytes 294920 | tf_op jit(solution)/shard_map/ppermute | solution.py:797
  28.1 0.0 collective-permute-done.5.rb
  28.1 3.6 %collective-permute-done.4.ra = f32[192,128]{1,0:T(8,128)S(1)} collective-permute-done((f32[192,128]{1,0:T(8,128)S(1)}, f32[192,128]{1,0:T(8,128)S(1)}, u32[]{:S(2)}, u32[]{:S(2)}) %collective-permute-start.4) | collective-permute-done | bytes 98336 | tf_op jit(solution)/shard_map/ppermute | solution.py:797
  31.7 0.7 collective-permute-start.7
  32.4 11.3 %collective-permute-start.6 = (f32[3,192,128]{2,1,0:T(8,128)S(1)}, f32[3,192,128]{2,1,0:T(8,128)S(1)}, u32[]{:S(2)}, u32[]{:S(2)}) collective-permute-start(f32[3,192,128]{2,1,0:T(8,128)S(1)} %pad_maximum_fusion), channel_id=1, source_target_pairs={{0,4},{8,12},{16,20},{24,28},{4,0},{12,8},{20,16},{28,24},{1,5},{9... | collective-permute-start | bytes 884744 | tf_op jit(solution)/shard_map/ppermute | solution.py:797
  43.7 0.0 collective-permute-done.7.tb
  43.7 1.2 %collective-permute-done.6.ta = f32[3,192,128]{2,1,0:T(8,128)S(1)} collective-permute-done((f32[3,192,128]{2,1,0:T(8,128)S(1)}, f32[3,192,128]{2,1,0:T(8,128)S(1)}, u32[]{:S(2)}, u32[]{:S(2)}) %collective-permute-start.6) | collective-permute-done | bytes 294944 | tf_op jit(solution)/shard_map/ppermute | solution.py:797
  44.9 3.7 %mid.1 = (f32[1,6,112,128]{3,2,1,0:T(8,128)S(1)}, f32[1,6,112,128]{3,2,1,0:T(8,128)S(1)}, f32[1,6,112,128]{3,2,1,0:T(8,128)S(1)}, f32[1,6,112,128]{3,2,1,0:T(8,1...) custom-call(f32[192,128]{1,0:T(8,128)S(1)} %get-tuple-element.49.own, ...), custom_call_target="tpu_custom_call" | custom-call | tf_op jit(solution)/shard_map/mid/pallas_call | solution.py:887
  48.7 18.1 %all_to_all.5.refs_0_ = f32[32,16,128]{2,1,0:T(8,128)S(1)} all-to-all(f32[32,16,128]{2,1,0:T(8,128)S(1)} %broadcast_in_dim.2), channel_id=1, replica_groups=mesh['gx'=8,'gy'=4] {'gx','gy'}, dimensions={0} | all-to-all | bytes 524288 | tf_op jit(solution)/shard_map/all_to_all | solution.py:900
  66.8 11.6 %up.1 = f32[6,128,128]{2,1,0:T(8,128)} custom-call(f32[32,16,128]{2,1,0:T(8,128)S(1)} %all_to_all.5.refs_0_, f32[4,6,104,128]{3,2,1,0:T(8,128)S(1)} %get-tuple-element.51.refs_1_, f32[4,6,104,128]{3,2,1,0:T(8,128)S(1)} %get-tuple-element.52.refs_2_, f32[4,6,104,128]{3,2,1,0:T(8,128)S(1)} %get-tuple-element.53.refs_3_, ...), custom_call_target="tpu_custom_call" | custom-call | tf_op jit(solution)/shard_map/up/pallas_call | solution.py:910
  (2 shorter events, 0.0 us)
Async XLA Ops:
  0.0 11.5 %copy-start.2 = (f32[8]{0:T(128)S(1)}, f32[8]{0:T(128)}, u32[]{:S(2)}) copy-start(f32[8]{0:T(128)} %refs_2_.1) | copy-start | bytes 100
  0.0 11.5 %copy-start.1 = (f32[8]{0:T(128)S(1)}, f32[8]{0:T(128)}, u32[]{:S(2)}) copy-start(f32[8]{0:T(128)} %refs_1_.1) | copy-start | bytes 100
  0.0 11.5 %copy-start = (f32[8]{0:T(128)S(1)}, f32[8]{0:T(128)}, u32[]{:S(2)}) copy-start(f32[8]{0:T(128)} %refs_0_.1) | copy-start | bytes 100
  1.8 7.1 %collective-permute-start = (f32[13,24,128]{2,1,0:T(8,128)S(1)}, f32[13,24,128]{2,1,0:T(8,128)S(1)}, u32[]{:S(2)}, u32[]{:S(2)}) collective-permute-start(f32[13,24,128]{2,1,0:T(8,128)S(1)} %get-tuple-element.44), channel_id=1, source_target_pairs={{0,1},{2,3},{1,0},{3,2},{4,5},{6,7},{5,4},{7,6},{8,9},{10,11},{9,8... | collective-permute-start | bytes 479240 | tf_op jit(solution)/shard_map/ppermute | solution.py:797
  4.8 4.1 %collective-permute-start.1 = (f32[13,24,128]{2,1,0:T(8,128)S(1)}, f32[13,24,128]{2,1,0:T(8,128)S(1)}, u32[]{:S(2)}, u32[]{:S(2)}) collective-permute-start(f32[13,24,128]{2,1,0:T(8,128)S(1)} %get-tuple-element.45), channel_id=1, source_target_pairs={{1,2},{2,1},{5,6},{6,5},{9,10},{10,9},{13,14},{14,13},{17,18},{18,... | collective-permute-start | bytes 479240 | tf_op jit(solution)/shard_map/ppermute | solution.py:797
  9.9 1.7 %collective-permute-start.2 = (f32[624,128]{1,0:T(8,128)S(1)}, f32[624,128]{1,0:T(8,128)S(1)}, u32[]{:S(2)}, u32[]{:S(2)}) collective-permute-start(f32[624,128]{1,0:T(8,128)S(1)} %get-tuple-element.47), channel_id=1, source_target_pairs={{0,4},{8,12},{16,20},{24,28},{4,0},{12,8},{20,16},{28,24},{1,5},{9... | collective-permute-start | bytes 958472 | tf_op jit(solution)/shard_map/ppermute | solution.py:797
  9.9 1.6 %collective-permute-start.3 = (f32[624,128]{1,0:T(8,128)S(1)}, f32[624,128]{1,0:T(8,128)S(1)}, u32[]{:S(2)}, u32[]{:S(2)}) collective-permute-start(f32[624,128]{1,0:T(8,128)S(1)} %get-tuple-element.48), channel_id=1, source_target_pairs={{4,8},{12,16},{20,24},{8,4},{16,12},{24,20},{5,9},{13,17},{21,25},... | collective-permute-start | bytes 958472 | tf_op jit(solution)/shard_map/ppermute | solution.py:797
  18.9 9.2 %collective-permute-start.5 = (f32[192,128]{1,0:T(8,128)S(1)}, f32[192,128]{1,0:T(8,128)S(1)}, u32[]{:S(2)}, u32[]{:S(2)}) collective-permute-start(f32[192,128]{1,0:T(8,128)S(1)} %get-tuple-element.49.own), channel_id=1, source_target_pairs={{1,2},{2,1},{5,6},{6,5},{9,10},{10,9},{13,14},{14,13},{17,18},{18,... | collective-permute-start | bytes 294920 | tf_op jit(solution)/shard_map/ppermute | solution.py:797
  19.6 12.1 %collective-permute-start.4 = (f32[192,128]{1,0:T(8,128)S(1)}, f32[192,128]{1,0:T(8,128)S(1)}, u32[]{:S(2)}, u32[]{:S(2)}) collective-permute-start(f32[192,128]{1,0:T(8,128)S(1)} %get-tuple-element.49.own), channel_id=1, source_target_pairs={{0,1},{2,3},{1,0},{3,2},{4,5},{6,7},{5,4},{7,6},{8,9},{10,11},{9,8... | collective-permute-start | bytes 294920 | tf_op jit(solution)/shard_map/ppermute | solution.py:797
  31.7 12.0 %collective-permute-start.7 = (f32[3,192,128]{2,1,0:T(8,128)S(1)}, f32[3,192,128]{2,1,0:T(8,128)S(1)}, u32[]{:S(2)}, u32[]{:S(2)}) collective-permute-start(f32[3,192,128]{2,1,0:T(8,128)S(1)} %pad_maximum_fusion), channel_id=1, source_target_pairs={{4,8},{12,16},{20,24},{8,4},{16,12},{24,20},{5,9},{13,17},{21,25},... | collective-permute-start | bytes 884744 | tf_op jit(solution)/shard_map/ppermute | solution.py:797
  32.4 12.5 %collective-permute-start.6 = (f32[3,192,128]{2,1,0:T(8,128)S(1)}, f32[3,192,128]{2,1,0:T(8,128)S(1)}, u32[]{:S(2)}, u32[]{:S(2)}) collective-permute-start(f32[3,192,128]{2,1,0:T(8,128)S(1)} %pad_maximum_fusion), channel_id=1, source_target_pairs={{0,4},{8,12},{16,20},{24,28},{4,0},{12,8},{20,16},{28,24},{1,5},{9... | collective-permute-start | bytes 884744 | tf_op jit(solution)/shard_map/ppermute | solution.py:797

commit v5 on v4

--- a/solution.py
+++ b/solution.py
@@ -192,6 +192,12 @@
     over(lo, hi, MOST["split"], body)
 
 
+def split_sweeps(s, lo, hi, layers):
+    for sweep in range(2):
+        split_half(s, 0, lo, hi, layers)
+        split_half(s, 1, lo, hi, layers)
+
+
 def sides_of(tiles, edge):
     count = len(tiles)
     left = [pltpu.roll(x, 1, 1) for x in tiles]
@@ -320,7 +326,7 @@
             shift = LANES // 2 * i - LANES * o
             if -LANES < shift < LANES:
                 pick = jnp.where(cell + shift == iota((LANES, LANES), 1), 0.25, 0.0)
-                part = pick_dot(parts[i], pick)
+                part = pick_dot(parts[i], pick, 2)
                 total = part if total is None else total + part
         for n, (_, target) in enumerate(pairs):
             for k in range(layers):
@@ -337,7 +343,7 @@
         o = i // 2
         shift = LANES // 2 * (i % 2)
         pick = (cell + shift == iota((LANES, LANES), 0)).astype(F32)
-        every = pick_dot(jnp.concatenate([coarse(o, k)[:tall] for k in range(layers)], 0), pick)
+        every = pick_dot(jnp.concatenate([coarse(o, k)[:tall] for k in range(layers)], 0), pick, 2)
         for k in range(layers):
             wide = every[k * tall : k * tall + n]
             for p in range(2):
@@ -371,7 +377,7 @@
             parts.append(part + ref[0, k, pl.ds(PAD + off + 1, mine, stride=2), :])
     source, target = iota((LANES, LANES), 0), iota((LANES, LANES), 1)
     hit = (source >= off) & ((source - off) // 2 == target) & (target < mine)
-    packed = pick_dot(jnp.concatenate(parts, 0), jnp.where(hit, 0.25, 0.0))
+    packed = pick_dot(jnp.concatenate(parts, 0), jnp.where(hit, 0.25, 0.0), 2)
     for pair in range(-(-layers // per)):
         total = jnp.zeros((mine, LANES), F32)
         for n in range(pair * per * 4, min(layers, (pair + 1) * per) * 4):
@@ -380,55 +386,8 @@
         payload[pair * mine : (pair + 1) * mine] = total
 
 
-def down_kernel(*refs, halo, half, kinds):
-    tables, (sp, ra, rb) = refs[:3], refs[3:6]
-    refs = list(refs[6:])
-    s = dict(zip(SPLIT_KEPT, refs[: len(SPLIT_KEPT)]))
-    refs = refs[len(SPLIT_KEPT) :]
-    nats = []
-    for level in range(1, FIRST):
-        nats.append(dict(zip(NAT_KEPT, refs[: len(NAT_KEPT)]), edge=False))
-        refs = refs[len(NAT_KEPT) :]
-    payload = refs.pop(0)
-    for name in ("lat", "vert", "stor", "diag"):
-        s[name] = refs.pop(0)
-    heat = refs.pop(0)
-    for level in range(1, FIRST):
-        for name in NAT_OTHER:
-            nats[level - 1][name] = refs.pop(0)
-    ress = [refs.pop(0) for level in range(1, FIRST)]
+def look_up(s, first, heat, tables, kinds, lo, hi):
     layers = s["u"].shape[1]
-    height = s["u"].shape[2]
-    hh = halo // 2
-    steps = (height - 2 * PAD) // 8
-    even = lax.axis_index("gx") % 2 == 0
-    zeros = jnp.zeros((PAD, LANES), F32)
-
-    def place(ref, index, q, pj):
-        at = (4 * q + pj) * hh
-        first, second = ra[at : at + hh], rb[at : at + hh]
-        ref[index + (slice(PAD, PAD + hh),)] = jnp.where(even, second, first)
-        ref[index + (slice(PAD + hh, PAD + hh + half),)] = sp[q, pj]
-        ref[index + (slice(PAD + hh + half, PAD + 2 * hh + half),)] = jnp.where(even, first, second)
-
-    for pj in range(4):
-        for k in range(layers):
-            for name in ("u", "lat"):
-                s[name][pj, k, :PAD] = zeros
-                s[name][pj, k, height - PAD :] = zeros
-            place(s["u"], (pj, k), k, pj)
-            place(s["diag"], (pj, k), layers + k, pj)
-        place(heat, (pj,), 2 * layers, pj)
-    for j in range(2):
-        for k in range(layers):
-            s["fro"][j, k, height - PAD :] = zeros
-
-    first = nats[0]
-    clear = [first[name] for name in ("lat", "vert", "stor", "f")] + ress
-    for ref in clear:
-        for k in range(layers):
-            ref[0, k, :PAD] = zeros
-            ref[0, k, ref.shape[2] - PAD :] = zeros
 
     def look(t):
         for k in range(layers):
@@ -450,7 +409,11 @@
             for i, name in enumerate(("lat", "vert", "stor")):
                 first[name][0, k, rows(t)] = sums[i] * 0.25
 
-    over(0, steps, MOST["look"], look)
+    over(lo, hi, MOST["look"], look)
+
+
+def split_setup(s, lo, hi):
+    layers = s["u"].shape[1]
 
     def faces(t):
         at = rows(t)
@@ -485,10 +448,88 @@
                     s["invd"][pj, k, at] = jnp.where(inside, 1.0 / jnp.where(inside, diag, 1.0), 0.0)
                     s["diag"][pj, k, at] = diag
 
-    over(0, steps, MOST["faces"], faces)
-    for sweep in range(2):
-        split_half(s, 0, 0, steps, layers)
-        split_half(s, 1, 0, steps, layers)
+    over(lo, hi, MOST["faces"], faces)
+
+
+SHARED = SPLIT_KEPT + ("lat", "vert", "stor", "diag", "heat", "lat1", "vert1", "stor1")
+
+
+def center_kernel(*refs, halo, half, kinds):
+    tables, sp, out = refs[:3], refs[3], refs[4:]
+    s = dict(zip(SHARED, out))
+    first = {name: s[name + "1"] for name in ("lat", "vert", "stor")}
+    layers, height, hh = s["u"].shape[1], s["u"].shape[2], halo // 2
+    body_rows = slice(PAD + hh, PAD + hh + half)
+    zeros = jnp.zeros((PAD, LANES), F32)
+    for pj in range(4):
+        for k in range(layers):
+            for name in ("u", "lat"):
+                s[name][pj, k, :PAD] = zeros
+                s[name][pj, k, height - PAD :] = zeros
+            s["u"][pj, k, body_rows] = sp[k, pj]
+            s["diag"][pj, k, body_rows] = sp[layers + k, pj]
+        s["heat"][pj, body_rows] = sp[2 * layers, pj]
+    for ref in first.values():
+        for k in range(layers):
+            ref[0, k, :PAD] = zeros
+            ref[0, k, height - PAD :] = zeros
+    look_up(s, first, s["heat"], tables, kinds, *bounds(hh, half, 0))
+    split_setup(s, *bounds(hh, half, 1))
+
+
+def bounds(hh, half, inner):
+    if inner:
+        return -(-(hh + 1) // 8), (hh + half - 1) // 8
+    return hh // 8, -(-(hh + half) // 8)
+
+
+def down_kernel(*refs, halo, half, kinds):
+    tables, (ra, rb) = refs[:3], refs[3:5]
+    refs = list(refs[5 + len(SHARED) :])
+    s = dict(zip(SHARED, refs[: len(SHARED)]))
+    refs = refs[len(SHARED) :]
+    nats = [{} for level in range(1, FIRST)]
+    for n, now in enumerate(nats):
+        now.update(zip(NAT_KEPT, refs[: len(NAT_KEPT)]), edge=False)
+        refs = refs[len(NAT_KEPT) :]
+    payload = refs.pop(0)
+    heat = s["heat"]
+    for n, now in enumerate(nats):
+        for name in NAT_OTHER:
+            now[name] = s[name + "1"] if n == 0 and name != "diag" else refs.pop(0)
+    ress = [refs.pop(0) for level in range(1, FIRST)]
+    layers = s["u"].shape[1]
+    height = s["u"].shape[2]
+    hh = halo // 2
+    steps = (height - 2 * PAD) // 8
+    even = lax.axis_index("gx") % 2 == 0
+    zeros = jnp.zeros((PAD, LANES), F32)
+
+    def place(ref, index, q, pj):
+        at = (4 * q + pj) * hh
+        first, second = ra[at : at + hh], rb[at : at + hh]
+        ref[index + (slice(PAD, PAD + hh),)] = jnp.where(even, second, first)
+        ref[index + (slice(PAD + hh + half, PAD + 2 * hh + half),)] = jnp.where(even, first, second)
+
+    for pj in range(4):
+        for k in range(layers):
+            place(s["u"], (pj, k), k, pj)
+            place(s["diag"], (pj, k), layers + k, pj)
+        place(heat, (pj,), 2 * layers, pj)
+    for j in range(2):
+        for k in range(layers):
+            s["fro"][j, k, height - PAD :] = zeros
+    first = nats[0]
+    for ref in [first["f"]] + ress:
+        for k in range(layers):
+            ref[0, k, :PAD] = zeros
+            ref[0, k, ref.shape[2] - PAD :] = zeros
+    lo, hi = bounds(hh, half, 1)
+    for begin, end in ((0, lo), (hi, steps)):
+        look_up(s, first, heat, tables, kinds, begin, end)
+    for begin, end in ((0, lo), (hi, steps)):
+        split_setup(s, begin, end)
+    split_sweeps(s, 0, steps, layers)
 
     def remain(t):
         sums = {}
@@ -776,9 +817,7 @@
                 now["u"][pj, k, rows(t)] = s["u"][pj, k, rows(t)] + value
 
     over(lo - 1, min(hi + 1, steps), MOST["add"], add)
-    for sweep in range(2):
-        split_half(now, 0, lo, hi, layers)
-        split_half(now, 1, lo, hi, layers)
+    split_sweeps(now, lo, hi, layers)
     source, target = iota((2 * LANES, 2 * half), 0), iota((2 * LANES, 2 * half), 1)
     pick = ((source % LANES == hh + target // 2) & (source // LANES == target % 2)).astype(F32)
     body_rows = slice(PAD + hh, PAD + hh + half)
@@ -855,23 +894,33 @@
 
     tall = up8(half + 2 * hh) + 2 * PAD
     four, two = (4, layers, tall, LANES), (2, layers, tall, LANES)
-    kept = [shape(*(four if name in ("u", "f", "invd", "fl") else two)) for name in SPLIT_KEPT]
     nat_shapes = [
         (1, layers, up8((height + 2 * halo) >> level) + 2 * PAD, LANES) for level in range(1, FIRST)
     ]
+    sizes = [four if name in ("u", "f", "invd", "fl") else two for name in SPLIT_KEPT]
+    sizes += [four] * 4 + [(4, tall, LANES)] + [nat_shapes[0]] * 3
+    shared = pl.pallas_call(
+        functools.partial(center_kernel, halo=halo, half=half, kinds=planar.shape[0]),
+        out_shape=tuple(shape(*d) for d in sizes),
+        in_specs=[SMEM] * 3 + [VMEM],
+        out_specs=(VMEM,) * len(sizes),
+        compiler_params=limit(24),
+        name="center",
+    )(planar, vertical, ratio, sp)
+    kept = []
     for d in nat_shapes:
         kept += [shape(*d)] * len(NAT_KEPT)
-    scratch = [pltpu.VMEM(four, F32)] * 4 + [pltpu.VMEM((4, tall, LANES), F32)]
-    scratch += other_scratch(nat_shapes)
     *saved, block = pl.pallas_call(
         functools.partial(down_kernel, halo=halo, half=half, kinds=planar.shape[0]),
-        out_shape=(*kept, packed_shape(layers, height >> FIRST)),
-        in_specs=[SMEM] * 3 + [VMEM] * 3,
-        out_specs=(VMEM,) * (len(kept) + 1),
-        scratch_shapes=scratch,
-        compiler_params=limit(30),
+        out_shape=(*[shape(*d) for d in sizes], *kept, packed_shape(layers, height >> FIRST)),
+        in_specs=[SMEM] * 3 + [VMEM] * (2 + len(sizes)),
+        out_specs=(VMEM,) * (len(sizes) + len(kept) + 1),
+        scratch_shapes=other_scratch(nat_shapes)[3:],
+        input_output_aliases={5 + n: n for n in range(len(sizes))},
+        compiler_params=limit(26),
         name="down",
-    )(planar, vertical, ratio, sp, a, b)
+    )(planar, vertical, ratio, a, b, *shared)
+    saved = saved[: len(SPLIT_KEPT)] + saved[len(sizes) :]
 
     a, b = swap(block, "gy", 0), swap(block, "gy", 1)
     column = jnp.stack([block, a, b])

time: 78.6 us -> 76 us (0.967)
  starting transfers between devices: 25.6 us -> 23.9 us
  waiting for transfers between devices: 9.13 us -> 8.22 us
    pallas_call x0 -> x1, Pallas kernels: none -> 2.53 us  [on_device(): pl.pallas_call(functools.partial(center_kernel, halo=halo, half=half, kin...]
    pallas_call x1, Pallas kernels: 7.38 us -> 5.42 us  [on_device(): pl.pallas_call(functools.partial(down_kernel, halo=halo, half=half, kinds...]
    ppermute x8, starting transfers between devices: 25.6 us -> 23.9 us  [swap(): return lax.ppermute(values, axis, pairs + [(b, a) for a, b in pairs])]
    ppermute x8, waiting for transfers between devices: 9.13 us -> 8.22 us  [swap(): return lax.ppermute(values, axis, pairs + [(b, a) for a, b in pairs])]
  transfers between devices with their start and end apart: 8 -> 8, of which waited for: 4 -> 3; matrix products, arithmetic and copies ran while one was open for 0% -> 0% of each run, Pallas kernels for 0% -> 3%
where the time goes in v5:
time: 76 us; the launch traced here: 75.8 us
  Pallas kernels  25.4 us (33%)
  starting transfers between devices  23.9 us (31%)
  blocking collectives  18.1 us (24%)
  waiting for transfers between devices  8.22 us (11%)
    ppermute x8, starting transfers between devices, swap(): return lax.ppermute(values, axis, pairs + [(b, a) for a, b in pairs])  23.9 us
    all_to_all x1, blocking collectives, on_device(): gathered = lax.all_to_all(sent, ('gx', 'gy'), 0, 0)  18.1 us
    pallas_call x1, Pallas kernels, on_device(): pl.pallas_call(functools.partial(up_kernel, halo=halo, half=half, spans=(...  11.1 us
    ppermute x8, waiting for transfers between devices, swap(): return lax.ppermute(values, axis, pairs + [(b, a) for a, b in pairs])  8.22 us
    pallas_call x1, Pallas kernels, on_device(): pl.pallas_call(functools.partial(down_kernel, halo=halo, half=half, kinds...  5.42 us
    pallas_call x1, Pallas kernels, on_device(): pl.pallas_call(mid_kernel, out_shape=(*kept, packed_shape(layers, height...  3.63 us
    pallas_call x1, Pallas kernels, on_device(): pl.pallas_call(functools.partial(center_kernel, halo=halo, half=half, kin...  2.53 us
    pallas_call x1, Pallas kernels, on_device(): pl.pallas_call(functools.partial(prep_kernel, halo=halo), out_shape=(shap...  1.78 us
  transfers between devices with their start and end apart: 8, of which 3 were waited for; matrix products, arithmetic and copies ran while one was open for 0% of the time, Pallas kernels for 3%

profile of v5, /device:TPU:0, one launch (start us, length us, event | category | flops | bytes accessed | tf_op | source)
XLA Modules:
  0.0 75.8 jit_solution(3282127780505880316)
XLA Ops:
  0.0 0.0 copy-start.2
  0.0 0.0 copy-start.1
  0.0 0.0 copy-start
  0.0 1.8 %prep.1 = (f32[13,128,128]{2,1,0:T(8,128)S(1)}, f32[13,24,128]{2,1,0:T(8,128)S(1)}, f32[13,24,128]{2,1,0:T(8,128)S(1)}) custom-call(f32[64]{0:T(128)} %watt_hbm.1, s32[8,8]{1,0:T(8,128)} %cat_hbm.1, f32[6,128,128]{2,1,0:T(8,128)} %u_hbm.1, s32[6,128,128]{2,1,0:T(8,128)} %sub_hbm.1), custom_call_target="tpu_custom_call" | custom-call | tf_op jit(solution)/shard_map/prep/pallas_call | solution.py:867
  1.8 3.0 %collective-permute-start = (f32[13,24,128]{2,1,0:T(8,128)S(1)}, f32[13,24,128]{2,1,0:T(8,128)S(1)}, u32[]{:S(2)}, u32[]{:S(2)}) collective-permute-start(f32[13,24,128]{2,1,0:T(8,128)S(1)} %get-tuple-element.61), channel_id=1, source_target_pairs={{0,1},{2,3},{1,0},{3,2},{4,5},{6,7},{5,4},{7,6},{8,9},{10,11},{9,8... | collective-permute-start | bytes 479240 | tf_op jit(solution)/shard_map/ppermute | solution.py:836
  4.8 0.7 collective-permute-start.1
  5.5 3.4 %collective-permute-done.ra = f32[13,24,128]{2,1,0:T(8,128)S(1)} collective-permute-done((f32[13,24,128]{2,1,0:T(8,128)S(1)}, f32[13,24,128]{2,1,0:T(8,128)S(1)}, u32[]{:S(2)}, u32[]{:S(2)}) %collective-permute-start) | collective-permute-done | bytes 159776 | tf_op jit(solution)/shard_map/ppermute | solution.py:836
  8.9 0.0 collective-permute-done.1.rb
  8.9 0.9 %split.1 = (f32[13,4,64,128]{3,2,1,0:T(8,128)S(1)}, f32[624,128]{1,0:T(8,128)S(1)}, f32[624,128]{1,0:T(8,128)S(1)}) custom-call(f32[13,128,128]{2,1,0:T(8,128)S(1)} %get-tuple-element.60.own, f32[13,24,128]{2,1,0:T(8,128)S(1)} %collective-permute-done.ra, f32[13,24,128]{2,1,0:T(8,128)S(1)} %collective-permute-done.1.rb), custom_call_target="tpu_custom_call" | custom-call | tf_op jit(solution)/shard_map/split/pallas_call | solution.py:884
  9.9 0.1 collective-permute-start.2
  9.9 0.7 collective-permute-start.3
  10.6 0.0 copy-done.2
  10.6 0.0 copy-done.1
  10.6 0.0 copy-done
  10.7 2.5 %center.1 = (f32[4,6,104,128]{3,2,1,0:T(8,128)S(1)}, f32[4,6,104,128]{3,2,1,0:T(8,128)S(1)}, f32[4,6,104,128]{3,2,1,0:T(8,128)S(1)}, f32[2,6,104,128]{3,2,1,0:T(...) custom-call(f32[8]{0:T(128)S(1)} %copy-done, ...), custom_call_target="tpu_custom_call" | custom-call | tf_op jit(solution)/shard_map/center/pallas_call | solution.py:902
  13.2 0.0 collective-permute-done.2.refs_3_
  13.2 0.0 collective-permute-done.3.refs_4_
  13.2 5.4 %down.1 = (f32[4,6,104,128]{3,2,1,0:T(8,128)S(1)}, f32[4,6,104,128]{3,2,1,0:T(8,128)S(1)}, f32[4,6,104,128]{3,2,1,0:T(8,128)S(1)}, f32[2,6,104,128]{3,2,1,0:T(8,...) custom-call(f32[8]{0:T(128)S(1)} %copy-done, ...), custom_call_target="tpu_custom_call", output_to_operand_aliasing={{0}: (5, {}), {1}: (6, {}), {2}: (7, {}), {3}: (8, {}), {4}... | custom-call | tf_op jit(solution)/shard_map/down/pallas_call | solution.py:913
  18.6 0.7 collective-permute-start.5
  19.3 8.5 %collective-permute-start.4 = (f32[192,128]{1,0:T(8,128)S(1)}, f32[192,128]{1,0:T(8,128)S(1)}, u32[]{:S(2)}, u32[]{:S(2)}) collective-permute-start(f32[192,128]{1,0:T(8,128)S(1)} %get-tuple-element.83.own), channel_id=1, source_target_pairs={{0,1},{2,3},{1,0},{3,2},{4,5},{6,7},{5,4},{7,6},{8,9},{10,11},{9,8... | collective-permute-start | bytes 294920 | tf_op jit(solution)/shard_map/ppermute | solution.py:836
  27.8 0.0 collective-permute-done.5.rb
  27.8 3.6 %collective-permute-done.4.ra = f32[192,128]{1,0:T(8,128)S(1)} collective-permute-done((f32[192,128]{1,0:T(8,128)S(1)}, f32[192,128]{1,0:T(8,128)S(1)}, u32[]{:S(2)}, u32[]{:S(2)}) %collective-permute-start.4) | collective-permute-done | bytes 98336 | tf_op jit(solution)/shard_map/ppermute | solution.py:836
  31.4 0.7 collective-permute-start.7
  32.1 9.6 %collective-permute-start.6 = (f32[3,192,128]{2,1,0:T(8,128)S(1)}, f32[3,192,128]{2,1,0:T(8,128)S(1)}, u32[]{:S(2)}, u32[]{:S(2)}) collective-permute-start(f32[3,192,128]{2,1,0:T(8,128)S(1)} %pad_maximum_fusion), channel_id=1, source_target_pairs={{0,4},{8,12},{16,20},{24,28},{4,0},{12,8},{20,16},{28,24},{1,5},{9... | collective-permute-start | bytes 884744 | tf_op jit(solution)/shard_map/ppermute | solution.py:836
  41.7 0.0 collective-permute-done.7.tb
  41.7 1.2 %collective-permute-done.6.ta = f32[3,192,128]{2,1,0:T(8,128)S(1)} collective-permute-done((f32[3,192,128]{2,1,0:T(8,128)S(1)}, f32[3,192,128]{2,1,0:T(8,128)S(1)}, u32[]{:S(2)}, u32[]{:S(2)}) %collective-permute-start.6) | collective-permute-done | bytes 294944 | tf_op jit(solution)/shard_map/ppermute | solution.py:836
  42.9 3.6 %mid.1 = (f32[1,6,112,128]{3,2,1,0:T(8,128)S(1)}, f32[1,6,112,128]{3,2,1,0:T(8,128)S(1)}, f32[1,6,112,128]{3,2,1,0:T(8,128)S(1)}, f32[1,6,112,128]{3,2,1,0:T(8,1...) custom-call(f32[192,128]{1,0:T(8,128)S(1)} %get-tuple-element.83.own, ...), custom_call_target="tpu_custom_call" | custom-call | tf_op jit(solution)/shard_map/mid/pallas_call | solution.py:936
  46.6 18.1 %all_to_all.5.refs_0_ = f32[32,16,128]{2,1,0:T(8,128)S(1)} all-to-all(f32[32,16,128]{2,1,0:T(8,128)S(1)} %broadcast_in_dim.2), channel_id=1, replica_groups=mesh['gx'=8,'gy'=4] {'gx','gy'}, dimensions={0} | all-to-all | bytes 524288 | tf_op jit(solution)/shard_map/all_to_all | solution.py:949
  64.7 11.1 %up.1 = f32[6,128,128]{2,1,0:T(8,128)} custom-call(f32[32,16,128]{2,1,0:T(8,128)S(1)} %all_to_all.5.refs_0_, f32[4,6,104,128]{3,2,1,0:T(8,128)S(1)} %get-tuple-element.85.refs_1_, f32[4,6,104,128]{3,2,1,0:T(8,128)S(1)} %get-tuple-element.86.refs_2_, f32[4,6,104,128]{3,2,1,0:T(8,128)S(1)} %get-tuple-element.87.refs_3_, ...), custom_call_target="tpu_custom_call" | custom-call | tf_op jit(solution)/shard_map/up/pallas_call | solution.py:959
  (2 shorter events, 0.1 us)
Async XLA Ops:
  0.0 10.6 %copy-start.2 = (f32[8]{0:T(128)S(1)}, f32[8]{0:T(128)}, u32[]{:S(2)}) copy-start(f32[8]{0:T(128)} %refs_2_.3) | copy-start | bytes 100
  0.0 10.6 %copy-start.1 = (f32[8]{0:T(128)S(1)}, f32[8]{0:T(128)}, u32[]{:S(2)}) copy-start(f32[8]{0:T(128)} %refs_1_.3) | copy-start | bytes 100
  0.0 10.6 %copy-start = (f32[8]{0:T(128)S(1)}, f32[8]{0:T(128)}, u32[]{:S(2)}) copy-start(f32[8]{0:T(128)} %refs_0_.3) | copy-start | bytes 100
  1.8 7.1 %collective-permute-start = (f32[13,24,128]{2,1,0:T(8,128)S(1)}, f32[13,24,128]{2,1,0:T(8,128)S(1)}, u32[]{:S(2)}, u32[]{:S(2)}) collective-permute-start(f32[13,24,128]{2,1,0:T(8,128)S(1)} %get-tuple-element.61), channel_id=1, source_target_pairs={{0,1},{2,3},{1,0},{3,2},{4,5},{6,7},{5,4},{7,6},{8,9},{10,11},{9,8... | collective-permute-start | bytes 479240 | tf_op jit(solution)/shard_map/ppermute | solution.py:836
  4.8 4.1 %collective-permute-start.1 = (f32[13,24,128]{2,1,0:T(8,128)S(1)}, f32[13,24,128]{2,1,0:T(8,128)S(1)}, u32[]{:S(2)}, u32[]{:S(2)}) collective-permute-start(f32[13,24,128]{2,1,0:T(8,128)S(1)} %get-tuple-element.62), channel_id=1, source_target_pairs={{1,2},{2,1},{5,6},{6,5},{9,10},{10,9},{13,14},{14,13},{17,18},{18,... | collective-permute-start | bytes 479240 | tf_op jit(solution)/shard_map/ppermute | solution.py:836
  9.9 3.3 %collective-permute-start.2 = (f32[624,128]{1,0:T(8,128)S(1)}, f32[624,128]{1,0:T(8,128)S(1)}, u32[]{:S(2)}, u32[]{:S(2)}) collective-permute-start(f32[624,128]{1,0:T(8,128)S(1)} %get-tuple-element.63), channel_id=1, source_target_pairs={{0,4},{8,12},{16,20},{24,28},{4,0},{12,8},{20,16},{28,24},{1,5},{9... | collective-permute-start | bytes 958472 | tf_op jit(solution)/shard_map/ppermute | solution.py:836
  9.9 3.3 %collective-permute-start.3 = (f32[624,128]{1,0:T(8,128)S(1)}, f32[624,128]{1,0:T(8,128)S(1)}, u32[]{:S(2)}, u32[]{:S(2)}) collective-permute-start(f32[624,128]{1,0:T(8,128)S(1)} %get-tuple-element.64), channel_id=1, source_target_pairs={{4,8},{12,16},{20,24},{8,4},{16,12},{24,20},{5,9},{13,17},{21,25},... | collective-permute-start | bytes 958472 | tf_op jit(solution)/shard_map/ppermute | solution.py:836
  18.6 9.2 %collective-permute-start.5 = (f32[192,128]{1,0:T(8,128)S(1)}, f32[192,128]{1,0:T(8,128)S(1)}, u32[]{:S(2)}, u32[]{:S(2)}) collective-permute-start(f32[192,128]{1,0:T(8,128)S(1)} %get-tuple-element.83.own), channel_id=1, source_target_pairs={{1,2},{2,1},{5,6},{6,5},{9,10},{10,9},{13,14},{14,13},{17,18},{18,... | collective-permute-start | bytes 294920 | tf_op jit(solution)/shard_map/ppermute | solution.py:836
  19.3 12.1 %collective-permute-start.4 = (f32[192,128]{1,0:T(8,128)S(1)}, f32[192,128]{1,0:T(8,128)S(1)}, u32[]{:S(2)}, u32[]{:S(2)}) collective-permute-start(f32[192,128]{1,0:T(8,128)S(1)} %get-tuple-element.83.own), channel_id=1, source_target_pairs={{0,1},{2,3},{1,0},{3,2},{4,5},{6,7},{5,4},{7,6},{8,9},{10,11},{9,8... | collective-permute-start | bytes 294920 | tf_op jit(solution)/shard_map/ppermute | solution.py:836
  31.4 10.3 %collective-permute-start.7 = (f32[3,192,128]{2,1,0:T(8,128)S(1)}, f32[3,192,128]{2,1,0:T(8,128)S(1)}, u32[]{:S(2)}, u32[]{:S(2)}) collective-permute-start(f32[3,192,128]{2,1,0:T(8,128)S(1)} %pad_maximum_fusion), channel_id=1, source_target_pairs={{4,8},{12,16},{20,24},{8,4},{16,12},{24,20},{5,9},{13,17},{21,25},... | collective-permute-start | bytes 884744 | tf_op jit(solution)/shard_map/ppermute | solution.py:836
  32.1 10.8 %collective-permute-start.6 = (f32[3,192,128]{2,1,0:T(8,128)S(1)}, f32[3,192,128]{2,1,0:T(8,128)S(1)}, u32[]{:S(2)}, u32[]{:S(2)}) collective-permute-start(f32[3,192,128]{2,1,0:T(8,128)S(1)} %pad_maximum_fusion), channel_id=1, source_target_pairs={{0,4},{8,12},{16,20},{24,28},{4,0},{12,8},{20,16},{28,24},{1,5},{9... | collective-permute-start | bytes 884744 | tf_op jit(solution)/shard_map/ppermute | solution.py:836

commit v6 on v5

--- a/solution.py
+++ b/solution.py
@@ -95,8 +95,23 @@
     ]
     for copy in copies:
         copy.start()
-    for copy in copies:
-        copy.wait()
+    even = lax.axis_index("gy") % 2 == 0
+
+    def send(q):
+        turned = planes[q].T
+        low, high = turned[:halo], turned[width - halo :]
+        a_ref[q] = jnp.where(even, high, low)
+        b_ref[q] = jnp.where(even, low, high)
+
+    copies[0].wait()
+    for q in range(layers):
+        send(q)
+    copies[1].wait()
+    for q in range(layers, 2 * layers):
+        planes[q] = (sub_ref[q - layers] + 1).astype(F32)
+        send(q)
+    copies[2].wait()
+    copies[3].wait()
     cat = cat_ref[...]
     power = jnp.zeros(cat.shape, F32)
     for n in range(watt.shape[0]):
@@ -104,14 +119,7 @@
     spread_r = (iota((height, cat.shape[0]), 0) // TILE == iota((height, cat.shape[0]), 1)).astype(F32)
     spread_c = (iota((cat.shape[1], width), 1) // TILE == iota((cat.shape[1], width), 0)).astype(F32)
     planes[2 * layers] = dot(dot(spread_r, power), spread_c)
-    even = lax.axis_index("gy") % 2 == 0
-    for q in range(2 * layers + 1):
-        if layers <= q < 2 * layers:
-            planes[q] = (sub_ref[q - layers] + 1).astype(F32)
-        turned = planes[q].T
-        low, high = turned[:halo], turned[width - halo :]
-        a_ref[q] = jnp.where(even, high, low)
-        b_ref[q] = jnp.where(even, low, high)
+    send(2 * layers)
 
 
 def split_kernel(own, ra, rb, out, a_ref, b_ref, scr, *, halo):
@@ -198,103 +206,120 @@
         split_half(s, 1, lo, hi, layers)
 
 
-def sides_of(tiles, edge):
-    count = len(tiles)
-    left = [pltpu.roll(x, 1, 1) for x in tiles]
-    right = [pltpu.roll(x, LANES - 1, 1) for x in tiles]
-    if count == 1 and not edge:
-        return left, right
-    lane = iota(tiles[0].shape, 1)
-    return (
-        [jnp.where(lane == 0, left[i - 1] if i else 0.0, left[i]) for i in range(count)],
-        [
-            jnp.where(lane == LANES - 1, right[i + 1] if i < count - 1 else 0.0, right[i])
-            for i in range(count)
-        ],
-    )
+def geometry(layers, width):
+    assert width <= LANES
+    fold = max(f for f in range(1, layers + 1) if layers % f == 0 and f * width <= LANES)
+    return fold, width, layers // fold
+
+
+def places(extent, geo):
+    lane = iota(extent, 1)
+    group = jnp.zeros(extent, jnp.int32)
+    for g in range(1, geo[0] + 1):
+        if g * geo[1] < LANES:
+            group = group + (lane >= g * geo[1]).astype(jnp.int32)
+    return group, lane - group * geo[1]
+
+
+def odd_cells(t, geo):
+    extent = (8 * t[1], LANES)
+    group, col = places(extent, geo)
+    return (iota(extent, 0) + col + group * geo[2]) % 2
 
 
 def nat_setup(s, factor):
-    tiles, layers, height, _ = s["lat"].shape
+    fold, width, deep = s["geo"]
+    height = s["lat"].shape[1]
     c = 0.5 * factor
 
     def body(t):
-        for k in range(layers):
-            lat = [s["lat"][i, k, rows(t)] for i in range(tiles)]
-            left, right = sides_of(lat, s["edge"])
-            for i in range(tiles):
-                stor = s["stor"][i, k, rows(t)]
-                above = c * (lat[i] + s["lat"][i, k, rows(t, -1)])
-                below = c * (lat[i] + s["lat"][i, k, rows(t, 1)])
-                before, after = c * (lat[i] + left[i]), c * (lat[i] + right[i])
-                diag = stor + above + below + before + after
-                vert = s["vert"][i, k, rows(t)]
-                if k > 0:
-                    face = 0.5 * (vert + s["vert"][i, k - 1, rows(t)])
-                    s["wl"][i, k, rows(t)] = face
-                    diag += face
-                if k < layers - 1:
-                    diag += 0.5 * (vert + s["vert"][i, k + 1, rows(t)])
-                inside = stor > 0.0
-                s["wr"][i, k, rows(t)] = above
-                s["wc"][i, k, rows(t)] = before
-                s["wcr"][i, k, rows(t)] = after
-                s["diag"][i, k, rows(t)] = diag
-                s["invd"][i, k, rows(t)] = jnp.where(inside, 1.0 / jnp.where(inside, diag, 1.0), 0.0)
-
-    s["wr"][:, :, height - PAD :] = jnp.zeros((tiles, layers, PAD, LANES), F32)
+        at = rows(t)
+        group, col = places((8 * t[1], LANES), s["geo"])
+        first, last = col == 0, col == width - 1
+        between = None
+        for k in range(deep):
+            lat, stor, vert = s["lat"][k, at], s["stor"][k, at], s["vert"][k, at]
+            above = c * (lat + s["lat"][k, rows(t, -1)])
+            below = c * (lat + s["lat"][k, rows(t, 1)])
+            before = c * (lat + jnp.where(first, 0.0, pltpu.roll(lat, 1, 1)))
+            after = c * (lat + jnp.where(last, 0.0, pltpu.roll(lat, LANES - 1, 1)))
+            diag = stor + above + below + before + after
+            if k > 0:
+                face = 0.5 * (vert + s["vert"][k - 1, at])
+                s["wl"][k, at] = face
+                diag += face
+            elif fold > 1:
+                between = 0.5 * (vert + pltpu.roll(s["vert"][deep - 1, at], width, 1))
+                between = jnp.where((group > 0) & (group < fold), between, 0.0)
+                s["wl"][0, at] = between
+                diag += between
+            if k < deep - 1:
+                diag += 0.5 * (vert + s["vert"][k + 1, at])
+            elif fold > 1:
+                diag += pltpu.roll(between, LANES - width, 1)
+            inside = stor > 0.0
+            s["wr"][k, at] = above
+            s["wc"][k, at] = jnp.where(first, 0.0, before)
+            s["wcr"][k, at] = jnp.where(last, 0.0, after)
+            s["diag"][k, at] = diag
+            s["invd"][k, at] = jnp.where(inside, 1.0 / jnp.where(inside, diag, 1.0), 0.0)
+
+    s["wr"][:, height - PAD :] = jnp.zeros((deep, PAD, LANES), F32)
     over(0, (height - 2 * PAD) // 8, MOST["setup"], body)
 
 
 def nat_block(s, t):
     u, at = s["u"], rows(t)
-    tiles, layers = u.shape[:2]
-    mid = [[u[i, k, at] for i in range(tiles)] for k in range(layers)]
-    wl = [None] * tiles
-    for k in range(layers):
-        left, right = sides_of(mid[k], s["edge"])
-        for i in range(tiles):
-            total = s["f"][i, k, at] + s["wr"][i, k, at] * u[i, k, rows(t, -1)]
-            total += s["wr"][i, k, rows(t, 1)] * u[i, k, rows(t, 1)]
-            total += s["wc"][i, k, at] * left[i] + s["wcr"][i, k, at] * right[i]
-            if k > 0:
-                total += wl[i] * mid[k - 1][i]
-            if k < layers - 1:
-                wl[i] = s["wl"][i, k + 1, at]
-                total += wl[i] * mid[k + 1][i]
-            yield i, k, total, mid[k][i]
+    fold, width, deep = s["geo"]
+    mid = [u[k, at] for k in range(deep)]
+    wl = s["wl"][0, at] if fold > 1 else None
+    between = None if wl is None else pltpu.roll(wl * mid[0], LANES - width, 1)
+    for k in range(deep):
+        total = s["f"][k, at] + s["wr"][k, at] * u[k, rows(t, -1)]
+        total += s["wr"][k, rows(t, 1)] * u[k, rows(t, 1)]
+        beside = s["wc"][k, at] * pltpu.roll(mid[k], 1, 1)
+        beside += s["wcr"][k, at] * pltpu.roll(mid[k], LANES - 1, 1)
+        if k > 0:
+            total += wl * mid[k - 1]
+        elif fold > 1:
+            total += wl * pltpu.roll(mid[deep - 1], width, 1)
+        if k < deep - 1:
+            wl = s["wl"][k + 1, at]
+            total += wl * mid[k + 1]
+        elif fold > 1:
+            total += between
+        yield k, total + beside, mid[k]
 
 
 def nat_half(s, colour, lo, hi):
     def body(t):
-        odd = (iota((8 * t[1], LANES), 0) + iota((8 * t[1], LANES), 1)) % 2
-        for i, k, total, old in nat_block(s, t):
-            value = total * s["invd"][i, k, rows(t)]
-            s["u"][i, k, rows(t)] = jnp.where(odd == (colour + k) % 2, value, old)
+        odd = odd_cells(t, s["geo"])
+        for k, total, old in nat_block(s, t):
+            value = total * s["invd"][k, rows(t)]
+            s["u"][k, rows(t)] = jnp.where(odd == (colour + k) % 2, value, old)
 
     over(lo, hi, MOST["nat"], body)
 
 
 def nat_first(s, lo, hi):
-    tiles, layers, height, _ = s["u"].shape
-    zeros = jnp.zeros((tiles, layers, PAD, LANES), F32)
-    s["u"][:, :, :PAD] = zeros
-    s["u"][:, :, height - PAD :] = zeros
+    deep, height, _ = s["u"].shape
+    zeros = jnp.zeros((deep, PAD, LANES), F32)
+    s["u"][:, :PAD] = zeros
+    s["u"][:, height - PAD :] = zeros
 
     def body(t):
-        odd = (iota((8 * t[1], LANES), 0) + iota((8 * t[1], LANES), 1)) % 2
-        for k in range(layers):
-            for i in range(tiles):
-                value = s["f"][i, k, rows(t)] * s["invd"][i, k, rows(t)]
-                s["u"][i, k, rows(t)] = jnp.where(odd == k % 2, value, 0.0)
+        odd = odd_cells(t, s["geo"])
+        for k in range(deep):
+            value = s["f"][k, rows(t)] * s["invd"][k, rows(t)]
+            s["u"][k, rows(t)] = jnp.where(odd == k % 2, value, 0.0)
 
     over(lo, hi, MOST["first"], body)
 
 
 def nat_residual(s, res, lo, hi):
     def body(t):
-        for i, k, total, old in nat_block(s, t):
-            res[i, k, rows(t)] = total - s["diag"][i, k, rows(t)] * old
+        for k, total, old in nat_block(s, t):
+            res[k, rows(t)] = total - s["diag"][k, rows(t)] * old
 
     over(lo, hi, MOST["residual"], body)
 
@@ -306,52 +331,71 @@
     nat_residual(s, res, 0, steps)
 
 
-def restrict_all(pairs):
-    tiles, layers = pairs[0][0].shape[:2]
-    count, height = pairs[0][1].shape[0], pairs[0][1].shape[2] - 2 * PAD
-    zeros = jnp.zeros((count, layers, PAD, LANES), F32)
-    parts = [[] for i in range(tiles)]
-    for source, target in pairs:
-        target[:, :, :PAD] = zeros
-        target[:, :, PAD + height :] = zeros
-        for k in range(layers):
-            for i in range(tiles):
-                part = source[i, k, pl.ds(PAD, height, stride=2), :]
-                parts[i].append(part + source[i, k, pl.ds(PAD + 1, height, stride=2), :])
-    parts = [jnp.concatenate(p, 0) for p in parts]
-    cell = iota((LANES, LANES), 0) // 2
-    for o in range(count):
-        total = None
-        for i in range(tiles):
-            shift = LANES // 2 * i - LANES * o
-            if -LANES < shift < LANES:
-                pick = jnp.where(cell + shift == iota((LANES, LANES), 1), 0.25, 0.0)
-                part = pick_dot(parts[i], pick, 2)
-                total = part if total is None else total + part
-        for n, (_, target) in enumerate(pairs):
-            for k in range(layers):
-                at = (n * layers + k) * height
-                target[o, k, PAD : PAD + height] = total[at : at + height]
-
-
-def prolong_into(s, u_in, coarse, mask):
-    tiles, layers, height, _ = s["u"].shape
+def move(parts, a, b, relation, scale):
+    jobs = {}
+    for ka in range(a[2]):
+        for kb in range(b[2]):
+            key = tuple(
+                (ga, gb)
+                for ga in range(a[0])
+                for gb in range(b[0])
+                if ga * a[2] + ka == gb * b[2] + kb
+            )
+            if key:
+                jobs.setdefault(key, []).append((ka, kb))
+    c, m = iota((LANES, LANES), 0), iota((LANES, LANES), 1)
+    out = [None] * b[2]
+    count = parts[0].shape[0]
+    for key, members in jobs.items():
+        hit = None
+        for ga, gb in key:
+            ca, mb = c - ga * a[1], m - gb * b[1]
+            here = (ca >= 0) & (ca < a[1]) & (mb >= 0) & (mb < b[1]) & relation(ca, mb)
+            hit = here if hit is None else hit | here
+        moved = pick_dot(
+            jnp.concatenate([parts[ka] for ka, _ in members], 0), jnp.where(hit, scale, 0.0), 2
+        )
+        for n, (_, kb) in enumerate(members):
+            part = moved[n * count : (n + 1) * count]
+            out[kb] = part if out[kb] is None else out[kb] + part
+    return out
+
+
+def pair_rows(ref, k, start, count):
+    part = ref[k, pl.ds(start, count, stride=2), :]
+    return part + ref[k, pl.ds(start + 1, count, stride=2), :]
+
+
+def restrict_all(pairs, a, b):
+    deep, height = pairs[0][1].shape[0], pairs[0][1].shape[1] - 2 * PAD
+    zeros = jnp.zeros((deep, PAD, LANES), F32)
+    for _, target in pairs:
+        target[:, :PAD] = zeros
+        target[:, PAD + height :] = zeros
+    parts = [
+        jnp.concatenate([pair_rows(source, k, PAD, height) for source, _ in pairs], 0)
+        for k in range(a[2])
+    ]
+    out = move(parts, a, b, lambda c, m: c // 2 == m, 0.25)
+    for n, (_, target) in enumerate(pairs):
+        for k in range(deep):
+            target[k, PAD : PAD + height] = out[k][n * height : (n + 1) * height]
+
+
+def prolong_into(s, u_in, coarse, geo, mask):
+    deep, height, _ = s["u"].shape
     n = (height - 2 * PAD) // 2
     tall = up8(n)
-    cell = iota((LANES, LANES), 1) // 2
-    for i in range(tiles):
-        o = i // 2
-        shift = LANES // 2 * (i % 2)
-        pick = (cell + shift == iota((LANES, LANES), 0)).astype(F32)
-        every = pick_dot(jnp.concatenate([coarse(o, k)[:tall] for k in range(layers)], 0), pick, 2)
-        for k in range(layers):
-            wide = every[k * tall : k * tall + n]
-            for p in range(2):
-                at = pl.ds(PAD + p, n, stride=2)
-                add = wide
-                if mask:
-                    add = jnp.where(s["invd"][i, k, at, :] > 0.0, wide, 0.0)
-                s["u"][i, k, at, :] = u_in[i, k, at, :] + add
+    parts = [coarse(k)[:tall] for k in range(geo[2])]
+    out = move(parts, geo, s["geo"], lambda c, m: c == m // 2, 1.0)
+    for k in range(deep):
+        wide = out[k][:n]
+        for p in range(2):
+            at = pl.ds(PAD + p, n, stride=2)
+            add = wide
+            if mask:
+                add = jnp.where(s["invd"][k, at, :] > 0.0, wide, 0.0)
+            s["u"][k, at, :] = u_in[k, at, :] + add
 
 
 def nat_up(s, lo, hi):
@@ -365,25 +409,24 @@
 NAT_OTHER = ("lat", "vert", "stor", "diag")
 
 
-def pack_own(payload, last, res, mine, off):
-    layers = res.shape[1]
+def pack_own(payload, last, res, layers, mine, off):
     group = 4 * mine
     per = LANES // group
     quantities = (res, last["lat"], last["vert"], last["stor"])
-    parts = []
-    for k in range(layers):
-        for ref in quantities:
-            part = ref[0, k, pl.ds(PAD + off, mine, stride=2), :]
-            parts.append(part + ref[0, k, pl.ds(PAD + off + 1, mine, stride=2), :])
-    source, target = iota((LANES, LANES), 0), iota((LANES, LANES), 1)
-    hit = (source >= off) & ((source - off) // 2 == target) & (target < mine)
-    packed = pick_dot(jnp.concatenate(parts, 0), jnp.where(hit, 0.25, 0.0), 2)
-    for pair in range(-(-layers // per)):
+    parts = [
+        jnp.concatenate([pair_rows(ref, k, PAD + off, mine) for ref in quantities], 0)
+        for k in range(last["geo"][2])
+    ]
+    packed = move(
+        parts, last["geo"], (1, mine, layers), lambda c, m: (c >= off) & ((c - off) // 2 == m), 0.25
+    )
+    for wide in range(-(-layers // per)):
         total = jnp.zeros((mine, LANES), F32)
-        for n in range(pair * per * 4, min(layers, (pair + 1) * per) * 4):
-            part, base = packed[n * mine : (n + 1) * mine], (n - pair * per * 4) * mine
+        for n in range(wide * per * 4, min(layers, (wide + 1) * per) * 4):
+            part = packed[n // 4][n % 4 * mine : (n % 4 + 1) * mine]
+            base = (n - wide * per * 4) * mine
             total += pltpu.roll(part, base, 1) if base else part
-        payload[pair * mine : (pair + 1) * mine] = total
+        payload[wide * mine : (wide + 1) * mine] = total
 
 
 def look_up(s, first, heat, tables, kinds, lo, hi):
@@ -407,7 +450,7 @@
                     f = f + heat[pj, rows(t)]
                 s["f"][at] = f
             for i, name in enumerate(("lat", "vert", "stor")):
-                first[name][0, k, rows(t)] = sums[i] * 0.25
+                first[name][k, rows(t)] = sums[i] * 0.25
 
     over(lo, hi, MOST["look"], look)
 
@@ -471,8 +514,8 @@
         s["heat"][pj, body_rows] = sp[2 * layers, pj]
     for ref in first.values():
         for k in range(layers):
-            ref[0, k, :PAD] = zeros
-            ref[0, k, height - PAD :] = zeros
+            ref[k, :PAD] = zeros
+            ref[k, height - PAD :] = zeros
     look_up(s, first, s["heat"], tables, kinds, *bounds(hh, half, 0))
     split_setup(s, *bounds(hh, half, 1))
 
@@ -483,14 +526,14 @@
     return hh // 8, -(-(hh + half) // 8)
 
 
-def down_kernel(*refs, halo, half, kinds):
+def down_kernel(*refs, halo, half, kinds, geos):
     tables, (ra, rb) = refs[:3], refs[3:5]
     refs = list(refs[5 + len(SHARED) :])
     s = dict(zip(SHARED, refs[: len(SHARED)]))
     refs = refs[len(SHARED) :]
     nats = [{} for level in range(1, FIRST)]
     for n, now in enumerate(nats):
-        now.update(zip(NAT_KEPT, refs[: len(NAT_KEPT)]), edge=False)
+        now.update(zip(NAT_KEPT, refs[: len(NAT_KEPT)]), geo=geos[n])
         refs = refs[len(NAT_KEPT) :]
     payload = refs.pop(0)
     heat = s["heat"]
@@ -521,9 +564,9 @@
             s["fro"][j, k, height - PAD :] = zeros
     first = nats[0]
     for ref in [first["f"]] + ress:
-        for k in range(layers):
-            ref[0, k, :PAD] = zeros
-            ref[0, k, ref.shape[2] - PAD :] = zeros
+        for k in range(ref.shape[0]):
+            ref[k, :PAD] = zeros
+            ref[k, ref.shape[1] - PAD :] = zeros
     lo, hi = bounds(hh, half, 1)
     for begin, end in ((0, lo), (hi, steps)):
         look_up(s, first, heat, tables, kinds, begin, end)
@@ -537,53 +580,51 @@
             r = total - s["diag"][pj, k, rows(t)] * s["u"][pj, k, rows(t)]
             sums[k] = sums[k] + r if k in sums else r
             if pj >= 2:
-                first["f"][0, k, rows(t)] = sums[k] * 0.25
+                first["f"][k, rows(t)] = sums[k] * 0.25
 
     over(0, steps, MOST["remain"], remain)
 
     for level in range(1, FIRST):
         now = nats[level - 1]
         nat_setup(now, 0.25**level)
-        count = (now["u"].shape[2] - 2 * PAD) // 8
+        count = (now["u"].shape[1] - 2 * PAD) // 8
         nat_down(now, ress[level - 1], count)
         if level < FIRST - 1:
             below = nats[level]
             pairs = [(now[name], below[name]) for name in ("lat", "vert", "stor")]
-            restrict_all(pairs + [(ress[level - 1], below["f"])])
-
-    pack_own(payload, nats[-1], ress[-1], 2 * half >> FIRST, halo >> (FIRST - 1))
-
-
-def mid_kernel(own, ra, rb, ta, tb, *refs):
+            restrict_all(pairs + [(ress[level - 1], below["f"])], now["geo"], below["geo"])
+
+    pack_own(payload, nats[-1], ress[-1], layers, 2 * half >> FIRST, halo >> (FIRST - 1))
+
+
+def mid_kernel(own, ra, rb, ta, tb, *refs, geos):
     refs = list(refs)
     count = LOCAL - FIRST
     nats = []
     for n in range(count):
-        nats.append(dict(zip(NAT_KEPT, refs[: len(NAT_KEPT)]), edge=False))
+        nats.append(dict(zip(NAT_KEPT, refs[: len(NAT_KEPT)]), geo=geos[n]))
         refs = refs[len(NAT_KEPT) :]
     payload = refs.pop(0)
     for n in range(count):
         for name in NAT_OTHER:
             nats[n][name] = refs.pop(0)
     ress = refs
-    layers = nats[0]["u"].shape[1]
+    layers = geos[0][0] * geos[0][2]
     mine = own.shape[0] // layers
+    assert geos[0][0] == 1
     even_y, even_x = lax.axis_index("gy") % 2 == 0, lax.axis_index("gx") % 2 == 0
     zeros = jnp.zeros((PAD, LANES), F32)
     for now, res in zip(nats, ress):
         for ref in [now[name] for name in ("lat", "vert", "stor", "f")] + [res]:
-            for k in range(layers):
-                ref[0, k, :PAD] = zeros
-                ref[0, k, ref.shape[2] - PAD :] = zeros
+            for k in range(ref.shape[0]):
+                ref[k, :PAD] = zeros
+                ref[k, ref.shape[1] - PAD :] = zeros
     group = iota((mine, LANES), 1) // mine
-    for v in range(3):
+
+    def assemble(v, middle_of, a_of, b_of):
         for k in range(layers):
             lines = slice(k * mine, (k + 1) * mine)
-            if v == 1:
-                middle, a, b = own[lines], ra[lines], rb[lines]
-            else:
-                first, second = (tb, ta) if v == 0 else (ta, tb)
-                middle, a, b = [jnp.where(even_x, first[n, lines], second[n, lines]) for n in range(3)]
+            middle, a, b = middle_of(lines), a_of(lines), b_of(lines)
             left, right = jnp.where(even_y, b, a), jnp.where(even_y, a, b)
             middle, right = pltpu.roll(middle, mine, 1), pltpu.roll(right, 2 * mine, 1)
             for n, name in enumerate(("f", "lat", "vert", "stor")):
@@ -592,60 +633,55 @@
                 value = jnp.where(group == (n + 3) % 4, 0.0, value)
                 if n:
                     value = pltpu.roll(value, LANES - n * mine, 1)
-                nats[0][name][0, k, PAD + v * mine : PAD + (v + 1) * mine] = value
+                nats[0][name][k, PAD + v * mine : PAD + (v + 1) * mine] = value
+
+    def rows_from(ref):
+        return [lambda lines, n=n: ref[n, lines] for n in range(3)]
+
+    def outer(above, below):
+        assemble(0, *rows_from(above))
+        assemble(2, *rows_from(below))
+
+    assemble(1, *[lambda lines, ref=ref: ref[lines] for ref in (own, ra, rb)])
+    pl.when(even_x)(lambda: outer(tb, ta))
+    pl.when(jnp.logical_not(even_x))(lambda: outer(ta, tb))
     for n, level in enumerate(range(FIRST, LOCAL)):
         now = nats[n]
         nat_setup(now, 0.25**level)
-        nat_down(now, ress[n], (now["u"].shape[2] - 2 * PAD) // 8)
+        nat_down(now, ress[n], (now["u"].shape[1] - 2 * PAD) // 8)
         if n < count - 1:
             pairs = [(now[name], nats[n + 1][name]) for name in ("lat", "vert", "stor")]
-            restrict_all(pairs + [(ress[n], nats[n + 1]["f"])])
-    pack_own(payload, nats[-1], ress[-1], mine >> count, mine >> (count - 1))
-
-
-def conjugate(s, width):
-    tiles, layers, height, _ = s["u"].shape
-    assert tiles == 1
-    n = height - 2 * PAD
-    fold = max(f for f in range(1, layers + 1) if layers % f == 0 and f * width <= LANES)
-    deep = layers // fold
-    row, lane = iota((n, LANES), 0), iota((n, LANES), 1)
+            restrict_all(pairs + [(ress[n], nats[n + 1]["f"])], geos[n], geos[n + 1])
+    pack_own(payload, nats[-1], ress[-1], layers, mine >> count, mine >> (count - 1))
+
+
+def conjugate(s):
+    fold, width, deep = s["geo"]
+    n = s["u"].shape[1] - 2 * PAD
     here, after = slice(PAD, PAD + n), slice(PAD + 1, PAD + 1 + n)
-
-    def folded(get, keep):
-        out = []
-        for k in range(deep):
-            total = None
-            for g in range(fold):
-                value = get(g * deep + k)
-                if value is None:
-                    continue
-                value = jnp.where(keep, value, 0.0)
-                if g:
-                    value = pltpu.roll(value, g * width, 1)
-                total = value if total is None else total + value
-            out.append(jnp.zeros((n, LANES), F32) if total is None else total)
-        return out
-
-    used = lane < width
-    above = folded(lambda k: s["wr"][0, k, here], used & (row > 0))
-    below = folded(lambda k: s["wr"][0, k, after], used & (row < n - 1))
-    before = folded(lambda k: s["wc"][0, k, here], used & (lane > 0))
-    behind = folded(lambda k: s["wcr"][0, k, here], lane < width - 1)
-    under = folded(lambda k: s["wl"][0, k, here] if k else None, used)
-    over_ = folded(lambda k: s["wl"][0, k + 1, here] if k < layers - 1 else None, used)
-    diag = folded(lambda k: s["diag"][0, k, here], used)
-    inv = folded(lambda k: s["invd"][0, k, here], used)
-    r = folded(lambda k: s["f"][0, k, here], used)
+    row = iota((n, LANES), 0)
+    planes = range(deep)
+    above = [jnp.where(row > 0, s["wr"][k, here], 0.0) for k in planes]
+    below = [jnp.where(row < n - 1, s["wr"][k, after], 0.0) for k in planes]
+    before, behind, diag, inv, r = [
+        [s[name][k, here] for k in planes] for name in ("wc", "wcr", "diag", "invd", "f")
+    ]
+    faces = [s["wl"][k, here] if k or fold > 1 else None for k in planes]
 
     def apply(v):
         out = []
-        for k in range(deep):
+        for k in planes:
             total = above[k] * pltpu.roll(v[k], 1, 0) + below[k] * pltpu.roll(v[k], n - 1, 0)
             total += before[k] * pltpu.roll(v[k], 1, 1) + behind[k] * pltpu.roll(v[k], LANES - 1, 1)
-            lower = v[k - 1] if k else pltpu.roll(v[deep - 1], width, 1)
-            upper = v[k + 1] if k < deep - 1 else pltpu.roll(v[0], LANES - width, 1)
-            out.append(diag[k] * v[k] - (total + under[k] * lower + over_[k] * upper))
+            if k > 0:
+                total += faces[k] * v[k - 1]
+            elif fold > 1:
+                total += faces[0] * pltpu.roll(v[deep - 1], width, 1)
+            if k < deep - 1:
+                total += faces[k + 1] * v[k + 1]
+            elif fold > 1:
+                total += pltpu.roll(faces[0] * v[0], LANES - width, 1)
+            out.append(diag[k] * v[k] - total)
         return out
 
     def inner(a, b):
@@ -669,29 +705,26 @@
 
     start = (*[jnp.zeros((n, LANES), F32)] * deep, *r, *[x * y for x, y in zip(r, inv)])
     out = lax.fori_loop(0, COARSE_ITERS, step, start)
-    for g in range(fold):
-        for k in range(deep):
-            value = pltpu.roll(out[k], LANES - g * width, 1) if g else out[k]
-            s["u"][0, g * deep + k, here] = jnp.where(used, value, 0.0)
+    for k in planes:
+        s["u"][k, here] = out[k]
 
 
 WHOLE = ("u", "f", "invd", "wr", "wc", "wcr", "wl", "lat", "vert", "stor", "diag")
 
 
-def up_kernel(*refs, halo, half, spans):
+def up_kernel(*refs, halo, half, spans, geos, whole_geos):
     refs = list(refs)
     gathered = refs.pop(0)
     s = dict(zip(SPLIT_KEPT, refs[: len(SPLIT_KEPT)]))
     refs = refs[len(SPLIT_KEPT) :]
     nats = []
-    for level in range(1, LOCAL):
-        nats.append(dict(zip(NAT_KEPT, refs[: len(NAT_KEPT)]), edge=False))
+    for geo in geos:
+        nats.append(dict(zip(NAT_KEPT, refs[: len(NAT_KEPT)]), geo=geo))
         refs = refs[len(NAT_KEPT) :]
     out = refs.pop(0)
     wholes = []
-    for level in range(LOCAL, LEVELS + 1):
-        edge = (spans[1] * 2 * half >> level) % LANES == 0
-        wholes.append(dict(zip(WHOLE, refs[: len(WHOLE)]), edge=edge))
+    for geo in whole_geos:
+        wholes.append(dict(zip(WHOLE, refs[: len(WHOLE)]), geo=geo))
         refs = refs[len(WHOLE) :]
     ress = [refs.pop(0) for level in range(LOCAL, LEVELS)]
     fresh = [refs.pop(0) for level in range(LOCAL)]
@@ -699,38 +732,41 @@
     nx, ny = spans
     layers = s["u"].shape[1]
     top = wholes[0]
-    tiles, _, tall, _ = top["u"].shape
+    fold, width, deep = top["geo"]
     mine = 2 * half >> LOCAL
     group = 4 * mine
     per = LANES // group
     lane = iota((mine, LANES), 1)
 
     for whole in wholes:
-        count, _, height, _ = whole["u"].shape
+        planes, height, _ = whole["u"].shape
         for name in ("u", "lat"):
-            zeros = jnp.zeros((count, layers, PAD, LANES), F32)
-            whole[name][:, :, :PAD] = zeros
-            whole[name][:, :, height - PAD :] = zeros
+            zeros = jnp.zeros((planes, PAD, LANES), F32)
+            whole[name][:, :PAD] = zeros
+            whole[name][:, height - PAD :] = zeros
 
     def gather(x):
         at = pl.ds(pl.multiple_of(x * mine, 8) + PAD, mine)
-        for i in range(tiles):
-            here = [y for y in range(ny) if y * mine // LANES == i]
-            for wide in range(-(-layers // per)):
-                lines = slice(wide * mine, (wide + 1) * mine)
-                parts = []
-                for y in here:
-                    part = gathered[x * ny + y, lines]
-                    to = y * mine % LANES
-                    parts.append(pltpu.roll(part, to, 1) if to else part)
-                for k in range(wide * per, min(layers, (wide + 1) * per)):
-                    for n, name in enumerate(("f", "lat", "vert", "stor")):
-                        base = (k % per) * group + n * mine
-                        total = jnp.zeros((mine, LANES), F32)
-                        for y, part in zip(here, parts):
-                            spot = (base + y * mine) % LANES
-                            total = jnp.where((lane >= spot) & (lane < spot + mine), part, total)
-                        top[name][i, k, at] = pltpu.roll(total, LANES - base, 1) if base else total
+        parts = []
+        for wide in range(-(-layers // per)):
+            lines = slice(wide * mine, (wide + 1) * mine)
+            turned = [gathered[x * ny + y, lines] for y in range(ny)]
+            parts.append([pltpu.roll(v, y * mine, 1) if y else v for y, v in enumerate(turned)])
+        for k in range(deep):
+            for n, name in enumerate(("f", "lat", "vert", "stor")):
+                value = None
+                for g in range(fold):
+                    layer = g * deep + k
+                    base = (layer % per) * group + n * mine
+                    total = jnp.zeros((mine, LANES), F32)
+                    for y in range(ny):
+                        spot = (base + y * mine) % LANES
+                        hit = (lane >= spot) & (lane < spot + mine)
+                        total = jnp.where(hit, parts[layer // per][y], total)
+                    turn = (g * width - base) % LANES
+                    total = pltpu.roll(total, turn, 1) if turn else total
+                    value = total if value is None else value + total
+                top[name][k, at] = value
 
     def gather_some(step, carry):
         for n in range(4):
@@ -742,40 +778,39 @@
     for n, level in enumerate(range(LOCAL, LEVELS)):
         now, below = wholes[n], wholes[n + 1]
         nat_setup(now, 0.25**level)
-        nat_down(now, ress[n], (now["u"].shape[2] - 2 * PAD) // 8)
+        nat_down(now, ress[n], (now["u"].shape[1] - 2 * PAD) // 8)
         pairs = [(now[name], below[name]) for name in ("lat", "vert", "stor")]
-        restrict_all(pairs + [(ress[n], below["f"])])
+        restrict_all(pairs + [(ress[n], below["f"])], now["geo"], below["geo"])
     nat_setup(wholes[-1], 0.25**LEVELS)
-    conjugate(wholes[-1], spans[1] * 2 * half >> LEVELS)
+    conjugate(wholes[-1])
+
+    def planes_of(ref):
+        return lambda k: ref[k, PAD : ref.shape[1] - PAD]
+
     for n in reversed(range(len(wholes) - 1)):
         now, below = wholes[n], wholes[n + 1]
-        prolong_into(now, now["u"], lambda o, k: below["u"][o, k, PAD : below["u"].shape[2] - PAD], False)
-        nat_up(now, 0, (now["u"].shape[2] - 2 * PAD) // 8)
+        prolong_into(now, now["u"], planes_of(below["u"]), below["geo"], False)
+        nat_up(now, 0, (now["u"].shape[1] - 2 * PAD) // 8)
 
     x, y = lax.axis_index("gx"), lax.axis_index("gy")
     reach = (2 * half >> FIRST) >> (LOCAL - FIRST)
-    need = (nats[-1]["u"].shape[2] - 2 * PAD) // 2
-    height = top["u"].shape[2]
-    for i in range(tiles):
-        for k in range(layers):
-            wider[i, k, :height] = top["u"][i, k]
-            wider[i, k, height:] = jnp.zeros((PAD, LANES), F32)
+    height = top["u"].shape[1]
+    need = (nats[-1]["u"].shape[1] - 2 * PAD) // 2
+    lanes = iota((height, LANES), 1)
+    for layer in range(layers):
+        g, k = layer // deep, layer % deep
+        value = top["u"][k]
+        if g:
+            value = pltpu.roll(value, LANES - g * width, 1)
+        wider[layer, :height] = jnp.where(lanes < width, value, 0.0)
+        wider[layer, height:] = jnp.zeros((PAD, LANES), F32)
     begin = PAD + x * mine - reach
-    shift = y * mine - reach
-
-    def window(o, k):
-        parts = [wider[i, k, pl.ds(begin, need)] for i in range(tiles)]
-        turn = lax.rem(4 * LANES - shift, LANES)
-        lanes = iota((need, LANES), 1)
-        first = lax.div(shift + LANES, LANES) - 1
-        value = jnp.zeros((need, LANES), F32)
-        for i in range(tiles):
-            moved = pltpu.roll(parts[i], turn, 1)
-            value = jnp.where((first == i) & (lanes < turn) | (first == i) & (turn == 0), moved, value)
-            value = jnp.where((first == i - 1) & (lanes >= turn) & (turn != 0), moved, value)
-        return value
-
-    coarse = window
+    turn = lax.rem(LANES + reach - y * mine, LANES)
+
+    def coarse(k):
+        return pltpu.roll(wider[k, pl.ds(begin, need)], turn, 1)
+
+    coarse_geo = (1, nats[-1]["geo"][1] // 2, layers)
     margins, above = [], 0
     for level in range(LOCAL):
         margins.append(above + 4)
@@ -784,25 +819,25 @@
         now = dict(nats[level - 1])
         before = now["u"]
         now["u"] = fresh[level]
-        height = before.shape[2]
-        for i in range(before.shape[0]):
-            for k in range(layers):
-                now["u"][i, k, :PAD] = jnp.zeros((PAD, LANES), F32)
-                now["u"][i, k, height - PAD :] = jnp.zeros((PAD, LANES), F32)
-        prolong_into(now, before, coarse, level == LOCAL - 1)
+        planes, height, _ = before.shape
+        now["u"][:, :PAD] = jnp.zeros((planes, PAD, LANES), F32)
+        now["u"][:, height - PAD :] = jnp.zeros((planes, PAD, LANES), F32)
+        prolong_into(now, before, coarse, coarse_geo, level == LOCAL - 1)
         own = 2 * half >> level
         side = halo >> level if level < FIRST else (2 * half >> FIRST) >> (level - FIRST)
         reach = margins[level]
         nat_up(now, (side - reach) // 8, min(-(-(side + own + reach) // 8), (height - 2 * PAD) // 8))
-        coarse = functools.partial(lambda ref, o, k: ref[o, k, PAD : ref.shape[2] - PAD], now["u"])
+        coarse, coarse_geo = planes_of(now["u"]), now["geo"]
         if level == FIRST:
-            skip = side - (halo >> FIRST)
-            coarse = functools.partial(
-                lambda ref, o, k: pltpu.roll(
-                    ref[o, k, PAD + skip : ref.shape[2] - PAD], LANES - skip, 1
-                ),
-                now["u"],
-            )
+            assert coarse_geo[0] == 1
+            skip, blocks = side - (halo >> FIRST), now["u"]
+
+            def coarse(k):
+                return pltpu.roll(
+                    blocks[k, PAD + skip : blocks.shape[1] - PAD], LANES - skip, 1
+                )
+
+            coarse_geo = (1, (2 * half + 2 * halo) >> FIRST, layers)
 
     now = dict(s)
     now["u"] = fresh[0]
@@ -812,7 +847,7 @@
 
     def add(t):
         for k in range(layers):
-            value = fresh[1][0, k, rows(t)]
+            value = fresh[1][k, rows(t)]
             for pj in range(4):
                 now["u"][pj, k, rows(t)] = s["u"][pj, k, rows(t)] + value
 
@@ -843,10 +878,6 @@
 def packed_shape(layers, mine):
     per = LANES // (4 * mine)
     return shape(-(-layers // per) * mine, LANES)
-
-
-def whole_shape(level, layers, height, width):
-    return -(-(width >> level) // LANES), layers, up8(height >> level) + 2 * PAD, LANES
 
 
 def other_scratch(shapes):
@@ -894,9 +925,10 @@
 
     tall = up8(half + 2 * hh) + 2 * PAD
     four, two = (4, layers, tall, LANES), (2, layers, tall, LANES)
-    nat_shapes = [
-        (1, layers, up8((height + 2 * halo) >> level) + 2 * PAD, LANES) for level in range(1, FIRST)
-    ]
+    sides = [(height + 2 * halo) >> level for level in range(1, FIRST)]
+    geos = [geometry(layers, side) for side in sides]
+    assert geos[0][0] == 1
+    nat_shapes = [(geo[2], up8(side) + 2 * PAD, LANES) for geo, side in zip(geos, sides)]
     sizes = [four if name in ("u", "f", "invd", "fl") else two for name in SPLIT_KEPT]
     sizes += [four] * 4 + [(4, tall, LANES)] + [nat_shapes[0]] * 3
     shared = pl.pallas_call(
@@ -911,7 +943,9 @@
     for d in nat_shapes:
         kept += [shape(*d)] * len(NAT_KEPT)
     *saved, block = pl.pallas_call(
-        functools.partial(down_kernel, halo=halo, half=half, kinds=planar.shape[0]),
+        functools.partial(
+            down_kernel, halo=halo, half=half, kinds=planar.shape[0], geos=tuple(geos)
+        ),
         out_shape=(*[shape(*d) for d in sizes], *kept, packed_shape(layers, height >> FIRST)),
         in_specs=[SMEM] * 3 + [VMEM] * (2 + len(sizes)),
         out_specs=(VMEM,) * (len(sizes) + len(kept) + 1),
@@ -927,14 +961,14 @@
     above, below = swap(column, "gx", 0), swap(column, "gx", 1)
     mine = height >> FIRST
     assert 4 * mine <= LANES
-    block_shapes = [
-        (1, layers, up8(3 * mine >> n) + 2 * PAD, LANES) for n in range(LOCAL - FIRST)
-    ]
+    sides = [3 * mine >> n for n in range(LOCAL - FIRST)]
+    block_geos = [geometry(layers, side) for side in sides]
+    block_shapes = [(geo[2], up8(side) + 2 * PAD, LANES) for geo, side in zip(block_geos, sides)]
     kept = []
     for d in block_shapes:
         kept += [shape(*d)] * len(NAT_KEPT)
     *more, payload = pl.pallas_call(
-        mid_kernel,
+        functools.partial(mid_kernel, geos=tuple(block_geos)),
         out_shape=(*kept, packed_shape(layers, height >> LOCAL)),
         in_specs=[VMEM] * 5,
         out_specs=(VMEM,) * (len(kept) + 1),
@@ -948,16 +982,26 @@
     sent = jnp.broadcast_to(payload[None], (nx * ny,) + payload.shape)
     gathered = lax.all_to_all(sent, ("gx", "gy"), 0, 0)
 
+    whole_geos = [geometry(layers, ny * width >> level) for level in range(LOCAL, LEVELS + 1)]
+    wholes = [
+        (geo[2], up8(nx * height >> level) + 2 * PAD, LANES)
+        for geo, level in zip(whole_geos, range(LOCAL, LEVELS + 1))
+    ]
     scratch = []
-    for level in range(LOCAL, LEVELS + 1):
-        scratch += [pltpu.VMEM(whole_shape(level, layers, nx * height, ny * width), F32)] * len(WHOLE)
-    for level in range(LOCAL, LEVELS):
-        scratch.append(pltpu.VMEM(whole_shape(level, layers, nx * height, ny * width), F32))
+    for d in wholes:
+        scratch += [pltpu.VMEM(d, F32)] * len(WHOLE)
+    scratch += [pltpu.VMEM(d, F32) for d in wholes[:-1]]
     scratch += [pltpu.VMEM(four, F32)] + [pltpu.VMEM(d, F32) for d in nat_shapes]
-    wide, count, rows_of, _ = scratch[0].shape
-    scratch.append(pltpu.VMEM((wide, count, rows_of + PAD, LANES), F32))
+    scratch.append(pltpu.VMEM((layers, wholes[0][1] + PAD, LANES), F32))
     return pl.pallas_call(
-        functools.partial(up_kernel, halo=halo, half=half, spans=(nx, ny)),
+        functools.partial(
+            up_kernel,
+            halo=halo,
+            half=half,
+            spans=(nx, ny),
+            geos=tuple(geos + block_geos),
+            whole_geos=tuple(whole_geos),
+        ),
         out_shape=shape(layers, height, width),
         in_specs=[VMEM] * (1 + len(saved)),
         out_specs=VMEM,

time: 76 us -> 75.9 us (level)
  no operation moved by 1% of the time
where the time goes in v6:
time: 75.9 us; the launch traced here: 75.6 us
  Pallas kernels  25.2 us (33%)
  starting transfers between devices  23.9 us (31%)
  blocking collectives  18.1 us (24%)
  waiting for transfers between devices  8.22 us (11%)
    ppermute x8, starting transfers between devices, swap(): return lax.ppermute(values, axis, pairs + [(b, a) for a, b in pairs])  23.9 us
    all_to_all x1, blocking collectives, on_device(): gathered = lax.all_to_all(sent, ('gx', 'gy'), 0, 0)  18.1 us
    pallas_call x1, Pallas kernels, on_device(): pl.pallas_call(functools.partial(up_kernel, halo=halo, half=half, spans=(...  10.9 us
    ppermute x8, waiting for transfers between devices, swap(): return lax.ppermute(values, axis, pairs + [(b, a) for a, b in pairs])  8.22 us
    pallas_call x1, Pallas kernels, on_device(): pl.pallas_call(functools.partial(down_kernel, halo=halo, half=half, kinds...  5.77 us
    pallas_call x1, Pallas kernels, on_device(): pl.pallas_call(functools.partial(mid_kernel, geos=tuple(block_geos)), out...  3.12 us
    pallas_call x1, Pallas kernels, on_device(): pl.pallas_call(functools.partial(center_kernel, halo=halo, half=half, kin...  2.53 us
    pallas_call x1, Pallas kernels, on_device(): pl.pallas_call(functools.partial(prep_kernel, halo=halo), out_shape=(shap...  2 us
  transfers between devices with their start and end apart: 8, of which 3 were waited for; matrix products, arithmetic and copies ran while one was open for 0% of the time, Pallas kernels for 3%

profile of v6, /device:TPU:0, one launch (start us, length us, event | category | flops | bytes accessed | tf_op | source)
XLA Modules:
  0.0 75.6 jit_solution(13862512405654128788)
XLA Ops:
  0.0 0.0 copy-start.2
  0.0 0.0 copy-start.1
  0.0 0.0 copy-start
  0.0 2.0 %prep.1 = (f32[13,128,128]{2,1,0:T(8,128)S(1)}, f32[13,24,128]{2,1,0:T(8,128)S(1)}, f32[13,24,128]{2,1,0:T(8,128)S(1)}) custom-call(f32[64]{0:T(128)} %watt_hbm.1, s32[8,8]{1,0:T(8,128)} %cat_hbm.1, f32[6,128,128]{2,1,0:T(8,128)} %u_hbm.1, s32[6,128,128]{2,1,0:T(8,128)} %sub_hbm.1), custom_call_target="tpu_custom_call" | custom-call | tf_op jit(solution)/shard_map/prep/pallas_call | solution.py:898
  2.0 3.0 %collective-permute-start = (f32[13,24,128]{2,1,0:T(8,128)S(1)}, f32[13,24,128]{2,1,0:T(8,128)S(1)}, u32[]{:S(2)}, u32[]{:S(2)}) collective-permute-start(f32[13,24,128]{2,1,0:T(8,128)S(1)} %get-tuple-element.61), channel_id=1, source_target_pairs={{0,1},{2,3},{1,0},{3,2},{4,5},{6,7},{5,4},{7,6},{8,9},{10,11},{9,8... | collective-permute-start | bytes 479240 | tf_op jit(solution)/shard_map/ppermute | solution.py:871
  5.0 0.7 collective-permute-start.1
  5.7 3.4 %collective-permute-done.ra = f32[13,24,128]{2,1,0:T(8,128)S(1)} collective-permute-done((f32[13,24,128]{2,1,0:T(8,128)S(1)}, f32[13,24,128]{2,1,0:T(8,128)S(1)}, u32[]{:S(2)}, u32[]{:S(2)}) %collective-permute-start) | collective-permute-done | bytes 159776 | tf_op jit(solution)/shard_map/ppermute | solution.py:871
  9.2 0.0 collective-permute-done.1.rb
  9.2 0.9 %split.1 = (f32[13,4,64,128]{3,2,1,0:T(8,128)S(1)}, f32[624,128]{1,0:T(8,128)S(1)}, f32[624,128]{1,0:T(8,128)S(1)}) custom-call(f32[13,128,128]{2,1,0:T(8,128)S(1)} %get-tuple-element.60.own, f32[13,24,128]{2,1,0:T(8,128)S(1)} %collective-permute-done.ra, f32[13,24,128]{2,1,0:T(8,128)S(1)} %collective-permute-done.1.rb), custom_call_target="tpu_custom_call" | custom-call | tf_op jit(solution)/shard_map/split/pallas_call | solution.py:915
  10.1 0.1 collective-permute-start.2
  10.2 0.7 collective-permute-start.3
  10.8 0.0 copy-done.2
  10.8 0.0 copy-done.1
  10.9 0.0 copy-done
  10.9 2.5 %center.1 = (f32[4,6,104,128]{3,2,1,0:T(8,128)S(1)}, f32[4,6,104,128]{3,2,1,0:T(8,128)S(1)}, f32[4,6,104,128]{3,2,1,0:T(8,128)S(1)}, f32[2,6,104,128]{3,2,1,0:T(...) custom-call(f32[8]{0:T(128)S(1)} %copy-done, ...), custom_call_target="tpu_custom_call" | custom-call | tf_op jit(solution)/shard_map/center/pallas_call | solution.py:934
  13.4 0.0 collective-permute-done.2.refs_3_
  13.4 0.0 collective-permute-done.3.refs_4_
  13.4 5.8 %down.1 = (f32[4,6,104,128]{3,2,1,0:T(8,128)S(1)}, f32[4,6,104,128]{3,2,1,0:T(8,128)S(1)}, f32[4,6,104,128]{3,2,1,0:T(8,128)S(1)}, f32[2,6,104,128]{3,2,1,0:T(8,...) custom-call(f32[8]{0:T(128)S(1)} %copy-done, ...), custom_call_target="tpu_custom_call", output_to_operand_aliasing={{0}: (5, {}), {1}: (6, {}), {2}: (7, {}), {3}: (8, {}), {4}... | custom-call | tf_op jit(solution)/shard_map/down/pallas_call | solution.py:945
  19.2 0.7 collective-permute-start.5
  19.9 8.5 %collective-permute-start.4 = (f32[192,128]{1,0:T(8,128)S(1)}, f32[192,128]{1,0:T(8,128)S(1)}, u32[]{:S(2)}, u32[]{:S(2)}) collective-permute-start(f32[192,128]{1,0:T(8,128)S(1)} %get-tuple-element.83.own), channel_id=1, source_target_pairs={{0,1},{2,3},{1,0},{3,2},{4,5},{6,7},{5,4},{7,6},{8,9},{10,11},{9,8... | collective-permute-start | bytes 294920 | tf_op jit(solution)/shard_map/ppermute | solution.py:871
  28.4 0.0 collective-permute-done.5.rb
  28.4 3.6 %collective-permute-done.4.ra = f32[192,128]{1,0:T(8,128)S(1)} collective-permute-done((f32[192,128]{1,0:T(8,128)S(1)}, f32[192,128]{1,0:T(8,128)S(1)}, u32[]{:S(2)}, u32[]{:S(2)}) %collective-permute-start.4) | collective-permute-done | bytes 98336 | tf_op jit(solution)/shard_map/ppermute | solution.py:871
  32.0 0.7 collective-permute-start.7
  32.7 9.6 %collective-permute-start.6 = (f32[3,192,128]{2,1,0:T(8,128)S(1)}, f32[3,192,128]{2,1,0:T(8,128)S(1)}, u32[]{:S(2)}, u32[]{:S(2)}) collective-permute-start(f32[3,192,128]{2,1,0:T(8,128)S(1)} %pad_maximum_fusion), channel_id=1, source_target_pairs={{0,4},{8,12},{16,20},{24,28},{4,0},{12,8},{20,16},{28,24},{1,5},{9... | collective-permute-start | bytes 884744 | tf_op jit(solution)/shard_map/ppermute | solution.py:871
  42.3 0.0 collective-permute-done.7.tb
  42.3 1.2 %collective-permute-done.6.ta = f32[3,192,128]{2,1,0:T(8,128)S(1)} collective-permute-done((f32[3,192,128]{2,1,0:T(8,128)S(1)}, f32[3,192,128]{2,1,0:T(8,128)S(1)}, u32[]{:S(2)}, u32[]{:S(2)}) %collective-permute-start.6) | collective-permute-done | bytes 294944 | tf_op jit(solution)/shard_map/ppermute | solution.py:871
  43.5 3.1 %mid.1 = (f32[6,112,128]{2,1,0:T(8,128)S(1)}, f32[6,112,128]{2,1,0:T(8,128)S(1)}, f32[6,112,128]{2,1,0:T(8,128)S(1)}, f32[6,112,128]{2,1,0:T(8,128)S(1)}, f32[6,...) custom-call(f32[192,128]{1,0:T(8,128)S(1)} %get-tuple-element.83.own, ...), custom_call_target="tpu_custom_call" | custom-call | tf_op jit(solution)/shard_map/mid/pallas_call | solution.py:970
  46.6 18.1 %all_to_all.5.refs_0_ = f32[32,16,128]{2,1,0:T(8,128)S(1)} all-to-all(f32[32,16,128]{2,1,0:T(8,128)S(1)} %broadcast_in_dim.2), channel_id=1, replica_groups=mesh['gx'=8,'gy'=4] {'gx','gy'}, dimensions={0} | all-to-all | bytes 524288 | tf_op jit(solution)/shard_map/all_to_all | solution.py:983
  64.7 10.9 %up.1 = f32[6,128,128]{2,1,0:T(8,128)} custom-call(f32[32,16,128]{2,1,0:T(8,128)S(1)} %all_to_all.5.refs_0_, f32[4,6,104,128]{3,2,1,0:T(8,128)S(1)} %get-tuple-element.85.refs_1_, f32[4,6,104,128]{3,2,1,0:T(8,128)S(1)} %get-tuple-element.86.refs_2_, f32[4,6,104,128]{3,2,1,0:T(8,128)S(1)} %get-tuple-element.87.refs_3_, ...), custom_call_target="tpu_custom_call" | custom-call | tf_op jit(solution)/shard_map/up/pallas_call | solution.py:996
  (2 shorter events, 0.1 us)
Async XLA Ops:
  0.0 10.8 %copy-start.2 = (f32[8]{0:T(128)S(1)}, f32[8]{0:T(128)}, u32[]{:S(2)}) copy-start(f32[8]{0:T(128)} %refs_2_.3) | copy-start | bytes 100
  0.0 10.8 %copy-start.1 = (f32[8]{0:T(128)S(1)}, f32[8]{0:T(128)}, u32[]{:S(2)}) copy-start(f32[8]{0:T(128)} %refs_1_.3) | copy-start | bytes 100
  0.0 10.9 %copy-start = (f32[8]{0:T(128)S(1)}, f32[8]{0:T(128)}, u32[]{:S(2)}) copy-start(f32[8]{0:T(128)} %refs_0_.3) | copy-start | bytes 100
  2.0 7.1 %collective-permute-start = (f32[13,24,128]{2,1,0:T(8,128)S(1)}, f32[13,24,128]{2,1,0:T(8,128)S(1)}, u32[]{:S(2)}, u32[]{:S(2)}) collective-permute-start(f32[13,24,128]{2,1,0:T(8,128)S(1)} %get-tuple-element.61), channel_id=1, source_target_pairs={{0,1},{2,3},{1,0},{3,2},{4,5},{6,7},{5,4},{7,6},{8,9},{10,11},{9,8... | collective-permute-start | bytes 479240 | tf_op jit(solution)/shard_map/ppermute | solution.py:871
  5.0 4.1 %collective-permute-start.1 = (f32[13,24,128]{2,1,0:T(8,128)S(1)}, f32[13,24,128]{2,1,0:T(8,128)S(1)}, u32[]{:S(2)}, u32[]{:S(2)}) collective-permute-start(f32[13,24,128]{2,1,0:T(8,128)S(1)} %get-tuple-element.62), channel_id=1, source_target_pairs={{1,2},{2,1},{5,6},{6,5},{9,10},{10,9},{13,14},{14,13},{17,18},{18,... | collective-permute-start | bytes 479240 | tf_op jit(solution)/shard_map/ppermute | solution.py:871
  10.1 3.3 %collective-permute-start.2 = (f32[624,128]{1,0:T(8,128)S(1)}, f32[624,128]{1,0:T(8,128)S(1)}, u32[]{:S(2)}, u32[]{:S(2)}) collective-permute-start(f32[624,128]{1,0:T(8,128)S(1)} %get-tuple-element.63), channel_id=1, source_target_pairs={{0,4},{8,12},{16,20},{24,28},{4,0},{12,8},{20,16},{28,24},{1,5},{9... | collective-permute-start | bytes 958472 | tf_op jit(solution)/shard_map/ppermute | solution.py:871
  10.2 3.3 %collective-permute-start.3 = (f32[624,128]{1,0:T(8,128)S(1)}, f32[624,128]{1,0:T(8,128)S(1)}, u32[]{:S(2)}, u32[]{:S(2)}) collective-permute-start(f32[624,128]{1,0:T(8,128)S(1)} %get-tuple-element.64), channel_id=1, source_target_pairs={{4,8},{12,16},{20,24},{8,4},{16,12},{24,20},{5,9},{13,17},{21,25},... | collective-permute-start | bytes 958472 | tf_op jit(solution)/shard_map/ppermute | solution.py:871
  19.2 9.2 %collective-permute-start.5 = (f32[192,128]{1,0:T(8,128)S(1)}, f32[192,128]{1,0:T(8,128)S(1)}, u32[]{:S(2)}, u32[]{:S(2)}) collective-permute-start(f32[192,128]{1,0:T(8,128)S(1)} %get-tuple-element.83.own), channel_id=1, source_target_pairs={{1,2},{2,1},{5,6},{6,5},{9,10},{10,9},{13,14},{14,13},{17,18},{18,... | collective-permute-start | bytes 294920 | tf_op jit(solution)/shard_map/ppermute | solution.py:871
  19.9 12.1 %collective-permute-start.4 = (f32[192,128]{1,0:T(8,128)S(1)}, f32[192,128]{1,0:T(8,128)S(1)}, u32[]{:S(2)}, u32[]{:S(2)}) collective-permute-start(f32[192,128]{1,0:T(8,128)S(1)} %get-tuple-element.83.own), channel_id=1, source_target_pairs={{0,1},{2,3},{1,0},{3,2},{4,5},{6,7},{5,4},{7,6},{8,9},{10,11},{9,8... | collective-permute-start | bytes 294920 | tf_op jit(solution)/shard_map/ppermute | solution.py:871
  32.0 10.3 %collective-permute-start.7 = (f32[3,192,128]{2,1,0:T(8,128)S(1)}, f32[3,192,128]{2,1,0:T(8,128)S(1)}, u32[]{:S(2)}, u32[]{:S(2)}) collective-permute-start(f32[3,192,128]{2,1,0:T(8,128)S(1)} %pad_maximum_fusion), channel_id=1, source_target_pairs={{4,8},{12,16},{20,24},{8,4},{16,12},{24,20},{5,9},{13,17},{21,25},... | collective-permute-start | bytes 884744 | tf_op jit(solution)/shard_map/ppermute | solution.py:871
  32.7 10.8 %collective-permute-start.6 = (f32[3,192,128]{2,1,0:T(8,128)S(1)}, f32[3,192,128]{2,1,0:T(8,128)S(1)}, u32[]{:S(2)}, u32[]{:S(2)}) collective-permute-start(f32[3,192,128]{2,1,0:T(8,128)S(1)} %pad_maximum_fusion), channel_id=1, source_target_pairs={{0,4},{8,12},{16,20},{24,28},{4,0},{12,8},{20,16},{28,24},{1,5},{9... | collective-permute-start | bytes 884744 | tf_op jit(solution)/shard_map/ppermute | solution.py:871

commit v7 on v6

--- a/solution.py
+++ b/solution.py
@@ -15,7 +15,7 @@
 COARSE_ITERS = 12
 LANES = 128
 PAD = 8
-MOST = dict(split=6, nat=12, first=12, residual=12, setup=6, look=1, faces=4, remain=6, add=4)
+MOST = dict(split=12, nat=12, first=12, residual=12, setup=12, look=1, faces=4, remain=12, add=12)
 HI = lax.Precision.HIGHEST
 F32 = jnp.float32
 VMEM = pl.BlockSpec(memory_space=pltpu.VMEM)
@@ -103,15 +103,8 @@
         a_ref[q] = jnp.where(even, high, low)
         b_ref[q] = jnp.where(even, low, high)
 
-    copies[0].wait()
-    for q in range(layers):
-        send(q)
-    copies[1].wait()
-    for q in range(layers, 2 * layers):
-        planes[q] = (sub_ref[q - layers] + 1).astype(F32)
-        send(q)
-    copies[2].wait()
-    copies[3].wait()
+    for copy in copies:
+        copy.wait()
     cat = cat_ref[...]
     power = jnp.zeros(cat.shape, F32)
     for n in range(watt.shape[0]):
@@ -119,7 +112,10 @@
     spread_r = (iota((height, cat.shape[0]), 0) // TILE == iota((height, cat.shape[0]), 1)).astype(F32)
     spread_c = (iota((cat.shape[1], width), 1) // TILE == iota((cat.shape[1], width), 0)).astype(F32)
     planes[2 * layers] = dot(dot(spread_r, power), spread_c)
-    send(2 * layers)
+    for q in range(2 * layers + 1):
+        if layers <= q < 2 * layers:
+            planes[q] = (sub_ref[q - layers] + 1).astype(F32)
+        send(q)
 
 
 def split_kernel(own, ra, rb, out, a_ref, b_ref, scr, *, halo):
@@ -429,7 +425,7 @@
         payload[wide * mine : (wide + 1) * mine] = total
 
 
-def look_up(s, first, heat, tables, kinds, lo, hi):
+def look_up(s, first, heat, kinds, lo, hi):
     layers = s["u"].shape[1]
 
     def look(t):
@@ -441,7 +437,7 @@
                 value = [jnp.zeros_like(label)] * 3
                 for n in range(kinds):
                     hit = label == float(n + 1)
-                    value = [jnp.where(hit, tables[i][n], value[i]) for i in range(3)]
+                    value = [jnp.where(hit, s["table"][i * kinds + n], value[i]) for i in range(3)]
                 for i, name in enumerate(("lat", "vert", "stor")):
                     s[name][at] = value[i]
                     sums[i] = value[i] if sums[i] is None else sums[i] + value[i]
@@ -494,7 +490,7 @@
     over(lo, hi, MOST["faces"], faces)
 
 
-SHARED = SPLIT_KEPT + ("lat", "vert", "stor", "diag", "heat", "lat1", "vert1", "stor1")
+SHARED = SPLIT_KEPT + ("lat", "vert", "stor", "diag", "heat", "lat1", "vert1", "stor1", "table")
 
 
 def center_kernel(*refs, halo, half, kinds):
@@ -516,7 +512,10 @@
         for k in range(layers):
             ref[k, :PAD] = zeros
             ref[k, height - PAD :] = zeros
-    look_up(s, first, s["heat"], tables, kinds, *bounds(hh, half, 0))
+    for i in range(3):
+        for n in range(kinds):
+            s["table"][i * kinds + n] = jnp.full((8, LANES), tables[i][n], F32)
+    look_up(s, first, s["heat"], kinds, *bounds(hh, half, 0))
     split_setup(s, *bounds(hh, half, 1))
 
 
@@ -527,8 +526,8 @@
 
 
 def down_kernel(*refs, halo, half, kinds, geos):
-    tables, (ra, rb) = refs[:3], refs[3:5]
-    refs = list(refs[5 + len(SHARED) :])
+    ra, rb = refs[:2]
+    refs = list(refs[2 + len(SHARED) :])
     s = dict(zip(SHARED, refs[: len(SHARED)]))
     refs = refs[len(SHARED) :]
     nats = [{} for level in range(1, FIRST)]
@@ -569,7 +568,7 @@
             ref[k, ref.shape[1] - PAD :] = zeros
     lo, hi = bounds(hh, half, 1)
     for begin, end in ((0, lo), (hi, steps)):
-        look_up(s, first, heat, tables, kinds, begin, end)
+        look_up(s, first, heat, kinds, begin, end)
     for begin, end in ((0, lo), (hi, steps)):
         split_setup(s, begin, end)
     split_sweeps(s, 0, steps, layers)
@@ -931,6 +930,7 @@
     nat_shapes = [(geo[2], up8(side) + 2 * PAD, LANES) for geo, side in zip(geos, sides)]
     sizes = [four if name in ("u", "f", "invd", "fl") else two for name in SPLIT_KEPT]
     sizes += [four] * 4 + [(4, tall, LANES)] + [nat_shapes[0]] * 3
+    sizes.append((3 * planar.shape[0], 8, LANES))
     shared = pl.pallas_call(
         functools.partial(center_kernel, halo=halo, half=half, kinds=planar.shape[0]),
         out_shape=tuple(shape(*d) for d in sizes),
@@ -947,13 +947,13 @@
             down_kernel, halo=halo, half=half, kinds=planar.shape[0], geos=tuple(geos)
         ),
         out_shape=(*[shape(*d) for d in sizes], *kept, packed_shape(layers, height >> FIRST)),
-        in_specs=[SMEM] * 3 + [VMEM] * (2 + len(sizes)),
+        in_specs=[VMEM] * (2 + len(sizes)),
         out_specs=(VMEM,) * (len(sizes) + len(kept) + 1),
         scratch_shapes=other_scratch(nat_shapes)[3:],
-        input_output_aliases={5 + n: n for n in range(len(sizes))},
+        input_output_aliases={2 + n: n for n in range(len(sizes))},
         compiler_params=limit(26),
         name="down",
-    )(planar, vertical, ratio, a, b, *shared)
+    )(a, b, *shared)
     saved = saved[: len(SPLIT_KEPT)] + saved[len(sizes) :]
 
     a, b = swap(block, "gy", 0), swap(block, "gy", 1)

time: 75.9 us -> 73.1 us (0.963)
  Pallas kernels: 25.2 us -> 22.4 us
    pallas_call x1, Pallas kernels: 5.77 us -> 4.4 us  [on_device(): pl.pallas_call(functools.partial(down_kernel, halo=halo, half=half, kinds...]
    pallas_call x1, Pallas kernels: 10.9 us -> 9.92 us  [on_device(): pl.pallas_call(functools.partial(up_kernel, halo=halo, half=half, spans=(...]
where the time goes in v7:
time: 73.1 us; the launch traced here: 72.9 us
  starting transfers between devices  24 us (33%)
  Pallas kernels  22.4 us (31%)
  blocking collectives  18.1 us (25%)
  waiting for transfers between devices  8.22 us (11%)
    ppermute x8, starting transfers between devices, swap(): return lax.ppermute(values, axis, pairs + [(b, a) for a, b in pairs])  24 us
    all_to_all x1, blocking collectives, on_device(): gathered = lax.all_to_all(sent, ('gx', 'gy'), 0, 0)  18.1 us
    pallas_call x1, Pallas kernels, on_device(): pl.pallas_call(functools.partial(up_kernel, halo=halo, half=half, spans=(...  9.92 us
    ppermute x8, waiting for transfers between devices, swap(): return lax.ppermute(values, axis, pairs + [(b, a) for a, b in pairs])  8.22 us
    pallas_call x1, Pallas kernels, on_device(): pl.pallas_call(functools.partial(down_kernel, halo=halo, half=half, kinds...  4.4 us
    pallas_call x1, Pallas kernels, on_device(): pl.pallas_call(functools.partial(mid_kernel, geos=tuple(block_geos)), out...  2.98 us
    pallas_call x1, Pallas kernels, on_device(): pl.pallas_call(functools.partial(center_kernel, halo=halo, half=half, kin...  2.41 us
    pallas_call x1, Pallas kernels, on_device(): pl.pallas_call(functools.partial(prep_kernel, halo=halo), out_shape=(shap...  1.78 us
  transfers between devices with their start and end apart: 8, of which 3 were waited for; matrix products, arithmetic and copies ran while one was open for 0% of the time, Pallas kernels for 3%

profile of v7, /device:TPU:0, one launch (start us, length us, event | category | flops | bytes accessed | tf_op | source)
XLA Modules:
  0.0 72.9 jit_solution(105348157563415941)
XLA Ops:
  0.0 0.0 copy-start.2
  0.0 0.0 copy-start.1
  0.0 0.0 copy-start
  0.0 1.8 %prep.1 = (f32[13,128,128]{2,1,0:T(8,128)S(1)}, f32[13,24,128]{2,1,0:T(8,128)S(1)}, f32[13,24,128]{2,1,0:T(8,128)S(1)}) custom-call(f32[64]{0:T(128)} %watt_hbm.1, s32[8,8]{1,0:T(8,128)} %cat_hbm.1, f32[6,128,128]{2,1,0:T(8,128)} %u_hbm.1, s32[6,128,128]{2,1,0:T(8,128)} %sub_hbm.1), custom_call_target="tpu_custom_call" | custom-call | tf_op jit(solution)/shard_map/prep/pallas_call | solution.py:897
  1.8 3.0 %collective-permute-start = (f32[13,24,128]{2,1,0:T(8,128)S(1)}, f32[13,24,128]{2,1,0:T(8,128)S(1)}, u32[]{:S(2)}, u32[]{:S(2)}) collective-permute-start(f32[13,24,128]{2,1,0:T(8,128)S(1)} %get-tuple-element.62), channel_id=1, source_target_pairs={{0,1},{2,3},{1,0},{3,2},{4,5},{6,7},{5,4},{7,6},{8,9},{10,11},{9,8... | collective-permute-start | bytes 479240 | tf_op jit(solution)/shard_map/ppermute | solution.py:870
  4.8 0.7 collective-permute-start.1
  5.5 3.4 %collective-permute-done.ra = f32[13,24,128]{2,1,0:T(8,128)S(1)} collective-permute-done((f32[13,24,128]{2,1,0:T(8,128)S(1)}, f32[13,24,128]{2,1,0:T(8,128)S(1)}, u32[]{:S(2)}, u32[]{:S(2)}) %collective-permute-start) | collective-permute-done | bytes 159776 | tf_op jit(solution)/shard_map/ppermute | solution.py:870
  8.9 0.0 collective-permute-done.1.rb
  8.9 0.9 %split.1 = (f32[13,4,64,128]{3,2,1,0:T(8,128)S(1)}, f32[624,128]{1,0:T(8,128)S(1)}, f32[624,128]{1,0:T(8,128)S(1)}) custom-call(f32[13,128,128]{2,1,0:T(8,128)S(1)} %get-tuple-element.61.own, f32[13,24,128]{2,1,0:T(8,128)S(1)} %collective-permute-done.ra, f32[13,24,128]{2,1,0:T(8,128)S(1)} %collective-permute-done.1.rb), custom_call_target="tpu_custom_call" | custom-call | tf_op jit(solution)/shard_map/split/pallas_call | solution.py:914
  9.9 0.1 collective-permute-start.2
  9.9 0.7 collective-permute-start.3
  10.6 0.0 copy-done.2
  10.6 0.0 copy-done.1
  10.6 0.0 copy-done
  10.6 2.4 %center.1 = (f32[4,6,104,128]{3,2,1,0:T(8,128)S(1)}, f32[4,6,104,128]{3,2,1,0:T(8,128)S(1)}, f32[4,6,104,128]{3,2,1,0:T(8,128)S(1)}, f32[2,6,104,128]{3,2,1,0:T(...) custom-call(f32[8]{0:T(128)S(1)} %copy-done, ...), custom_call_target="tpu_custom_call" | custom-call | tf_op jit(solution)/shard_map/center/pallas_call | solution.py:934
  13.1 0.0 collective-permute-done.2.refs_0_
  13.1 0.0 collective-permute-done.3.refs_1_
  13.1 4.4 %down.1 = (f32[4,6,104,128]{3,2,1,0:T(8,128)S(1)}, f32[4,6,104,128]{3,2,1,0:T(8,128)S(1)}, f32[4,6,104,128]{3,2,1,0:T(8,128)S(1)}, f32[2,6,104,128]{3,2,1,0:T(8,...) custom-call(f32[624,128]{1,0:T(8,128)S(1)} %collective-permute-done., ...), custom_call_target="tpu_custom_call", output_to_operand_aliasing={{0}: (2, {}), {1}: (3, {}), {2}: (4, {}), {3}: (5, {}), {4}... | custom-call | tf_op jit(solution)/shard_map/down/pallas_call | solution.py:945
  17.5 0.7 collective-permute-start.5
  18.2 8.5 %collective-permute-start.4 = (f32[192,128]{1,0:T(8,128)S(1)}, f32[192,128]{1,0:T(8,128)S(1)}, u32[]{:S(2)}, u32[]{:S(2)}) collective-permute-start(f32[192,128]{1,0:T(8,128)S(1)} %get-tuple-element.85.own), channel_id=1, source_target_pairs={{0,1},{2,3},{1,0},{3,2},{4,5},{6,7},{5,4},{7,6},{8,9},{10,11},{9,8... | collective-permute-start | bytes 294920 | tf_op jit(solution)/shard_map/ppermute | solution.py:870
  26.7 0.0 collective-permute-done.5.rb
  26.7 3.6 %collective-permute-done.4.ra = f32[192,128]{1,0:T(8,128)S(1)} collective-permute-done((f32[192,128]{1,0:T(8,128)S(1)}, f32[192,128]{1,0:T(8,128)S(1)}, u32[]{:S(2)}, u32[]{:S(2)}) %collective-permute-start.4) | collective-permute-done | bytes 98336 | tf_op jit(solution)/shard_map/ppermute | solution.py:870
  30.3 0.7 collective-permute-start.7
  31.0 9.7 %collective-permute-start.6 = (f32[3,192,128]{2,1,0:T(8,128)S(1)}, f32[3,192,128]{2,1,0:T(8,128)S(1)}, u32[]{:S(2)}, u32[]{:S(2)}) collective-permute-start(f32[3,192,128]{2,1,0:T(8,128)S(1)} %pad_maximum_fusion), channel_id=1, source_target_pairs={{0,4},{8,12},{16,20},{24,28},{4,0},{12,8},{20,16},{28,24},{1,5},{9... | collective-permute-start | bytes 884744 | tf_op jit(solution)/shard_map/ppermute | solution.py:870
  40.7 0.0 collective-permute-done.7.tb
  40.7 1.2 %collective-permute-done.6.ta = f32[3,192,128]{2,1,0:T(8,128)S(1)} collective-permute-done((f32[3,192,128]{2,1,0:T(8,128)S(1)}, f32[3,192,128]{2,1,0:T(8,128)S(1)}, u32[]{:S(2)}, u32[]{:S(2)}) %collective-permute-start.6) | collective-permute-done | bytes 294944 | tf_op jit(solution)/shard_map/ppermute | solution.py:870
  41.9 3.0 %mid.1 = (f32[6,112,128]{2,1,0:T(8,128)S(1)}, f32[6,112,128]{2,1,0:T(8,128)S(1)}, f32[6,112,128]{2,1,0:T(8,128)S(1)}, f32[6,112,128]{2,1,0:T(8,128)S(1)}, f32[6,...) custom-call(f32[192,128]{1,0:T(8,128)S(1)} %get-tuple-element.85.own, ...), custom_call_target="tpu_custom_call" | custom-call | tf_op jit(solution)/shard_map/mid/pallas_call | solution.py:970
  44.9 18.1 %all_to_all.5.refs_0_ = f32[32,16,128]{2,1,0:T(8,128)S(1)} all-to-all(f32[32,16,128]{2,1,0:T(8,128)S(1)} %broadcast_in_dim.2), channel_id=1, replica_groups=mesh['gx'=8,'gy'=4] {'gx','gy'}, dimensions={0} | all-to-all | bytes 524288 | tf_op jit(solution)/shard_map/all_to_all | solution.py:983
  63.0 9.9 %up.1 = f32[6,128,128]{2,1,0:T(8,128)} custom-call(f32[32,16,128]{2,1,0:T(8,128)S(1)} %all_to_all.5.refs_0_, f32[4,6,104,128]{3,2,1,0:T(8,128)S(1)} %get-tuple-element.87.refs_1_, f32[4,6,104,128]{3,2,1,0:T(8,128)S(1)} %get-tuple-element.88.refs_2_, f32[4,6,104,128]{3,2,1,0:T(8,128)S(1)} %get-tuple-element.89.refs_3_, ...), custom_call_target="tpu_custom_call" | custom-call | tf_op jit(solution)/shard_map/up/pallas_call | solution.py:996
  (2 shorter events, 0.1 us)
Async XLA Ops:
  0.0 10.6 %copy-start.2 = (f32[8]{0:T(128)S(1)}, f32[8]{0:T(128)}, u32[]{:S(2)}) copy-start(f32[8]{0:T(128)} %refs_2_.1) | copy-start | bytes 100
  0.0 10.6 %copy-start.1 = (f32[8]{0:T(128)S(1)}, f32[8]{0:T(128)}, u32[]{:S(2)}) copy-start(f32[8]{0:T(128)} %refs_1_.1) | copy-start | bytes 100
  0.0 10.6 %copy-start = (f32[8]{0:T(128)S(1)}, f32[8]{0:T(128)}, u32[]{:S(2)}) copy-start(f32[8]{0:T(128)} %refs_0_.1) | copy-start | bytes 100
  1.8 7.1 %collective-permute-start = (f32[13,24,128]{2,1,0:T(8,128)S(1)}, f32[13,24,128]{2,1,0:T(8,128)S(1)}, u32[]{:S(2)}, u32[]{:S(2)}) collective-permute-start(f32[13,24,128]{2,1,0:T(8,128)S(1)} %get-tuple-element.62), channel_id=1, source_target_pairs={{0,1},{2,3},{1,0},{3,2},{4,5},{6,7},{5,4},{7,6},{8,9},{10,11},{9,8... | collective-permute-start | bytes 479240 | tf_op jit(solution)/shard_map/ppermute | solution.py:870
  4.8 4.1 %collective-permute-start.1 = (f32[13,24,128]{2,1,0:T(8,128)S(1)}, f32[13,24,128]{2,1,0:T(8,128)S(1)}, u32[]{:S(2)}, u32[]{:S(2)}) collective-permute-start(f32[13,24,128]{2,1,0:T(8,128)S(1)} %get-tuple-element.63), channel_id=1, source_target_pairs={{1,2},{2,1},{5,6},{6,5},{9,10},{10,9},{13,14},{14,13},{17,18},{18,... | collective-permute-start | bytes 479240 | tf_op jit(solution)/shard_map/ppermute | solution.py:870
  9.9 3.2 %collective-permute-start.2 = (f32[624,128]{1,0:T(8,128)S(1)}, f32[624,128]{1,0:T(8,128)S(1)}, u32[]{:S(2)}, u32[]{:S(2)}) collective-permute-start(f32[624,128]{1,0:T(8,128)S(1)} %get-tuple-element.64), channel_id=1, source_target_pairs={{0,4},{8,12},{16,20},{24,28},{4,0},{12,8},{20,16},{28,24},{1,5},{9... | collective-permute-start | bytes 958472 | tf_op jit(solution)/shard_map/ppermute | solution.py:870
  9.9 3.2 %collective-permute-start.3 = (f32[624,128]{1,0:T(8,128)S(1)}, f32[624,128]{1,0:T(8,128)S(1)}, u32[]{:S(2)}, u32[]{:S(2)}) collective-permute-start(f32[624,128]{1,0:T(8,128)S(1)} %get-tuple-element.65), channel_id=1, source_target_pairs={{4,8},{12,16},{20,24},{8,4},{16,12},{24,20},{5,9},{13,17},{21,25},... | collective-permute-start | bytes 958472 | tf_op jit(solution)/shard_map/ppermute | solution.py:870
  17.5 9.2 %collective-permute-start.5 = (f32[192,128]{1,0:T(8,128)S(1)}, f32[192,128]{1,0:T(8,128)S(1)}, u32[]{:S(2)}, u32[]{:S(2)}) collective-permute-start(f32[192,128]{1,0:T(8,128)S(1)} %get-tuple-element.85.own), channel_id=1, source_target_pairs={{1,2},{2,1},{5,6},{6,5},{9,10},{10,9},{13,14},{14,13},{17,18},{18,... | collective-permute-start | bytes 294920 | tf_op jit(solution)/shard_map/ppermute | solution.py:870
  18.2 12.1 %collective-permute-start.4 = (f32[192,128]{1,0:T(8,128)S(1)}, f32[192,128]{1,0:T(8,128)S(1)}, u32[]{:S(2)}, u32[]{:S(2)}) collective-permute-start(f32[192,128]{1,0:T(8,128)S(1)} %get-tuple-element.85.own), channel_id=1, source_target_pairs={{0,1},{2,3},{1,0},{3,2},{4,5},{6,7},{5,4},{7,6},{8,9},{10,11},{9,8... | collective-permute-start | bytes 294920 | tf_op jit(solution)/shard_map/ppermute | solution.py:870
  30.3 10.4 %collective-permute-start.7 = (f32[3,192,128]{2,1,0:T(8,128)S(1)}, f32[3,192,128]{2,1,0:T(8,128)S(1)}, u32[]{:S(2)}, u32[]{:S(2)}) collective-permute-start(f32[3,192,128]{2,1,0:T(8,128)S(1)} %pad_maximum_fusion), channel_id=1, source_target_pairs={{4,8},{12,16},{20,24},{8,4},{16,12},{24,20},{5,9},{13,17},{21,25},... | collective-permute-start | bytes 884744 | tf_op jit(solution)/shard_map/ppermute | solution.py:870
  31.0 10.9 %collective-permute-start.6 = (f32[3,192,128]{2,1,0:T(8,128)S(1)}, f32[3,192,128]{2,1,0:T(8,128)S(1)}, u32[]{:S(2)}, u32[]{:S(2)}) collective-permute-start(f32[3,192,128]{2,1,0:T(8,128)S(1)} %pad_maximum_fusion), channel_id=1, source_target_pairs={{0,4},{8,12},{16,20},{24,28},{4,0},{12,8},{20,16},{28,24},{1,5},{9... | collective-permute-start | bytes 884744 | tf_op jit(solution)/shard_map/ppermute | solution.py:870

commit v8 on v7

--- a/solution.py
+++ b/solution.py
@@ -713,7 +713,7 @@
 
 def up_kernel(*refs, halo, half, spans, geos, whole_geos):
     refs = list(refs)
-    gathered = refs.pop(0)
+    gathered, traded = refs.pop(0), refs.pop(0)
     s = dict(zip(SPLIT_KEPT, refs[: len(SPLIT_KEPT)]))
     refs = refs[len(SPLIT_KEPT) :]
     nats = []
@@ -744,12 +744,18 @@
             whole[name][:, :PAD] = zeros
             whole[name][:, height - PAD :] = zeros
 
-    def gather(x):
+    parity = lax.axis_index("gx") % 2
+
+    def gather(x, core):
         at = pl.ds(pl.multiple_of(x * mine, 8) + PAD, mine)
         parts = []
         for wide in range(-(-layers // per)):
             lines = slice(wide * mine, (wide + 1) * mine)
-            turned = [gathered[x * ny + y, lines] for y in range(ny)]
+            at_x = lax.div(x, 2) * ny
+            turned = [
+                jnp.where(parity == core, gathered[at_x + y, lines], traded[at_x + y, lines])
+                for y in range(ny)
+            ]
             parts.append([pltpu.roll(v, y * mine, 1) if y else v for y, v in enumerate(turned)])
         for k in range(deep):
             for n, name in enumerate(("f", "lat", "vert", "stor")):
@@ -769,10 +775,10 @@
 
     def gather_some(step, carry):
         for n in range(4):
-            gather(jnp.minimum(4 * step + n, nx - 1))
+            gather(4 * step + n, n % 2)
         return carry
 
-    lax.fori_loop(0, -(-nx // 4), gather_some, 0)
+    lax.fori_loop(0, nx // 4, gather_some, 0)
 
     for n, level in enumerate(range(LOCAL, LEVELS)):
         now, below = wholes[n], wholes[n + 1]
@@ -979,8 +985,11 @@
     saved += more
     nat_shapes += block_shapes
 
-    sent = jnp.broadcast_to(payload[None], (nx * ny,) + payload.shape)
-    gathered = lax.all_to_all(sent, ("gx", "gy"), 0, 0)
+    assert nx % 4 == 0
+    groups = [[x * ny + y for x in range(c, nx, 2) for y in range(ny)] for c in range(2)]
+    sent = jnp.broadcast_to(payload[None], (nx // 2 * ny,) + payload.shape)
+    gathered = lax.all_to_all(sent, ("gx", "gy"), 0, 0, axis_index_groups=groups)
+    traded = swap(gathered, "gx", 0)
 
     whole_geos = [geometry(layers, ny * width >> level) for level in range(LOCAL, LEVELS + 1)]
     wholes = [
@@ -1003,12 +1012,12 @@
             whole_geos=tuple(whole_geos),
         ),
         out_shape=shape(layers, height, width),
-        in_specs=[VMEM] * (1 + len(saved)),
+        in_specs=[VMEM] * (2 + len(saved)),
         out_specs=VMEM,
         scratch_shapes=scratch,
         compiler_params=limit(16, scratch),
         name="up",
-    )(gathered, *saved)
+    )(gathered, traded, *saved)
 
 
 def solution(mesh):

time: 73.1 us -> 72.4 us (level)
  blocking collectives: 18.1 us -> 16 us
  waiting for transfers between devices: 8.22 us -> 9.56 us
    all_to_all x1, blocking collectives: 18.1 us -> 16 us  [on_device(): lax.all_to_all(sent, ('gx', 'gy'), 0, 0, axis_index_groups=groups)]
    ppermute x8 -> x9, waiting for transfers between devices: 8.22 us -> 9.56 us  [swap(): return lax.ppermute(values, axis, pairs + [(b, a) for a, b in pairs])]
    ppermute x8 -> x9, starting transfers between devices: 24 us -> 24 us  [swap(): return lax.ppermute(values, axis, pairs + [(b, a) for a, b in pairs])]
  transfers between devices with their start and end apart: 8 -> 9, of which waited for: 3 -> 4; matrix products, arithmetic and copies ran while one was open for 0% -> 0% of each run, Pallas kernels for 3% -> 3%
where the time goes in v8:
time: 72.4 us; the launch traced here: 72.2 us
  starting transfers between devices  24 us (33%)
  Pallas kernels  22.4 us (31%)
  blocking collectives  16 us (22%)
  waiting for transfers between devices  9.56 us (13%)
    ppermute x9, starting transfers between devices, swap(): return lax.ppermute(values, axis, pairs + [(b, a) for a, b in pairs])  24 us
    all_to_all x1, blocking collectives, on_device(): lax.all_to_all(sent, ('gx', 'gy'), 0, 0, axis_index_groups=groups)  16 us
    pallas_call x1, Pallas kernels, on_device(): pl.pallas_call(functools.partial(up_kernel, halo=halo, half=half, spans=(...  9.93 us
    ppermute x9, waiting for transfers between devices, swap(): return lax.ppermute(values, axis, pairs + [(b, a) for a, b in pairs])  9.56 us
    pallas_call x1, Pallas kernels, on_device(): pl.pallas_call(functools.partial(down_kernel, halo=halo, half=half, kinds...  4.4 us
    pallas_call x1, Pallas kernels, on_device(): pl.pallas_call(functools.partial(mid_kernel, geos=tuple(block_geos)), out...  2.98 us
    pallas_call x1, Pallas kernels, on_device(): pl.pallas_call(functools.partial(center_kernel, halo=halo, half=half, kin...  2.41 us
    pallas_call x1, Pallas kernels, on_device(): pl.pallas_call(functools.partial(prep_kernel, halo=halo), out_shape=(shap...  1.78 us
  transfers between devices with their start and end apart: 9, of which 4 were waited for; matrix products, arithmetic and copies ran while one was open for 0% of the time, Pallas kernels for 3%

profile of v8, /device:TPU:0, one launch (start us, length us, event | category | flops | bytes accessed | tf_op | source)
XLA Modules:
  0.0 72.2 jit_solution(13315307712112771483)
XLA Ops:
  0.0 0.0 copy-start.2
  0.0 0.0 copy-start.1
  0.0 0.0 copy-start
  0.0 1.8 %prep.1 = (f32[13,128,128]{2,1,0:T(8,128)S(1)}, f32[13,24,128]{2,1,0:T(8,128)S(1)}, f32[13,24,128]{2,1,0:T(8,128)S(1)}) custom-call(f32[64]{0:T(128)} %watt_hbm.1, s32[8,8]{1,0:T(8,128)} %cat_hbm.1, f32[6,128,128]{2,1,0:T(8,128)} %u_hbm.1, s32[6,128,128]{2,1,0:T(8,128)} %sub_hbm.1), custom_call_target="tpu_custom_call" | custom-call | tf_op jit(solution)/shard_map/prep/pallas_call | solution.py:903
  1.8 3.0 %collective-permute-start = (f32[13,24,128]{2,1,0:T(8,128)S(1)}, f32[13,24,128]{2,1,0:T(8,128)S(1)}, u32[]{:S(2)}, u32[]{:S(2)}) collective-permute-start(f32[13,24,128]{2,1,0:T(8,128)S(1)} %get-tuple-element.62), channel_id=1, source_target_pairs={{0,1},{2,3},{1,0},{3,2},{4,5},{6,7},{5,4},{7,6},{8,9},{10,11},{9,8... | collective-permute-start | bytes 479240 | tf_op jit(solution)/shard_map/ppermute | solution.py:876
  4.8 0.7 collective-permute-start.1
  5.5 3.4 %collective-permute-done.ra = f32[13,24,128]{2,1,0:T(8,128)S(1)} collective-permute-done((f32[13,24,128]{2,1,0:T(8,128)S(1)}, f32[13,24,128]{2,1,0:T(8,128)S(1)}, u32[]{:S(2)}, u32[]{:S(2)}) %collective-permute-start) | collective-permute-done | bytes 159776 | tf_op jit(solution)/shard_map/ppermute | solution.py:876
  8.9 0.0 collective-permute-done.1.rb
  8.9 0.9 %split.1 = (f32[13,4,64,128]{3,2,1,0:T(8,128)S(1)}, f32[624,128]{1,0:T(8,128)S(1)}, f32[624,128]{1,0:T(8,128)S(1)}) custom-call(f32[13,128,128]{2,1,0:T(8,128)S(1)} %get-tuple-element.61.own, f32[13,24,128]{2,1,0:T(8,128)S(1)} %collective-permute-done.ra, f32[13,24,128]{2,1,0:T(8,128)S(1)} %collective-permute-done.1.rb), custom_call_target="tpu_custom_call" | custom-call | tf_op jit(solution)/shard_map/split/pallas_call | solution.py:920
  9.9 0.1 collective-permute-start.2
  9.9 0.7 collective-permute-start.3
  10.6 0.0 copy-done.2
  10.6 0.0 copy-done.1
  10.6 0.0 copy-done
  10.6 2.4 %center.1 = (f32[4,6,104,128]{3,2,1,0:T(8,128)S(1)}, f32[4,6,104,128]{3,2,1,0:T(8,128)S(1)}, f32[4,6,104,128]{3,2,1,0:T(8,128)S(1)}, f32[2,6,104,128]{3,2,1,0:T(...) custom-call(f32[8]{0:T(128)S(1)} %copy-done, ...), custom_call_target="tpu_custom_call" | custom-call | tf_op jit(solution)/shard_map/center/pallas_call | solution.py:940
  13.1 0.0 collective-permute-done.2.refs_0_
  13.1 0.0 collective-permute-done.3.refs_1_
  13.1 4.4 %down.1 = (f32[4,6,104,128]{3,2,1,0:T(8,128)S(1)}, f32[4,6,104,128]{3,2,1,0:T(8,128)S(1)}, f32[4,6,104,128]{3,2,1,0:T(8,128)S(1)}, f32[2,6,104,128]{3,2,1,0:T(8,...) custom-call(f32[624,128]{1,0:T(8,128)S(1)} %collective-permute-done., ...), custom_call_target="tpu_custom_call", output_to_operand_aliasing={{0}: (2, {}), {1}: (3, {}), {2}: (4, {}), {3}: (5, {}), {4}... | custom-call | tf_op jit(solution)/shard_map/down/pallas_call | solution.py:951
  17.5 0.7 collective-permute-start.5
  18.2 8.5 %collective-permute-start.4 = (f32[192,128]{1,0:T(8,128)S(1)}, f32[192,128]{1,0:T(8,128)S(1)}, u32[]{:S(2)}, u32[]{:S(2)}) collective-permute-start(f32[192,128]{1,0:T(8,128)S(1)} %get-tuple-element.85.own), channel_id=1, source_target_pairs={{0,1},{2,3},{1,0},{3,2},{4,5},{6,7},{5,4},{7,6},{8,9},{10,11},{9,8... | collective-permute-start | bytes 294920 | tf_op jit(solution)/shard_map/ppermute | solution.py:876
  26.7 0.0 collective-permute-done.5.rb
  26.7 3.6 %collective-permute-done.4.ra = f32[192,128]{1,0:T(8,128)S(1)} collective-permute-done((f32[192,128]{1,0:T(8,128)S(1)}, f32[192,128]{1,0:T(8,128)S(1)}, u32[]{:S(2)}, u32[]{:S(2)}) %collective-permute-start.4) | collective-permute-done | bytes 98336 | tf_op jit(solution)/shard_map/ppermute | solution.py:876
  30.3 0.7 collective-permute-start.7
  31.0 9.7 %collective-permute-start.6 = (f32[3,192,128]{2,1,0:T(8,128)S(1)}, f32[3,192,128]{2,1,0:T(8,128)S(1)}, u32[]{:S(2)}, u32[]{:S(2)}) collective-permute-start(f32[3,192,128]{2,1,0:T(8,128)S(1)} %pad_maximum_fusion), channel_id=1, source_target_pairs={{0,4},{8,12},{16,20},{24,28},{4,0},{12,8},{20,16},{28,24},{1,5},{9... | collective-permute-start | bytes 884744 | tf_op jit(solution)/shard_map/ppermute | solution.py:876
  40.7 0.0 collective-permute-done.7.tb
  40.7 1.2 %collective-permute-done.6.ta = f32[3,192,128]{2,1,0:T(8,128)S(1)} collective-permute-done((f32[3,192,128]{2,1,0:T(8,128)S(1)}, f32[3,192,128]{2,1,0:T(8,128)S(1)}, u32[]{:S(2)}, u32[]{:S(2)}) %collective-permute-start.6) | collective-permute-done | bytes 294944 | tf_op jit(solution)/shard_map/ppermute | solution.py:876
  41.9 3.0 %mid.1 = (f32[6,112,128]{2,1,0:T(8,128)S(1)}, f32[6,112,128]{2,1,0:T(8,128)S(1)}, f32[6,112,128]{2,1,0:T(8,128)S(1)}, f32[6,112,128]{2,1,0:T(8,128)S(1)}, f32[6,...) custom-call(f32[192,128]{1,0:T(8,128)S(1)} %get-tuple-element.85.own, ...), custom_call_target="tpu_custom_call" | custom-call | tf_op jit(solution)/shard_map/mid/pallas_call | solution.py:976
  44.9 16.0 %all_to_all.5.refs_0_ = f32[16,16,128]{2,1,0:T(8,128)S(1)} all-to-all(f32[16,16,128]{2,1,0:T(8,128)S(1)} %broadcast_in_dim.2), channel_id=1, replica_groups={{0,1,2,3,8,9,10,11,16,17,18,19,24,25,26,27},{4,5,6,7,12,13,14,15,20,21,..., dimensions={0} | all-to-all | bytes 262144 | tf_op jit(solution)/shard_map/all_to_all | solution.py:991
  60.9 0.0 collective-permute-start.8
  60.9 1.3 %collective-permute-done.8.refs_1_ = f32[16,16,128]{2,1,0:T(8,128)S(1)} collective-permute-done((f32[16,16,128]{2,1,0:T(8,128)S(1)}, f32[16,16,128]{2,1,0:T(8,128)S(1)}, u32[]{:S(2)}, u32[]{:S(2)}) %collective-permute-start.8) | collective-permute-done | bytes 131104 | tf_op jit(solution)/shard_map/ppermute | solution.py:876
  62.2 9.9 %up.1 = f32[6,128,128]{2,1,0:T(8,128)} custom-call(f32[16,16,128]{2,1,0:T(8,128)S(1)} %all_to_all.5.refs_0_, f32[16,16,128]{2,1,0:T(8,128)S(1)} %collective-permute-done.8.refs_1_, f32[4,6,104,128]{3,2,1,0:T(8,128)S(1)} %get-tuple-element.87.refs_2_, f32[4,6,104,128]{3,2,1,0:T(8,128)S(1)} %get-tuple-element.88.refs_3_, ...), custom_call_target="tpu_custom_call" | custom-call | tf_op jit(solution)/shard_map/up/pallas_call | solution.py:1005
  (2 shorter events, 0.0 us)
Async XLA Ops:
  0.0 10.6 %copy-start.2 = (f32[8]{0:T(128)S(1)}, f32[8]{0:T(128)}, u32[]{:S(2)}) copy-start(f32[8]{0:T(128)} %refs_2_.1) | copy-start | bytes 100
  0.0 10.6 %copy-start.1 = (f32[8]{0:T(128)S(1)}, f32[8]{0:T(128)}, u32[]{:S(2)}) copy-start(f32[8]{0:T(128)} %refs_1_.1) | copy-start | bytes 100
  0.0 10.6 %copy-start = (f32[8]{0:T(128)S(1)}, f32[8]{0:T(128)}, u32[]{:S(2)}) copy-start(f32[8]{0:T(128)} %refs_0_.1) | copy-start | bytes 100
  1.8 7.1 %collective-permute-start = (f32[13,24,128]{2,1,0:T(8,128)S(1)}, f32[13,24,128]{2,1,0:T(8,128)S(1)}, u32[]{:S(2)}, u32[]{:S(2)}) collective-permute-start(f32[13,24,128]{2,1,0:T(8,128)S(1)} %get-tuple-element.62), channel_id=1, source_target_pairs={{0,1},{2,3},{1,0},{3,2},{4,5},{6,7},{5,4},{7,6},{8,9},{10,11},{9,8... | collective-permute-start | bytes 479240 | tf_op jit(solution)/shard_map/ppermute | solution.py:876
  4.8 4.1 %collective-permute-start.1 = (f32[13,24,128]{2,1,0:T(8,128)S(1)}, f32[13,24,128]{2,1,0:T(8,128)S(1)}, u32[]{:S(2)}, u32[]{:S(2)}) collective-permute-start(f32[13,24,128]{2,1,0:T(8,128)S(1)} %get-tuple-element.63), channel_id=1, source_target_pairs={{1,2},{2,1},{5,6},{6,5},{9,10},{10,9},{13,14},{14,13},{17,18},{18,... | collective-permute-start | bytes 479240 | tf_op jit(solution)/shard_map/ppermute | solution.py:876
  9.9 3.2 %collective-permute-start.2 = (f32[624,128]{1,0:T(8,128)S(1)}, f32[624,128]{1,0:T(8,128)S(1)}, u32[]{:S(2)}, u32[]{:S(2)}) collective-permute-start(f32[624,128]{1,0:T(8,128)S(1)} %get-tuple-element.64), channel_id=1, source_target_pairs={{0,4},{8,12},{16,20},{24,28},{4,0},{12,8},{20,16},{28,24},{1,5},{9... | collective-permute-start | bytes 958472 | tf_op jit(solution)/shard_map/ppermute | solution.py:876
  9.9 3.2 %collective-permute-start.3 = (f32[624,128]{1,0:T(8,128)S(1)}, f32[624,128]{1,0:T(8,128)S(1)}, u32[]{:S(2)}, u32[]{:S(2)}) collective-permute-start(f32[624,128]{1,0:T(8,128)S(1)} %get-tuple-element.65), channel_id=1, source_target_pairs={{4,8},{12,16},{20,24},{8,4},{16,12},{24,20},{5,9},{13,17},{21,25},... | collective-permute-start | bytes 958472 | tf_op jit(solution)/shard_map/ppermute | solution.py:876
  17.5 9.2 %collective-permute-start.5 = (f32[192,128]{1,0:T(8,128)S(1)}, f32[192,128]{1,0:T(8,128)S(1)}, u32[]{:S(2)}, u32[]{:S(2)}) collective-permute-start(f32[192,128]{1,0:T(8,128)S(1)} %get-tuple-element.85.own), channel_id=1, source_target_pairs={{1,2},{2,1},{5,6},{6,5},{9,10},{10,9},{13,14},{14,13},{17,18},{18,... | collective-permute-start | bytes 294920 | tf_op jit(solution)/shard_map/ppermute | solution.py:876
  18.2 12.1 %collective-permute-start.4 = (f32[192,128]{1,0:T(8,128)S(1)}, f32[192,128]{1,0:T(8,128)S(1)}, u32[]{:S(2)}, u32[]{:S(2)}) collective-permute-start(f32[192,128]{1,0:T(8,128)S(1)} %get-tuple-element.85.own), channel_id=1, source_target_pairs={{0,1},{2,3},{1,0},{3,2},{4,5},{6,7},{5,4},{7,6},{8,9},{10,11},{9,8... | collective-permute-start | bytes 294920 | tf_op jit(solution)/shard_map/ppermute | solution.py:876
  30.3 10.4 %collective-permute-start.7 = (f32[3,192,128]{2,1,0:T(8,128)S(1)}, f32[3,192,128]{2,1,0:T(8,128)S(1)}, u32[]{:S(2)}, u32[]{:S(2)}) collective-permute-start(f32[3,192,128]{2,1,0:T(8,128)S(1)} %pad_maximum_fusion), channel_id=1, source_target_pairs={{4,8},{12,16},{20,24},{8,4},{16,12},{24,20},{5,9},{13,17},{21,25},... | collective-permute-start | bytes 884744 | tf_op jit(solution)/shard_map/ppermute | solution.py:876
  31.0 10.9 %collective-permute-start.6 = (f32[3,192,128]{2,1,0:T(8,128)S(1)}, f32[3,192,128]{2,1,0:T(8,128)S(1)}, u32[]{:S(2)}, u32[]{:S(2)}) collective-permute-start(f32[3,192,128]{2,1,0:T(8,128)S(1)} %pad_maximum_fusion), channel_id=1, source_target_pairs={{0,4},{8,12},{16,20},{24,28},{4,0},{12,8},{20,16},{28,24},{1,5},{9... | collective-permute-start | bytes 884744 | tf_op jit(solution)/shard_map/ppermute | solution.py:876
  60.9 1.3 %collective-permute-start.8 = (f32[16,16,128]{2,1,0:T(8,128)S(1)}, f32[16,16,128]{2,1,0:T(8,128)S(1)}, u32[]{:S(2)}, u32[]{:S(2)}) collective-permute-start(f32[16,16,128]{2,1,0:T(8,128)S(1)} %all_to_all.5.refs_0_), channel_id=1, source_target_pairs={{0,4},{8,12},{16,20},{24,28},{4,0},{12,8},{20,16},{28,24},{1,5},{9... | collective-permute-start | bytes 393224 | tf_op jit(solution)/shard_map/ppermute | solution.py:876

commit v9 on v8

--- a/solution.py
+++ b/solution.py
@@ -135,7 +135,7 @@
         right = jnp.where(even_y, ra[q], rb[q])
         sides = jnp.concatenate([left, right, jnp.zeros((LANES - 2 * halo, height), F32)], 0).T
         planes.append(jnp.concatenate([own[q], sides], 1))
-    first = pick_dot(jnp.concatenate(planes[:layers] + planes[2 * layers :], 0), pick)
+    first = pick_dot(jnp.concatenate(planes[:layers] + planes[2 * layers :], 0), pick, 2)
     second = pick_dot(jnp.concatenate(planes[layers : 2 * layers], 0), pick, 1)
     for q in range(2 * layers + 1):
         if layers <= q < 2 * layers:
@@ -703,7 +703,7 @@
         return (*e, *r, *p)
 
     start = (*[jnp.zeros((n, LANES), F32)] * deep, *r, *[x * y for x, y in zip(r, inv)])
-    out = lax.fori_loop(0, COARSE_ITERS, step, start)
+    out = lax.fori_loop(0, COARSE_ITERS, step, start, unroll=3)
     for k in planes:
         s["u"][k, here] = out[k]
 
@@ -774,11 +774,11 @@
                 top[name][k, at] = value
 
     def gather_some(step, carry):
-        for n in range(4):
-            gather(4 * step + n, n % 2)
+        for n in range(8):
+            gather(8 * step + n, n % 2)
         return carry
 
-    lax.fori_loop(0, nx // 4, gather_some, 0)
+    lax.fori_loop(0, nx // 8, gather_some, 0)
 
     for n, level in enumerate(range(LOCAL, LEVELS)):
         now, below = wholes[n], wholes[n + 1]
@@ -865,7 +865,7 @@
     both = [
         jnp.concatenate([now["u"][2 * p + j, k, body_rows] for k, p in spots], 0) for j in range(2)
     ]
-    every = pick_dot(jnp.concatenate(both, 1), pick)
+    every = pick_dot(jnp.concatenate(both, 1), pick, 2)
     for n, (k, p) in enumerate(spots):
         out[k, pl.ds(p, half, stride=2), :] = every[n * half : (n + 1) * half]
 
@@ -985,7 +985,7 @@
     saved += more
     nat_shapes += block_shapes
 
-    assert nx % 4 == 0
+    assert nx % 8 == 0
     groups = [[x * ny + y for x in range(c, nx, 2) for y in range(ny)] for c in range(2)]
     sent = jnp.broadcast_to(payload[None], (nx // 2 * ny,) + payload.shape)
     gathered = lax.all_to_all(sent, ("gx", "gy"), 0, 0, axis_index_groups=groups)

time: 72.4 us -> 72 us (level)
  no operation moved by 1% of the time
where the time goes in v9:
time: 72 us; the launch traced here: 71.8 us
  starting transfers between devices  24 us (33%)
  Pallas kernels  22 us (31%)
  blocking collectives  16 us (22%)
  waiting for transfers between devices  9.56 us (13%)
    ppermute x9, starting transfers between devices, swap(): return lax.ppermute(values, axis, pairs + [(b, a) for a, b in pairs])  24 us
    all_to_all x1, blocking collectives, on_device(): lax.all_to_all(sent, ('gx', 'gy'), 0, 0, axis_index_groups=groups)  16 us
    pallas_call x1, Pallas kernels, on_device(): pl.pallas_call(functools.partial(up_kernel, halo=halo, half=half, spans=(...  9.63 us
    ppermute x9, waiting for transfers between devices, swap(): return lax.ppermute(values, axis, pairs + [(b, a) for a, b in pairs])  9.56 us
    pallas_call x1, Pallas kernels, on_device(): pl.pallas_call(functools.partial(down_kernel, halo=halo, half=half, kinds...  4.4 us
    pallas_call x1, Pallas kernels, on_device(): pl.pallas_call(functools.partial(mid_kernel, geos=tuple(block_geos)), out...  2.98 us
    pallas_call x1, Pallas kernels, on_device(): pl.pallas_call(functools.partial(center_kernel, halo=halo, half=half, kin...  2.41 us
    pallas_call x1, Pallas kernels, on_device(): pl.pallas_call(functools.partial(prep_kernel, halo=halo), out_shape=(shap...  1.78 us
  transfers between devices with their start and end apart: 9, of which 4 were waited for; matrix products, arithmetic and copies ran while one was open for 0% of the time, Pallas kernels for 3%

profile of v9, /device:TPU:0, one launch (start us, length us, event | category | flops | bytes accessed | tf_op | source)
XLA Modules:
  0.0 71.8 jit_solution(3315298190197406176)
XLA Ops:
  0.0 0.0 copy-start.2
  0.0 0.0 copy-start.1
  0.0 0.0 copy-start
  0.0 1.8 %prep.1 = (f32[13,128,128]{2,1,0:T(8,128)S(1)}, f32[13,24,128]{2,1,0:T(8,128)S(1)}, f32[13,24,128]{2,1,0:T(8,128)S(1)}) custom-call(f32[64]{0:T(128)} %watt_hbm.1, s32[8,8]{1,0:T(8,128)} %cat_hbm.1, f32[6,128,128]{2,1,0:T(8,128)} %u_hbm.1, s32[6,128,128]{2,1,0:T(8,128)} %sub_hbm.1), custom_call_target="tpu_custom_call" | custom-call | tf_op jit(solution)/shard_map/prep/pallas_call | solution.py:903
  1.8 3.0 %collective-permute-start = (f32[13,24,128]{2,1,0:T(8,128)S(1)}, f32[13,24,128]{2,1,0:T(8,128)S(1)}, u32[]{:S(2)}, u32[]{:S(2)}) collective-permute-start(f32[13,24,128]{2,1,0:T(8,128)S(1)} %get-tuple-element.62), channel_id=1, source_target_pairs={{0,1},{2,3},{1,0},{3,2},{4,5},{6,7},{5,4},{7,6},{8,9},{10,11},{9,8... | collective-permute-start | bytes 479240 | tf_op jit(solution)/shard_map/ppermute | solution.py:876
  4.8 0.7 collective-permute-start.1
  5.5 3.4 %collective-permute-done.ra = f32[13,24,128]{2,1,0:T(8,128)S(1)} collective-permute-done((f32[13,24,128]{2,1,0:T(8,128)S(1)}, f32[13,24,128]{2,1,0:T(8,128)S(1)}, u32[]{:S(2)}, u32[]{:S(2)}) %collective-permute-start) | collective-permute-done | bytes 159776 | tf_op jit(solution)/shard_map/ppermute | solution.py:876
  8.9 0.0 collective-permute-done.1.rb
  8.9 0.8 %split.1 = (f32[13,4,64,128]{3,2,1,0:T(8,128)S(1)}, f32[624,128]{1,0:T(8,128)S(1)}, f32[624,128]{1,0:T(8,128)S(1)}) custom-call(f32[13,128,128]{2,1,0:T(8,128)S(1)} %get-tuple-element.61.own, f32[13,24,128]{2,1,0:T(8,128)S(1)} %collective-permute-done.ra, f32[13,24,128]{2,1,0:T(8,128)S(1)} %collective-permute-done.1.rb), custom_call_target="tpu_custom_call" | custom-call | tf_op jit(solution)/shard_map/split/pallas_call | solution.py:920
  9.8 0.1 collective-permute-start.2
  9.8 0.7 collective-permute-start.3
  10.5 0.0 copy-done.2
  10.5 0.0 copy-done.1
  10.5 0.0 copy-done
  10.5 2.4 %center.1 = (f32[4,6,104,128]{3,2,1,0:T(8,128)S(1)}, f32[4,6,104,128]{3,2,1,0:T(8,128)S(1)}, f32[4,6,104,128]{3,2,1,0:T(8,128)S(1)}, f32[2,6,104,128]{3,2,1,0:T(...) custom-call(f32[8]{0:T(128)S(1)} %copy-done, ...), custom_call_target="tpu_custom_call" | custom-call | tf_op jit(solution)/shard_map/center/pallas_call | solution.py:940
  13.0 0.0 collective-permute-done.2.refs_0_
  13.0 0.0 collective-permute-done.3.refs_1_
  13.0 4.4 %down.1 = (f32[4,6,104,128]{3,2,1,0:T(8,128)S(1)}, f32[4,6,104,128]{3,2,1,0:T(8,128)S(1)}, f32[4,6,104,128]{3,2,1,0:T(8,128)S(1)}, f32[2,6,104,128]{3,2,1,0:T(8,...) custom-call(f32[624,128]{1,0:T(8,128)S(1)} %collective-permute-done., ...), custom_call_target="tpu_custom_call", output_to_operand_aliasing={{0}: (2, {}), {1}: (3, {}), {2}: (4, {}), {3}: (5, {}), {4}... | custom-call | tf_op jit(solution)/shard_map/down/pallas_call | solution.py:951
  17.4 0.7 collective-permute-start.5
  18.1 8.5 %collective-permute-start.4 = (f32[192,128]{1,0:T(8,128)S(1)}, f32[192,128]{1,0:T(8,128)S(1)}, u32[]{:S(2)}, u32[]{:S(2)}) collective-permute-start(f32[192,128]{1,0:T(8,128)S(1)} %get-tuple-element.85.own), channel_id=1, source_target_pairs={{0,1},{2,3},{1,0},{3,2},{4,5},{6,7},{5,4},{7,6},{8,9},{10,11},{9,8... | collective-permute-start | bytes 294920 | tf_op jit(solution)/shard_map/ppermute | solution.py:876
  26.6 0.0 collective-permute-done.5.rb
  26.6 3.6 %collective-permute-done.4.ra = f32[192,128]{1,0:T(8,128)S(1)} collective-permute-done((f32[192,128]{1,0:T(8,128)S(1)}, f32[192,128]{1,0:T(8,128)S(1)}, u32[]{:S(2)}, u32[]{:S(2)}) %collective-permute-start.4) | collective-permute-done | bytes 98336 | tf_op jit(solution)/shard_map/ppermute | solution.py:876
  30.2 0.7 collective-permute-start.7
  30.9 9.7 %collective-permute-start.6 = (f32[3,192,128]{2,1,0:T(8,128)S(1)}, f32[3,192,128]{2,1,0:T(8,128)S(1)}, u32[]{:S(2)}, u32[]{:S(2)}) collective-permute-start(f32[3,192,128]{2,1,0:T(8,128)S(1)} %pad_maximum_fusion), channel_id=1, source_target_pairs={{0,4},{8,12},{16,20},{24,28},{4,0},{12,8},{20,16},{28,24},{1,5},{9... | collective-permute-start | bytes 884744 | tf_op jit(solution)/shard_map/ppermute | solution.py:876
  40.6 0.0 collective-permute-done.7.tb
  40.6 1.2 %collective-permute-done.6.ta = f32[3,192,128]{2,1,0:T(8,128)S(1)} collective-permute-done((f32[3,192,128]{2,1,0:T(8,128)S(1)}, f32[3,192,128]{2,1,0:T(8,128)S(1)}, u32[]{:S(2)}, u32[]{:S(2)}) %collective-permute-start.6) | collective-permute-done | bytes 294944 | tf_op jit(solution)/shard_map/ppermute | solution.py:876
  41.8 3.0 %mid.1 = (f32[6,112,128]{2,1,0:T(8,128)S(1)}, f32[6,112,128]{2,1,0:T(8,128)S(1)}, f32[6,112,128]{2,1,0:T(8,128)S(1)}, f32[6,112,128]{2,1,0:T(8,128)S(1)}, f32[6,...) custom-call(f32[192,128]{1,0:T(8,128)S(1)} %get-tuple-element.85.own, ...), custom_call_target="tpu_custom_call" | custom-call | tf_op jit(solution)/shard_map/mid/pallas_call | solution.py:976
  44.8 16.0 %all_to_all.5.refs_0_ = f32[16,16,128]{2,1,0:T(8,128)S(1)} all-to-all(f32[16,16,128]{2,1,0:T(8,128)S(1)} %broadcast_in_dim.2), channel_id=1, replica_groups={{0,1,2,3,8,9,10,11,16,17,18,19,24,25,26,27},{4,5,6,7,12,13,14,15,20,21,..., dimensions={0} | all-to-all | bytes 262144 | tf_op jit(solution)/shard_map/all_to_all | solution.py:991
  60.8 0.0 collective-permute-start.8
  60.8 1.3 %collective-permute-done.8.refs_1_ = f32[16,16,128]{2,1,0:T(8,128)S(1)} collective-permute-done((f32[16,16,128]{2,1,0:T(8,128)S(1)}, f32[16,16,128]{2,1,0:T(8,128)S(1)}, u32[]{:S(2)}, u32[]{:S(2)}) %collective-permute-start.8) | collective-permute-done | bytes 131104 | tf_op jit(solution)/shard_map/ppermute | solution.py:876
  62.1 9.6 %up.1 = f32[6,128,128]{2,1,0:T(8,128)} custom-call(f32[16,16,128]{2,1,0:T(8,128)S(1)} %all_to_all.5.refs_0_, f32[16,16,128]{2,1,0:T(8,128)S(1)} %collective-permute-done.8.refs_1_, f32[4,6,104,128]{3,2,1,0:T(8,128)S(1)} %get-tuple-element.87.refs_2_, f32[4,6,104,128]{3,2,1,0:T(8,128)S(1)} %get-tuple-element.88.refs_3_, ...), custom_call_target="tpu_custom_call" | custom-call | tf_op jit(solution)/shard_map/up/pallas_call | solution.py:1005
  (2 shorter events, 0.0 us)
Async XLA Ops:
  0.0 10.5 %copy-start.2 = (f32[8]{0:T(128)S(1)}, f32[8]{0:T(128)}, u32[]{:S(2)}) copy-start(f32[8]{0:T(128)} %refs_2_.1) | copy-start | bytes 100
  0.0 10.5 %copy-start.1 = (f32[8]{0:T(128)S(1)}, f32[8]{0:T(128)}, u32[]{:S(2)}) copy-start(f32[8]{0:T(128)} %refs_1_.1) | copy-start | bytes 100
  0.0 10.5 %copy-start = (f32[8]{0:T(128)S(1)}, f32[8]{0:T(128)}, u32[]{:S(2)}) copy-start(f32[8]{0:T(128)} %refs_0_.1) | copy-start | bytes 100
  1.8 7.1 %collective-permute-start = (f32[13,24,128]{2,1,0:T(8,128)S(1)}, f32[13,24,128]{2,1,0:T(8,128)S(1)}, u32[]{:S(2)}, u32[]{:S(2)}) collective-permute-start(f32[13,24,128]{2,1,0:T(8,128)S(1)} %get-tuple-element.62), channel_id=1, source_target_pairs={{0,1},{2,3},{1,0},{3,2},{4,5},{6,7},{5,4},{7,6},{8,9},{10,11},{9,8... | collective-permute-start | bytes 479240 | tf_op jit(solution)/shard_map/ppermute | solution.py:876
  4.8 4.1 %collective-permute-start.1 = (f32[13,24,128]{2,1,0:T(8,128)S(1)}, f32[13,24,128]{2,1,0:T(8,128)S(1)}, u32[]{:S(2)}, u32[]{:S(2)}) collective-permute-start(f32[13,24,128]{2,1,0:T(8,128)S(1)} %get-tuple-element.63), channel_id=1, source_target_pairs={{1,2},{2,1},{5,6},{6,5},{9,10},{10,9},{13,14},{14,13},{17,18},{18,... | collective-permute-start | bytes 479240 | tf_op jit(solution)/shard_map/ppermute | solution.py:876
  9.8 3.2 %collective-permute-start.2 = (f32[624,128]{1,0:T(8,128)S(1)}, f32[624,128]{1,0:T(8,128)S(1)}, u32[]{:S(2)}, u32[]{:S(2)}) collective-permute-start(f32[624,128]{1,0:T(8,128)S(1)} %get-tuple-element.64), channel_id=1, source_target_pairs={{0,4},{8,12},{16,20},{24,28},{4,0},{12,8},{20,16},{28,24},{1,5},{9... | collective-permute-start | bytes 958472 | tf_op jit(solution)/shard_map/ppermute | solution.py:876
  9.8 3.2 %collective-permute-start.3 = (f32[624,128]{1,0:T(8,128)S(1)}, f32[624,128]{1,0:T(8,128)S(1)}, u32[]{:S(2)}, u32[]{:S(2)}) collective-permute-start(f32[624,128]{1,0:T(8,128)S(1)} %get-tuple-element.65), channel_id=1, source_target_pairs={{4,8},{12,16},{20,24},{8,4},{16,12},{24,20},{5,9},{13,17},{21,25},... | collective-permute-start | bytes 958472 | tf_op jit(solution)/shard_map/ppermute | solution.py:876
  17.4 9.2 %collective-permute-start.5 = (f32[192,128]{1,0:T(8,128)S(1)}, f32[192,128]{1,0:T(8,128)S(1)}, u32[]{:S(2)}, u32[]{:S(2)}) collective-permute-start(f32[192,128]{1,0:T(8,128)S(1)} %get-tuple-element.85.own), channel_id=1, source_target_pairs={{1,2},{2,1},{5,6},{6,5},{9,10},{10,9},{13,14},{14,13},{17,18},{18,... | collective-permute-start | bytes 294920 | tf_op jit(solution)/shard_map/ppermute | solution.py:876
  18.1 12.1 %collective-permute-start.4 = (f32[192,128]{1,0:T(8,128)S(1)}, f32[192,128]{1,0:T(8,128)S(1)}, u32[]{:S(2)}, u32[]{:S(2)}) collective-permute-start(f32[192,128]{1,0:T(8,128)S(1)} %get-tuple-element.85.own), channel_id=1, source_target_pairs={{0,1},{2,3},{1,0},{3,2},{4,5},{6,7},{5,4},{7,6},{8,9},{10,11},{9,8... | collective-permute-start | bytes 294920 | tf_op jit(solution)/shard_map/ppermute | solution.py:876
  30.2 10.4 %collective-permute-start.7 = (f32[3,192,128]{2,1,0:T(8,128)S(1)}, f32[3,192,128]{2,1,0:T(8,128)S(1)}, u32[]{:S(2)}, u32[]{:S(2)}) collective-permute-start(f32[3,192,128]{2,1,0:T(8,128)S(1)} %pad_maximum_fusion), channel_id=1, source_target_pairs={{4,8},{12,16},{20,24},{8,4},{16,12},{24,20},{5,9},{13,17},{21,25},... | collective-permute-start | bytes 884744 | tf_op jit(solution)/shard_map/ppermute | solution.py:876
  30.9 10.9 %collective-permute-start.6 = (f32[3,192,128]{2,1,0:T(8,128)S(1)}, f32[3,192,128]{2,1,0:T(8,128)S(1)}, u32[]{:S(2)}, u32[]{:S(2)}) collective-permute-start(f32[3,192,128]{2,1,0:T(8,128)S(1)} %pad_maximum_fusion), channel_id=1, source_target_pairs={{0,4},{8,12},{16,20},{24,28},{4,0},{12,8},{20,16},{28,24},{1,5},{9... | collective-permute-start | bytes 884744 | tf_op jit(solution)/shard_map/ppermute | solution.py:876
  60.8 1.3 %collective-permute-start.8 = (f32[16,16,128]{2,1,0:T(8,128)S(1)}, f32[16,16,128]{2,1,0:T(8,128)S(1)}, u32[]{:S(2)}, u32[]{:S(2)}) collective-permute-start(f32[16,16,128]{2,1,0:T(8,128)S(1)} %all_to_all.5.refs_0_), channel_id=1, source_target_pairs={{0,4},{8,12},{16,20},{24,28},{4,0},{12,8},{20,16},{28,24},{1,5},{9... | collective-permute-start | bytes 393224 | tf_op jit(solution)/shard_map/ppermute | solution.py:876
